TPU v7x, 256 devices: a whole 4x4x8 slice. The times are simulated.
256 devices in a mesh: grp: 4 (over y), dev: 64 (over z, x, core).
Axes of the slice: x: 4, y: 4, z: 8, core: 2. Of those that a mesh axis runs over, the one named last changes fastest.
Arguments:
- nz_user: int32 [32768, 128], P(('grp', 'dev')), may hold values from 0 to 65535
- nz_sub: int32 [32768, 128], P(('grp', 'dev')), may hold values from 0 to 16383
- nz_value: float32 [32768, 128], P(('grp', 'dev')), may hold values from -1 to 1
- tile_word: int32 [32768], P(('grp', 'dev')), may hold values from 0 to 16383, as said below
- word_owner: int32 [16384], replicated, may hold values from 0 to 16383, as said below
- user_factor: bfloat16 [64, 65536], P(None, 'dev'), may hold values from -6 to 6
- sub_factor: bfloat16 [64, 16384], P(None, 'dev'), may hold values from -6 to 6
Outputs:
- word_rows: float32 [64, 16384], P(None, ('grp', 'dev'))
Inputs may be any that keep to these rules, and one draw needn't show every extreme that they name: A permutation of the word indices: word w is summed into column word_owner[w] of word_rows. `tile_word`: tile i lies on device i // 128 (grp+dev order). On every device at most 2 tiles belong to words whose output column lies on any one other device, and on every device that bound is reached for some other device.
All inputs are finite; a program needn't handle non-finite values.
Results may differ from a plain program's by a relative error of at most 0.0003.
Values may be sent and summed in bfloat16 or wider, within the bound.
No kernel may reach another device: no remote copies, remote signals or barrier semaphores. Data moves between devices by JAX's collectives and lax.ppermute only.
A program may use at most 64 MiB of HBM per device.

v0:
```python
import jax
import jax.numpy as jnp
from jax import lax
from jax.sharding import PartitionSpec as P

CAP = 2


def cut_along(value, dim, peers):
    shape = value.shape
    pieces = value.reshape(*shape[:dim], peers, shape[dim] // peers, *shape[dim + 1 :])
    return jnp.moveaxis(pieces, dim, 0)


def joined_along(pieces, dim):
    pieces = jnp.moveaxis(pieces, 0, dim)
    shape = pieces.shape
    return pieces.reshape(*shape[:dim], shape[dim] * shape[dim + 1], *shape[dim + 2 :])


def exchange_both(value, axis, axes, splits, concats):
    sizes = [lax.axis_size(a) for a in axes]
    pieces = cut_along(value, splits[0], sizes[0])
    pieces = jnp.moveaxis(cut_along(pieces, splits[1] + 1, sizes[1]), 0, 1)
    inside = pieces.shape[2:]
    pieces = pieces.reshape(-1, *inside)
    pieces = lax.all_to_all(pieces, axis, split_axis=0, concat_axis=0, tiled=True)
    pieces = joined_along(pieces.reshape(*sizes, *inside), concats[0] + 1)
    return joined_along(pieces, concats[1])


def tile_sums(user_table, sub_table, nz_user, nz_sub, nz_value):
    tile_count, tile_width = nz_user.shape
    block_tiles = min(tile_count, 128)
    block_count = tile_count // block_tiles

    def one_block(block_args):
        users_block, subs_block, vals_block = block_args
        user_rows = jnp.take(user_table, users_block, axis=0).astype(jnp.float32)
        sub_rows = jnp.take(sub_table, subs_block, axis=0).astype(jnp.float32)
        return jnp.sum(user_rows * sub_rows * vals_block[:, :, None], axis=1)

    block_sums = lax.map(
        one_block,
        (
            nz_user.reshape(block_count, block_tiles, tile_width),
            nz_sub.reshape(block_count, block_tiles, tile_width),
            nz_value.reshape(block_count, block_tiles, tile_width),
        ),
    )
    return block_sums.reshape(tile_count, block_sums.shape[2])


def shards(nz_user, nz_sub, nz_value, tile_word, word_owner, user_factor, sub_factor):
    users_all, subs_all = (
        lax.all_gather(user_factor, "dev", axis=1, tiled=True),
        lax.all_gather(sub_factor, "dev", axis=1, tiled=True),
    )
    user_table = jnp.transpose(users_all)
    sub_table = jnp.transpose(subs_all)
    tile_rows = tile_sums(user_table, sub_table, nz_user, nz_sub, nz_value)
    tile_count, rank_width = tile_rows.shape
    grp_size = lax.axis_size("grp")
    dev_size = lax.axis_size("dev")
    devices_all = grp_size * dev_size
    words_total = word_owner.shape[0]
    words_local = words_total // devices_all
    out_rows = jnp.take(word_owner, tile_word)
    self_index = lax.axis_index("grp") * dev_size + lax.axis_index("dev")
    owner_dev = out_rows // words_local
    local_row = out_rows - owner_dev * words_local
    owned = owner_dev == self_index
    columns = jnp.arange(words_local, dtype=jnp.int32)
    own_table = (owned[:, None] & (local_row[:, None] == columns[None, :])).astype(jnp.float32)
    own_part = jnp.einsum("tr,tk->rk", tile_rows, own_table, precision=lax.Precision.HIGHEST)
    peer_ids = jnp.arange(devices_all, dtype=jnp.int32)
    outgoing = (jnp.logical_not(owned)[:, None] & (owner_dev[:, None] == peer_ids[None, :])).astype(
        jnp.float32
    )
    tile_ids = jnp.arange(tile_count, dtype=jnp.int32)
    earlier_table = (tile_ids[:, None] > tile_ids[None, :]).astype(jnp.float32)
    earlier = jnp.dot(
        earlier_table, outgoing, precision=lax.Precision.HIGHEST, preferred_element_type=jnp.float32
    )
    position = jnp.sum(earlier * outgoing, axis=1).astype(jnp.int32)
    send_slot = jnp.where(owned, devices_all * CAP, owner_dev * CAP + position)
    slot_ids = jnp.arange(devices_all * CAP, dtype=jnp.int32)
    slot_table = (send_slot[:, None] == slot_ids[None, :]).astype(jnp.float32)
    send_rows = jnp.einsum("ts,tr->sr", slot_table, tile_rows, precision=lax.Precision.HIGHEST)
    filled = jnp.sum(slot_table, axis=0)
    send_ids = (
        jnp.dot(
            local_row.astype(jnp.float32),
            slot_table,
            precision=lax.Precision.HIGHEST,
            preferred_element_type=jnp.float32,
        )
        + filled
        - 1.0
    )
    send_rows = send_rows.reshape(grp_size, dev_size, CAP * rank_width)
    send_ids = send_ids.reshape(grp_size, dev_size, CAP)
    got_rows, got_ids = (
        exchange_both(send_rows, ("dev", "grp"), ("dev", "grp"), (1, 0), (1, 0)),
        exchange_both(send_ids, ("dev", "grp"), ("dev", "grp"), (1, 0), (1, 0)),
    )
    got_rows = got_rows.reshape(devices_all * CAP, rank_width)
    got_ids = got_ids.reshape(devices_all * CAP).astype(jnp.int32)
    got_table = (got_ids[:, None] == columns[None, :]).astype(jnp.float32)
    far_part = jnp.einsum("sr,sk->rk", got_rows, got_table, precision=lax.Precision.HIGHEST)
    return own_part + far_part


def solution(mesh):
    return jax.shard_map(
        shards,
        mesh=mesh,
        in_specs=(
            P(("grp", "dev"), None),
            P(("grp", "dev"), None),
            P(("grp", "dev"), None),
            P(("grp", "dev")),
            P(),
            P(None, "dev"),
            P(None, "dev"),
        ),
        out_specs=P(None, ("grp", "dev")),
        check_vma=False,
    )
```

profile of v0, /device:TPU:1, one launch (start us, length us, event | category | flops | bytes accessed | tf_op | source)
XLA Modules:
  0.0 297.3 jit_solution(12197286190946821888)
XLA Ops:
  6.5 0.0 copy-start
  6.5 0.0 all-gather.5.cloned.1.call-start
  6.5 1.5 copy.45
  8.1 0.0 all-gather.5.cloned.1.call-update
  8.1 0.0 all-gather.3.cloned.1.call-start
  8.1 1.8 copy.44
  9.9 0.0 all-gather.3.cloned.1.call-update
  9.9 0.7 compare_select_fusion.2
  10.6 0.0 copy-done
  10.6 1.1 gather_fusion.2
  11.8 0.7 fusion.17
  12.4 0.3 fusion
  12.8 0.7 add_select_fusion
  13.4 0.1 convert_reduce_fusion
  13.6 0.3 fusion.1
  13.8 0.1 reshape_reshape.14
  14.0 0.7 copy.55
  14.7 15.6 %all-to-all-start.1 = ((f32[256,1,1,2]{3,2,1,0:T(1,128)}), f32[256,1,1,2]{3,2,1,0:T(1,128)S(1)}, u32[]{:S(2)}, u32[]{:S(2)}) async-start(f32[256,1,1,2]{3,2,1,0:T(1,128)} %bitcast.14), calls=%async_computation.1 | async-start | bytes 262144 | tf_op jit(solution)/shard_map/all_to_all | solution.py:27
  30.4 0.9 compare_and_fusion
  31.3 0.9 bitcast_clamp_fusion.1
  32.1 0.9 bitcast_clamp_fusion
  33.0 60.6 %all-gather.5.cloned.1.call-done = bf16[64,16384]{0,1:T(8,128)(2,1)} async-done(((bf16[64,256]{0,1:T(8,128)(2,1)}), bf16[64,16384]{0,1:T(8,128)(2,1)}) %all-gather.5.cloned.1.call-update) | async-done | bytes 2097168 | tf_op jit(solution)/shard_map/all_gather | solution.py:57
  93.6 58.1 %gather_fusion.1 = bf16[16384,64]{1,0:T(8,128)(2,1)} fusion(bf16[16384,64]{1,0:T(8,128)(2,1)} %bitcast.38, s32[16384]{0:T(1024)S(1)} %bitcast_clamp_fusion), kind=kCustom, calls=%fused_computation.1 | custom fusion | bytes 4259840 | tf_op jit(solution)/shard_map/while/body/eval_jaxpr/jit(_take)/gather | solution.py:40
  151.8 41.1 %all-gather.3.cloned.1.call-done = bf16[64,65536]{0,1:T(8,128)(2,1)} async-done(((bf16[64,1024]{0,1:T(8,128)(2,1)}), bf16[64,65536]{0,1:T(8,128)(2,1)}) %all-gather.3.cloned.1.call-update) | async-done | bytes 8388624 | tf_op jit(solution)/shard_map/all_gather | solution.py:56
  192.8 0.0 copy-start.1
  192.8 63.3 %gather_fusion = bf16[16384,64]{1,0:T(8,128)(2,1)} fusion(bf16[65536,64]{1,0:T(8,128)(2,1)} %bitcast.39, s32[16384]{0:T(1024)S(1)} %bitcast_clamp_fusion.1), kind=kCustom, calls=%fused_computation | custom fusion | bytes 4259840 | tf_op jit(solution)/shard_map/while/body/eval_jaxpr/jit(_take)/gather | solution.py:39
  256.2 0.0 copy-done.1
  256.2 10.6 %multiply_reduce_fusion = f32[128,64]{1,0:T(8,128)S(1)} fusion(f32[128,128]{1,0:T(8,128)S(1)} %copy-done.1, pred[128,128]{1,0:T(8,128)(4,1)S(1)} %get-tuple-element.30, pred[128,128]{1,0:T(8,128)(4,1)S(1)} %get-tuple-element.32, bf16[16384,64]{1,0:T(8,128)(2,1)} %gather_fusion.1, bf16[16384,64]{1,0:T(8,128)(2,1)} %gather_fusion), kind=kLoop, calls=%fused_computation.3 | loop fusion | flops 7331840 | bytes 4325376 | tf_op jit(solution)/shard_map/while/body/eval_jaxpr/reduce_sum | solution.py:41
  266.8 0.5 fusion.2
  267.2 0.1 reshape_reshape.12
  267.3 0.7 copy.47
  268.1 0.0 all-to-all-done.1
  268.1 8.5 %all-to-all-start = ((f32[256,1,1,128]{3,2,1,0:T(1,128)}), f32[256,1,1,128]{3,2,1,0:T(1,128)S(1)}, u32[]{:S(2)}, u32[]{:S(2)}) async-start(f32[256,1,1,128]{3,2,1,0:T(1,128)} %bitcast.8), calls=%async_computation | async-start | bytes 262144 | tf_op jit(solution)/shard_map/all_to_all | solution.py:27
  276.5 0.1 copy.52
  276.6 0.1 convert_element_type.45
  276.8 0.6 copy.53
  277.3 0.2 convert_element_type.47
  277.5 0.3 fusion.11
  277.8 11.5 %all-to-all-done = f32[256,1,1,128]{3,2,1,0:T(1,128)S(1)} async-done(((f32[256,1,1,128]{3,2,1,0:T(1,128)}), f32[256,1,1,128]{3,2,1,0:T(1,128)S(1)}, u32[]{:S(2)}, u32[]{:S(2)}) %all-to-all-start) | async-done | bytes 131104 | tf_op jit(solution)/shard_map/all_to_all | solution.py:27
  289.3 0.1 reshape_reshape_reshape.4
  289.4 1.1 convolution_add_fusion
  (4 shorter events, 0.0 us)
Async XLA Ops:
  6.5 4.1 %copy-start = (s32[16384]{0:T(1024)S(1)}, s32[16384]{0:T(1024)}, u32[]{:S(2)}) copy-start(s32[16384]{0:T(1024)} %param.11) | copy-start | bytes 196612
  6.5 87.1 %all-gather.5.cloned.1.call-start = ((), (), s32[]{:S(2)}) async-start(), calls=%async_computation.3 | async-start | bytes 4259840 | tf_op jit(solution)/shard_map/all_gather | solution.py:57
  8.1 184.8 %all-gather.3.cloned.1.call-start = ((), (), s32[]{:S(2)}) async-start(), calls=%async_computation.2 | async-start | bytes 17039360 | tf_op jit(solution)/shard_map/all_gather | solution.py:56
  14.7 253.4 %all-to-all-start.1 = ((f32[256,1,1,2]{3,2,1,0:T(1,128)}), f32[256,1,1,2]{3,2,1,0:T(1,128)S(1)}, u32[]{:S(2)}, u32[]{:S(2)}) async-start(f32[256,1,1,2]{3,2,1,0:T(1,128)} %bitcast.14), calls=%async_computation.1 | async-start | bytes 262144 | tf_op jit(solution)/shard_map/all_to_all | solution.py:27
  192.8 63.3 %copy-start.1 = (f32[128,128]{1,0:T(8,128)S(1)}, f32[128,128]{1,0:T(8,128)}, u32[]{:S(2)}) copy-start(f32[128,128]{1,0:T(8,128)} %param.9) | copy-start | bytes 196612
  268.1 21.2 %all-to-all-start = ((f32[256,1,1,128]{3,2,1,0:T(1,128)}), f32[256,1,1,128]{3,2,1,0:T(1,128)S(1)}, u32[]{:S(2)}, u32[]{:S(2)}) async-start(f32[256,1,1,128]{3,2,1,0:T(1,128)} %bitcast.8), calls=%async_computation | async-start | bytes 262144 | tf_op jit(solution)/shard_map/all_to_all | solution.py:27
Sparse Core Ops, SparseCore 0:
  10.1 83.5 all-gather.4
  96.4 96.3 all-gather.2
where the time goes:
time: 298 us; the launch traced here: 297 us
  local copies, waits for them, and re-layouts  129 us (43%)
  waiting for transfers between devices  113 us (38%)
  starting transfers between devices  24.2 us (8%)
  other arithmetic  15.4 us (5%)
  between operations  13.5 us (5%)
    gather x1, local copies, waits for them, and re-layouts, one_block(): user_rows = jnp.take(user_table, users_block, axis=0).astype(jnp.float32)  63.3 us
    all_gather x1, waiting for transfers between devices, shards(): lax.all_gather(sub_factor, 'dev', axis=1, tiled=True)  60.6 us
    gather x1, local copies, waits for them, and re-layouts, one_block(): sub_rows = jnp.take(sub_table, subs_block, axis=0).astype(jnp.float32)  58.1 us
    all_gather x1, waiting for transfers between devices, shards(): lax.all_gather(user_factor, 'dev', axis=1, tiled=True)  41.1 us
    all_to_all x2, starting transfers between devices, exchange_both(): lax.all_to_all(pieces, axis, split_axis=0, concat_axis=0, tiled=True)  24.1 us
    all_to_all x2, waiting for transfers between devices, exchange_both(): lax.all_to_all(pieces, axis, split_axis=0, concat_axis=0, tiled=True)  11.5 us
    reduce_sum x1, other arithmetic, one_block(): return jnp.sum(user_rows * sub_rows * vals_block[:, :, None], axis=1)  10.6 us
  transfers between devices with their start and end apart: 4, of which 3 were waited for; matrix products, arithmetic and copies ran while one was open for 48% of the time, Pallas kernels for 0%

commit v1 on v0

--- a/solution.py
+++ b/solution.py
@@ -1,6 +1,10 @@
+import functools
+
 import jax
 import jax.numpy as jnp
 from jax import lax
+from jax.experimental import pallas as pl
+from jax.experimental.pallas import tpu as pltpu
 from jax.sharding import PartitionSpec as P
 
 CAP = 2
@@ -29,36 +33,121 @@
     return joined_along(pieces, concats[1])
 
 
-def tile_sums(user_table, sub_table, nz_user, nz_sub, nz_value):
-    tile_count, tile_width = nz_user.shape
-    block_tiles = min(tile_count, 128)
-    block_count = tile_count // block_tiles
-
-    def one_block(block_args):
-        users_block, subs_block, vals_block = block_args
-        user_rows = jnp.take(user_table, users_block, axis=0).astype(jnp.float32)
-        sub_rows = jnp.take(sub_table, subs_block, axis=0).astype(jnp.float32)
-        return jnp.sum(user_rows * sub_rows * vals_block[:, :, None], axis=1)
-
-    block_sums = lax.map(
-        one_block,
-        (
-            nz_user.reshape(block_count, block_tiles, tile_width),
-            nz_sub.reshape(block_count, block_tiles, tile_width),
-            nz_value.reshape(block_count, block_tiles, tile_width),
-        ),
-    )
-    return block_sums.reshape(tile_count, block_sums.shape[2])
+NT = 8
+CH = NT * 128
+BLOCK = 640
+
+
+def merged(rows):
+    sublane = lax.broadcasted_iota(jnp.int32, (8, 128), 0)
+    out = jnp.broadcast_to(rows[0], (8, 128))
+    for k in range(1, 8):
+        out = jnp.where(sublane == k, jnp.broadcast_to(rows[k], (8, 128)), out)
+    return out
+
+
+def tile_kernel(devs, tiles, idx_hbm, w0_ref, w1_ref, tab_hbm, out_ref, utab, stab, stage, bufa, bufb, sem, isem):
+    f32 = jnp.float32
+    bufs = (bufa, bufb)
+    steps = tiles // (2 * NT)
+
+    def icopy(c, b):
+        return pltpu.make_async_copy(idx_hbm.at[pl.ds(c * 2 * CH, 2 * CH)], bufs[b], isem.at[b])
+
+    icopy(0, 0).start()
+    icopy(1, 1).start()
+
+    def tcopy(d):
+        rows = pl.ds(pl.multiple_of(d * BLOCK, 128), BLOCK)
+        return pltpu.make_async_copy(tab_hbm.at[rows, :], stage.at[rows, :], sem.at[d])
+
+    for d in range(devs):
+        tcopy(d).start()
+    low = lax.broadcasted_iota(jnp.int32, (128, 128), 1) < 64
+
+    def conv(d, carry):
+        tcopy(d).wait()
+        base = pl.multiple_of(d * BLOCK, 128)
+        utab[pl.ds(pl.multiple_of(d * 512, 512), 512), :] = stage[pl.ds(base, 512), :].astype(f32)
+        x = stage[pl.ds(base + 512, 128), :].astype(f32)
+        r = pltpu.roll(x, 64, 1)
+        stab[pl.ds(pl.multiple_of(d * 256, 256), 128), :] = jnp.where(low, x, r)
+        stab[pl.ds(pl.multiple_of(d * 256 + 128, 128), 128), :] = jnp.where(low, r, x)
+        return carry
+
+    lax.fori_loop(0, devs, conv, 0)
+
+    def tile(buf, j, t):
+        w0 = w0_ref[pl.ds(t, 1), :]
+        w1 = w1_ref[pl.ds(t, 1), :]
+        w = jnp.concatenate([jnp.broadcast_to(w0, (64, 128)), jnp.broadcast_to(w1, (64, 128))], 0).T
+        acc = jnp.zeros((8, 128), f32)
+        for g in range(16):
+            first = j * 128 + g * 8
+            ur = merged([utab[pl.ds(buf[first + k], 1), :] for k in range(8)])
+            sr = merged([stab[pl.ds(buf[CH + first + k], 1), :] for k in range(8)])
+            acc = acc + ur * sr * w[g * 8 : (g + 1) * 8, :]
+        out_ref[pl.ds(t, 1), :] = jnp.sum(acc, axis=0, keepdims=True)
+
+    def body(i, carry):
+        for b in range(2):
+            c = i * 2 + b
+            icopy(c, b).wait()
+            for j in range(NT):
+                tile(bufs[b], j, c * NT + j)
+
+            @pl.when(i < steps - 1)
+            def _():
+                icopy(c + 2, b).start()
+
+        return carry
+
+    lax.fori_loop(0, steps, body, 0)
+
+
+def tile_sums(table, nz_user, nz_sub, nz_value):
+    tiles, width = nz_user.shape
+    devs = lax.axis_size("dev")
+    user_row = (nz_user >> 10) * 512 + (nz_user & 511)
+    high = ((nz_user >> 9) & 1) == 1
+    w1 = jnp.where(high, nz_value, 0.0)
+    w0 = jnp.where(high, 0.0, nz_value)
+    idx = jnp.concatenate([user_row.reshape(-1, 1, CH), nz_sub.reshape(-1, 1, CH)], axis=1).reshape(-1)
+    out = pl.pallas_call(
+        functools.partial(tile_kernel, devs, tiles),
+        out_shape=jax.ShapeDtypeStruct((tiles, 128), jnp.float32),
+        in_specs=[
+            pl.BlockSpec(memory_space=pltpu.HBM),
+            pl.BlockSpec(memory_space=pltpu.VMEM),
+            pl.BlockSpec(memory_space=pltpu.VMEM),
+            pl.BlockSpec(memory_space=pltpu.HBM),
+        ],
+        out_specs=pl.BlockSpec(memory_space=pltpu.VMEM),
+        scratch_shapes=[
+            pltpu.VMEM((devs * 512, 128), jnp.float32),
+            pltpu.VMEM((devs * 256, 128), jnp.float32),
+            pltpu.VMEM((devs * BLOCK, 128), jnp.bfloat16),
+            pltpu.SMEM((2 * CH,), jnp.int32),
+            pltpu.SMEM((2 * CH,), jnp.int32),
+            pltpu.SemaphoreType.DMA((devs,)),
+            pltpu.SemaphoreType.DMA((2,)),
+        ],
+        compiler_params=pltpu.CompilerParams(vmem_limit_bytes=44 * 2**20),
+        name="tile_sums",
+    )(idx, w0, w1, table)
+    return out[:, :64] + out[:, 64:]
+
+
+def packed(factor):
+    rows = jnp.transpose(factor)
+    half = rows.shape[0] // 2
+    return jnp.concatenate([rows[:half], rows[half:]], axis=1)
 
 
 def shards(nz_user, nz_sub, nz_value, tile_word, word_owner, user_factor, sub_factor):
-    users_all, subs_all = (
-        lax.all_gather(user_factor, "dev", axis=1, tiled=True),
-        lax.all_gather(sub_factor, "dev", axis=1, tiled=True),
-    )
-    user_table = jnp.transpose(users_all)
-    sub_table = jnp.transpose(subs_all)
-    tile_rows = tile_sums(user_table, sub_table, nz_user, nz_sub, nz_value)
+    mine = jnp.concatenate([packed(user_factor), packed(sub_factor)], axis=0)
+    table = lax.all_gather(mine, "dev", axis=0, tiled=True)
+    tile_rows = tile_sums(table, nz_user, nz_sub, nz_value)
     tile_count, rank_width = tile_rows.shape
     grp_size = lax.axis_size("grp")
     dev_size = lax.axis_size("dev")

time: 298 us -> 157 us (0.53)
  local copies, waits for them, and re-layouts: 129 us -> 5.9 us
  waiting for transfers between devices: 113 us -> 79 us
  Pallas kernels: 0 us -> 25.5 us
  other arithmetic: 15.4 us -> 6.48 us
    gather x2 -> x0, local copies, waits for them, and re-layouts: 121 us -> none  [the longest x1 63.3 us: one_block(): user_rows = jnp.take(user_table, users_block, axis=0).astype(jnp.float32)]
    all_gather x2 -> x1, waiting for transfers between devices: 102 us -> 67.5 us  [shards(): table = lax.all_gather(mine, 'dev', axis=0, tiled=True)]
    pallas_call x0 -> x1, Pallas kernels: none -> 25.5 us  [tile_sums(): pl.pallas_call(functools.partial(tile_kernel, devs, tiles), out_shape=jax...]
    reduce_sum x1 -> x0, other arithmetic: 10.6 us -> none  [one_block(): return jnp.sum(user_rows * sub_rows * vals_block[:, :, None], axis=1)]
  transfers between devices with their start and end apart: 4 -> 3, of which waited for: 3 -> 2; matrix products, arithmetic and copies ran while one was open for 48% -> 7% of each run, Pallas kernels for 0% -> 16%
where the time goes in v1:
time: 157 us
  waiting for transfers between devices  79 us (50%)
  Pallas kernels  25.5 us (16%)
  starting transfers between devices  24.2 us (15%)
  between operations  13.5 us (9%)
  other arithmetic  6.48 us (4%)
  local copies, waits for them, and re-layouts  5.9 us (4%)
  matrix products  2.43 us (2%)
    all_gather x1, waiting for transfers between devices, shards(): table = lax.all_gather(mine, 'dev', axis=0, tiled=True)  67.5 us
    pallas_call x1, Pallas kernels, tile_sums(): pl.pallas_call(functools.partial(tile_kernel, devs, tiles), out_shape=jax...  25.5 us
    all_to_all x2, starting transfers between devices, exchange_both(): lax.all_to_all(pieces, axis, split_axis=0, concat_axis=0, tiled=True)  24.2 us
    all_to_all x2, waiting for transfers between devices, exchange_both(): lax.all_to_all(pieces, axis, split_axis=0, concat_axis=0, tiled=True)  11.5 us
  transfers between devices with their start and end apart: 3, of which 2 were waited for; matrix products, arithmetic and copies ran while one was open for 7% of the time, Pallas kernels for 16%

profile of v1, /device:TPU:1, one launch (start us, length us, event | category | flops | bytes accessed | tf_op | source)
XLA Modules:
  0.0 157.0 jit_solution(6406752604417263450)
XLA Ops:
  6.5 0.0 copy-start
  6.5 0.0 all-gather.2.cloned.1.call-start
  6.5 1.1 copy.54
  7.7 0.9 copy.55
  8.6 0.8 maximum_maximum_fusion
  9.4 0.0 all-gather.2.cloned.1.call-update
  9.4 0.7 compare_select_fusion
  10.1 0.0 copy-done
  10.1 1.1 gather_fusion
  11.2 0.7 fusion.17
  11.9 0.3 fusion
  12.2 0.7 add_select_fusion
  12.9 0.1 convert_reduce_fusion
  13.0 0.3 fusion.1
  13.3 0.1 reshape_reshape.14
  13.4 0.7 copy.65
  14.2 15.6 %all-to-all-start.1 = ((f32[256,1,1,2]{3,2,1,0:T(1,128)}), f32[256,1,1,2]{3,2,1,0:T(1,128)S(1)}, u32[]{:S(2)}, u32[]{:S(2)}) async-start(f32[256,1,1,2]{3,2,1,0:T(1,128)} %bitcast.12), calls=%async_computation.1 | async-start | bytes 262144 | tf_op jit(solution)/shard_map/all_to_all | solution.py:31
  29.8 0.9 and_add_fusion
  30.7 0.9 add_bitcast_fusion
  31.7 0.9 broadcast_select_fusion
  32.6 0.9 broadcast_select_fusion.1.w0_ref
  33.4 67.5 %all-gather.2.cloned.1.call-done.tab_hbm = bf16[40960,128]{1,0:T(8,128)(2,1)} async-done(((bf16[640,128]{1,0:T(8,128)(2,1)}), bf16[40960,128]{1,0:T(8,128)(2,1)}) %all-gather.2.cloned.1.call-update) | async-done | bytes 10485776 | tf_op jit(solution)/shard_map/all_gather | solution.py:149
  100.9 25.5 %tile_sums.1 = f32[128,128]{1,0:T(8,128)S(1)} custom-call(s32[32768]{0:T(1024)S(1)} %bitcast.33, f32[128,128]{1,0:T(8,128)S(1)} %broadcast_select_fusion.1.w0_ref, f32[128,128]{1,0:T(8,128)S(1)} %get-tuple-element.8.w1_ref, bf16[40960,128]{1,0:T(8,128)(2,1)} %all-gather.2.cloned.1.call-done.tab_hbm), custom_call_target="tpu_custom_call" | custom-call | tf_op jit(solution)/shard_map/tile_sums/pallas_call | solution.py:116
  126.4 0.5 fusion.2
  126.8 0.1 reshape_reshape.12
  126.9 0.7 copy.57
  127.7 0.0 all-to-all-done.1
  127.7 8.6 %all-to-all-start = ((f32[256,1,1,128]{3,2,1,0:T(1,128)}), f32[256,1,1,128]{3,2,1,0:T(1,128)S(1)}, u32[]{:S(2)}, u32[]{:S(2)}) async-start(f32[256,1,1,128]{3,2,1,0:T(1,128)} %bitcast.6), calls=%async_computation | async-start | bytes 262144 | tf_op jit(solution)/shard_map/all_to_all | solution.py:31
  136.3 0.1 copy.62
  136.3 0.1 convert_element_type.35
  136.5 0.6 copy.63
  137.0 0.2 convert_element_type.37
  137.2 0.3 fusion.11
  137.5 11.5 %all-to-all-done = f32[256,1,1,128]{3,2,1,0:T(1,128)S(1)} async-done(((f32[256,1,1,128]{3,2,1,0:T(1,128)}), f32[256,1,1,128]{3,2,1,0:T(1,128)S(1)}, u32[]{:S(2)}, u32[]{:S(2)}) %all-to-all-start) | async-done | bytes 131104 | tf_op jit(solution)/shard_map/all_to_all | solution.py:31
  149.0 0.1 reshape_reshape_reshape.4
  149.1 1.1 convolution_add_fusion
  (7 shorter events, 0.1 us)
Async XLA Ops:
  6.5 3.5 %copy-start = (s32[16384]{0:T(1024)S(1)}, s32[16384]{0:T(1024)}, u32[]{:S(2)}) copy-start(s32[16384]{0:T(1024)} %param.11) | copy-start | bytes 196612
  6.5 94.4 %all-gather.2.cloned.1.call-start = ((), (), s32[]{:S(2)}) async-start(), calls=%async_computation.2 | async-start | bytes 10649600 | tf_op jit(solution)/shard_map/all_gather | solution.py:149
  14.2 113.5 %all-to-all-start.1 = ((f32[256,1,1,2]{3,2,1,0:T(1,128)}), f32[256,1,1,2]{3,2,1,0:T(1,128)S(1)}, u32[]{:S(2)}, u32[]{:S(2)}) async-start(f32[256,1,1,2]{3,2,1,0:T(1,128)} %bitcast.12), calls=%async_computation.1 | async-start | bytes 262144 | tf_op jit(solution)/shard_map/all_to_all | solution.py:31
  127.7 21.3 %all-to-all-start = ((f32[256,1,1,128]{3,2,1,0:T(1,128)}), f32[256,1,1,128]{3,2,1,0:T(1,128)S(1)}, u32[]{:S(2)}, u32[]{:S(2)}) async-start(f32[256,1,1,128]{3,2,1,0:T(1,128)} %bitcast.6), calls=%async_computation | async-start | bytes 262144 | tf_op jit(solution)/shard_map/all_to_all | solution.py:31
Sparse Core Ops, SparseCore 0:
  10.1 90.7 all-gather.1

commit v2 on v1

--- a/solution.py
+++ b/solution.py
@@ -35,7 +35,9 @@
 
 NT = 8
 CH = NT * 128
-BLOCK = 640
+SHARD_U = 256
+SHARD_S = 64
+SHARD = SHARD_U + SHARD_S
 
 
 def merged(rows):
@@ -46,8 +48,9 @@
     return out
 
 
-def tile_kernel(devs, tiles, idx_hbm, w0_ref, w1_ref, tab_hbm, out_ref, utab, stab, stage, bufa, bufb, sem, isem):
+def tile_kernel(counts, tiles, idx_hbm, w0_ref, w1_ref, *refs):
     f32 = jnp.float32
+    pieces, (out_ref, utab, stab, bufa, bufb, isem) = refs[: len(counts)], refs[len(counts) :]
     bufs = (bufa, bufb)
     steps = tiles // (2 * NT)
 
@@ -56,26 +59,24 @@
 
     icopy(0, 0).start()
     icopy(1, 1).start()
-
-    def tcopy(d):
-        rows = pl.ds(pl.multiple_of(d * BLOCK, 128), BLOCK)
-        return pltpu.make_async_copy(tab_hbm.at[rows, :], stage.at[rows, :], sem.at[d])
-
-    for d in range(devs):
-        tcopy(d).start()
-    low = lax.broadcasted_iota(jnp.int32, (128, 128), 1) < 64
-
-    def conv(d, carry):
-        tcopy(d).wait()
-        base = pl.multiple_of(d * BLOCK, 128)
-        utab[pl.ds(pl.multiple_of(d * 512, 512), 512), :] = stage[pl.ds(base, 512), :].astype(f32)
-        x = stage[pl.ds(base + 512, 128), :].astype(f32)
-        r = pltpu.roll(x, 64, 1)
-        stab[pl.ds(pl.multiple_of(d * 256, 256), 128), :] = jnp.where(low, x, r)
-        stab[pl.ds(pl.multiple_of(d * 256 + 128, 128), 128), :] = jnp.where(low, r, x)
-        return carry
-
-    lax.fori_loop(0, devs, conv, 0)
+    low = lax.broadcasted_iota(jnp.int32, (SHARD_S, 128), 1) < 64
+    first_slot = 0
+    for piece, count in zip(pieces, counts):
+
+        def conv(i, carry, piece=piece, first_slot=first_slot):
+            src = pl.multiple_of(i * SHARD, SHARD_S)
+            slot = first_slot + i
+            urow = pl.multiple_of(slot * SHARD_U, SHARD_U)
+            srow = pl.multiple_of(slot * 2 * SHARD_S, 2 * SHARD_S)
+            utab[pl.ds(urow, SHARD_U), :] = piece[pl.ds(src, SHARD_U), :].astype(f32)
+            x = piece[pl.ds(src + SHARD_U, SHARD_S), :].astype(f32)
+            r = pltpu.roll(x, 64, 1)
+            stab[pl.ds(srow, SHARD_S), :] = jnp.where(low, x, r)
+            stab[pl.ds(srow + SHARD_S, SHARD_S), :] = jnp.where(low, r, x)
+            return carry
+
+        lax.fori_loop(0, count, conv, 0)
+        first_slot += count
 
     def tile(buf, j, t):
         w0 = w0_ref[pl.ds(t, 1), :]
@@ -105,37 +106,70 @@
     lax.fori_loop(0, steps, body, 0)
 
 
-def tile_sums(table, nz_user, nz_sub, nz_value):
+def slot_of(dev, color):
+    me = lax.axis_index("dev")
+    dz = ((dev >> 3) - (me >> 3)) & 7
+    dx = ((dev >> 1) - (me >> 1)) & 3
+    other = (dev ^ me) & 1
+    return (color * 2 + other) * 32 + jnp.where(color == 1, dx * 8 + dz, dz * 4 + dx)
+
+
+def tile_sums(pieces, nz_user, nz_sub, nz_value):
     tiles, width = nz_user.shape
-    devs = lax.axis_size("dev")
-    user_row = (nz_user >> 10) * 512 + (nz_user & 511)
+    counts = tuple(p.shape[0] // SHARD for p in pieces)
+    slots = sum(counts)
+    user_row = slot_of(nz_user >> 10, (nz_user >> 8) & 1) * SHARD_U + (nz_user & 255)
+    sub_row = (slot_of(nz_sub >> 8, (nz_sub >> 6) & 1) * 2 + ((nz_sub >> 7) & 1)) * SHARD_S + (nz_sub & 63)
     high = ((nz_user >> 9) & 1) == 1
     w1 = jnp.where(high, nz_value, 0.0)
     w0 = jnp.where(high, 0.0, nz_value)
-    idx = jnp.concatenate([user_row.reshape(-1, 1, CH), nz_sub.reshape(-1, 1, CH)], axis=1).reshape(-1)
+    idx = jnp.concatenate([user_row.reshape(-1, 1, CH), sub_row.reshape(-1, 1, CH)], axis=1).reshape(-1)
+    vmem = pl.BlockSpec(memory_space=pltpu.VMEM)
     out = pl.pallas_call(
-        functools.partial(tile_kernel, devs, tiles),
+        functools.partial(tile_kernel, counts, tiles),
         out_shape=jax.ShapeDtypeStruct((tiles, 128), jnp.float32),
-        in_specs=[
-            pl.BlockSpec(memory_space=pltpu.HBM),
-            pl.BlockSpec(memory_space=pltpu.VMEM),
-            pl.BlockSpec(memory_space=pltpu.VMEM),
-            pl.BlockSpec(memory_space=pltpu.HBM),
-        ],
-        out_specs=pl.BlockSpec(memory_space=pltpu.VMEM),
+        in_specs=[pl.BlockSpec(memory_space=pltpu.HBM), vmem, vmem] + [vmem] * len(pieces),
+        out_specs=vmem,
         scratch_shapes=[
-            pltpu.VMEM((devs * 512, 128), jnp.float32),
-            pltpu.VMEM((devs * 256, 128), jnp.float32),
-            pltpu.VMEM((devs * BLOCK, 128), jnp.bfloat16),
+            pltpu.VMEM((slots * SHARD_U, 128), jnp.float32),
+            pltpu.VMEM((slots * 2 * SHARD_S, 128), jnp.float32),
             pltpu.SMEM((2 * CH,), jnp.int32),
             pltpu.SMEM((2 * CH,), jnp.int32),
-            pltpu.SemaphoreType.DMA((devs,)),
             pltpu.SemaphoreType.DMA((2,)),
         ],
         compiler_params=pltpu.CompilerParams(vmem_limit_bytes=44 * 2**20),
         name="tile_sums",
-    )(idx, w0, w1, table)
+    )(idx, w0, w1, *pieces)
     return out[:, :64] + out[:, 64:]
+
+
+def sent(value, dz, dx, dc=0):
+    devs = lax.axis_size("dev")
+    pairs = [(d, ((d // 8 + dz) % 8) * 8 + ((d % 8 // 2 + dx) % 4) * 2 + ((d % 2) ^ dc)) for d in range(devs)]
+    return lax.ppermute(value, "dev", pairs)
+
+
+def along_z(block):
+    half = block.shape[0] // 2
+    up, down = [], []
+    p = m = block
+    for _ in range(3):
+        p, m = sent(p, 1, 0), sent(m, -1, 0)
+        up.append(p)
+        down.append(m)
+    return [block] + down + [sent(p[:half], 1, 0), sent(m[half:], -1, 0)] + up[::-1]
+
+
+def gathered(mine_a, mine_b):
+    block_a = jnp.concatenate([mine_a, sent(mine_a, 0, -1), sent(mine_a, 0, 2), sent(mine_a, 0, 1)], axis=0)
+    pieces_a = along_z(block_a)
+    block_b = jnp.concatenate(along_z(mine_b), axis=0)
+    half = block_b.shape[0] // 2
+    p, m = sent(block_b, 0, 1), sent(block_b, 0, -1)
+    pieces_b = [block_b, m, sent(p[:half], 0, 1), sent(m[half:], 0, -1), p]
+    other_a = [sent(v, 0, 0, 1) for v in pieces_a]
+    other_b = [sent(v, 0, 0, 1) for v in pieces_b]
+    return pieces_a + other_a + pieces_b + other_b
 
 
 def packed(factor):
@@ -145,9 +179,10 @@
 
 
 def shards(nz_user, nz_sub, nz_value, tile_word, word_owner, user_factor, sub_factor):
-    mine = jnp.concatenate([packed(user_factor), packed(sub_factor)], axis=0)
-    table = lax.all_gather(mine, "dev", axis=0, tiled=True)
-    tile_rows = tile_sums(table, nz_user, nz_sub, nz_value)
+    users, subs = packed(user_factor), packed(sub_factor)
+    mine_a = jnp.concatenate([users[:SHARD_U], subs[:SHARD_S]], axis=0)
+    mine_b = jnp.concatenate([users[SHARD_U:], subs[SHARD_S:]], axis=0)
+    tile_rows = tile_sums(gathered(mine_a, mine_b), nz_user, nz_sub, nz_value)
     tile_count, rank_width = tile_rows.shape
     grp_size = lax.axis_size("grp")
     dev_size = lax.axis_size("dev")
@@ -175,26 +210,16 @@
     send_slot = jnp.where(owned, devices_all * CAP, owner_dev * CAP + position)
     slot_ids = jnp.arange(devices_all * CAP, dtype=jnp.int32)
     slot_table = (send_slot[:, None] == slot_ids[None, :]).astype(jnp.float32)
-    send_rows = jnp.einsum("ts,tr->sr", slot_table, tile_rows, precision=lax.Precision.HIGHEST)
-    filled = jnp.sum(slot_table, axis=0)
-    send_ids = (
-        jnp.dot(
-            local_row.astype(jnp.float32),
-            slot_table,
-            precision=lax.Precision.HIGHEST,
-            preferred_element_type=jnp.float32,
-        )
-        + filled
-        - 1.0
-    )
-    send_rows = send_rows.reshape(grp_size, dev_size, CAP * rank_width)
-    send_ids = send_ids.reshape(grp_size, dev_size, CAP)
-    got_rows, got_ids = (
-        exchange_both(send_rows, ("dev", "grp"), ("dev", "grp"), (1, 0), (1, 0)),
-        exchange_both(send_ids, ("dev", "grp"), ("dev", "grp"), (1, 0), (1, 0)),
-    )
-    got_rows = got_rows.reshape(devices_all * CAP, rank_width)
-    got_ids = got_ids.reshape(devices_all * CAP).astype(jnp.int32)
+    with_ids = jnp.concatenate(
+        [tile_rows, (local_row + 1).astype(jnp.float32)[:, None], jnp.zeros((tile_count, 127 - rank_width), jnp.float32)],
+        axis=1,
+    )
+    send = jnp.einsum("ts,tr->sr", slot_table, with_ids, precision=lax.Precision.HIGHEST)
+    send = send.reshape(grp_size, dev_size, CAP * 128)
+    got = exchange_both(send, ("dev", "grp"), ("dev", "grp"), (1, 0), (1, 0))
+    got = got.reshape(devices_all * CAP, 128)
+    got_rows = got[:, :rank_width]
+    got_ids = got[:, rank_width].astype(jnp.int32) - 1
     got_table = (got_ids[:, None] == columns[None, :]).astype(jnp.float32)
     far_part = jnp.einsum("sr,sk->rk", got_rows, got_table, precision=lax.Precision.HIGHEST)
     return own_part + far_part

time: 157 us -> 154 us (0.981)
  waiting for transfers between devices: 79 us -> 17 us
  starting transfers between devices: 24.2 us -> 55.8 us
  blocking collectives: 0 us -> 24.9 us
  between operations: 13.5 us -> 0.51 us
  local copies, waits for them, and re-layouts: 5.9 us -> 18.2 us
  Pallas kernels: 25.5 us -> 30.9 us
  other arithmetic: 6.48 us -> 3.95 us
    all_gather x1 -> x0, waiting for transfers between devices: 67.5 us -> none  [shards(): table = lax.all_gather(mine, 'dev', axis=0, tiled=True)]
    ppermute x0 -> x37, starting transfers between devices: none -> 55.8 us  [sent(): return lax.ppermute(value, 'dev', pairs)]
    all_to_all x0 -> x1, blocking collectives: none -> 24.9 us  [exchange_both(): lax.all_to_all(pieces, axis, split_axis=0, concat_axis=0, tiled=True)]
    all_to_all x2 -> x0, starting transfers between devices: 24.2 us -> none  [exchange_both(): lax.all_to_all(pieces, axis, split_axis=0, concat_axis=0, tiled=True)]
    ppermute x0 -> x37, waiting for transfers between devices: none -> 17 us  [sent(): return lax.ppermute(value, 'dev', pairs)]
    unnamed x5 -> x68, local copies, waits for them, and re-layouts: 1.99 us -> 14.4 us
    all_to_all x2 -> x0, waiting for transfers between devices: 11.5 us -> none  [exchange_both(): lax.all_to_all(pieces, axis, split_axis=0, concat_axis=0, tiled=True)]
    pallas_call x1, Pallas kernels: 25.5 us -> 30.9 us  [tile_sums(): pl.pallas_call(functools.partial(tile_kernel, counts, tiles), out_shape=j...]
  transfers between devices with their start and end apart: 3 -> 37, of which waited for: 2 -> 7; matrix products, arithmetic and copies ran while one was open for 7% -> 5% of each run, Pallas kernels for 16% -> 0%
where the time goes in v2:
time: 154 us; the launch traced here: 153 us
  starting transfers between devices  55.8 us (36%)
  Pallas kernels  30.9 us (20%)
  blocking collectives  24.9 us (16%)
  local copies, waits for them, and re-layouts  18.2 us (12%)
  waiting for transfers between devices  17 us (11%)
  other arithmetic  3.95 us (3%)
  matrix products  2.15 us (1%)
    ppermute x37, starting transfers between devices, sent(): return lax.ppermute(value, 'dev', pairs)  55.8 us
    pallas_call x1, Pallas kernels, tile_sums(): pl.pallas_call(functools.partial(tile_kernel, counts, tiles), out_shape=j...  30.9 us
    all_to_all x1, blocking collectives, exchange_both(): lax.all_to_all(pieces, axis, split_axis=0, concat_axis=0, tiled=True)  24.9 us
    ppermute x37, waiting for transfers between devices, sent(): return lax.ppermute(value, 'dev', pairs)  17 us
    unnamed x68, local copies, waits for them, and re-layouts  14.4 us
  transfers between devices with their start and end apart: 37, of which 7 were waited for; matrix products, arithmetic and copies ran while one was open for 5% of the time, Pallas kernels for 0%

profile of v2, /device:TPU:1, one launch (start us, length us, event | category | flops | bytes accessed | tf_op | source)
XLA Modules:
  0.0 153.4 jit_solution(7572152076254339008)
XLA Ops:
  0.0 1.1 copy.20
  1.2 0.7 copy-done.21
  2.2 3.4 %collective-permute-start = (bf16[320,128]{1,0:T(8,128)(2,1)S(1)}, bf16[320,128]{1,0:T(8,128)(2,1)S(1)}, u32[]{:S(2)}, u32[]{:S(2)}) collective-permute-start(bf16[320,128]{1,0:T(8,128)(2,1)S(1)} %pad_maximum_fusion), channel_id=1, source_target_pairs={{0,6},{1,7},{2,0},{3,1},{4,2},{5,3},{6,4},{7,5},{8,14},{9,15},{10,... | collective-permute-start | bytes 245768 | tf_op jit(solution)/shard_map/ppermute | solution.py:149
  5.6 5.6 %collective-permute-start.20 = (bf16[320,128]{1,0:T(8,128)(2,1)S(1)}, bf16[320,128]{1,0:T(8,128)(2,1)S(1)}, u32[]{:S(2)}, u32[]{:S(2)}) collective-permute-start(bf16[320,128]{1,0:T(8,128)(2,1)S(1)} %pad_maximum_fusion.1), channel_id=1, source_target_pairs={{0,56},{1,57},{2,58},{3,59},{4,60},{5,61},{6,62},{7,63},{8,0},{9,1... | collective-permute-start | bytes 245768 | tf_op jit(solution)/shard_map/ppermute | solution.py:149
  11.2 0.5 collective-permute-start.1
  11.7 0.6 collective-permute-start.2
  12.3 3.7 %collective-permute-done.1 = bf16[320,128]{1,0:T(8,128)(2,1)S(1)} collective-permute-done((bf16[320,128]{1,0:T(8,128)(2,1)S(1)}, bf16[320,128]{1,0:T(8,128)(2,1)S(1)}, u32[]{:S(2)}, u32[]{:S(2)}) %collective-permute-start.1) | collective-permute-done | bytes 81952 | tf_op jit(solution)/shard_map/ppermute | solution.py:149
  16.1 1.1 collective-permute-done.2
  17.3 2.7 %collective-permute-start.3 = (bf16[1280,128]{1,0:T(8,128)(2,1)S(1)}, bf16[1280,128]{1,0:T(8,128)(2,1)}, u32[]{:S(2)}, u32[]{:S(2)}) collective-permute-start(bf16[1280,128]{1,0:T(8,128)(2,1)S(1)} %constant_dynamic-update-slice_fusion.refs_0_), channel_id=1, source_target_pairs={{0,56},{1,57},{2,58},{3,59},{4,60},{5,61},{6,62},{7,63},{8,0},{9,1... | collective-permute-start | bytes 983048 | tf_op jit(solution)/shard_map/ppermute | solution.py:149
  20.0 2.7 %collective-permute-start.11 = (bf16[1280,128]{1,0:T(8,128)(2,1)S(1)}, bf16[1280,128]{1,0:T(8,128)(2,1)S(1)}, u32[]{:S(2)}, u32[]{:S(2)}) collective-permute-start(bf16[1280,128]{1,0:T(8,128)(2,1)S(1)} %constant_dynamic-update-slice_fusion.refs_0_), channel_id=1, source_target_pairs={{0,1},{1,0},{2,3},{3,2},{4,5},{5,4},{6,7},{7,6},{8,9},{9,8},{10,11... | collective-permute-start | bytes 983048 | tf_op jit(solution)/shard_map/ppermute | solution.py:149
  22.7 1.7 %collective-permute-start.21 = (bf16[320,128]{1,0:T(8,128)(2,1)S(1)}, bf16[320,128]{1,0:T(8,128)(2,1)S(1)}, u32[]{:S(2)}, u32[]{:S(2)}) collective-permute-start(bf16[320,128]{1,0:T(8,128)(2,1)S(1)} %collective-permute-done.20), channel_id=1, source_target_pairs={{0,56},{1,57},{2,58},{3,59},{4,60},{5,61},{6,62},{7,63},{8,0},{9,1... | collective-permute-start | bytes 245768 | tf_op jit(solution)/shard_map/ppermute | solution.py:149
  24.4 2.9 %collective-permute-done.21 = bf16[320,128]{1,0:T(8,128)(2,1)S(1)} collective-permute-done((bf16[320,128]{1,0:T(8,128)(2,1)S(1)}, bf16[320,128]{1,0:T(8,128)(2,1)S(1)}, u32[]{:S(2)}, u32[]{:S(2)}) %collective-permute-start.21) | collective-permute-done | bytes 81952 | tf_op jit(solution)/shard_map/ppermute | solution.py:149
  27.3 2.9 %collective-permute-start.22 = (bf16[320,128]{1,0:T(8,128)(2,1)S(1)}, bf16[320,128]{1,0:T(8,128)(2,1)S(1)}, u32[]{:S(2)}, u32[]{:S(2)}) collective-permute-start(bf16[320,128]{1,0:T(8,128)(2,1)S(1)} %collective-permute-done.21), channel_id=1, source_target_pairs={{0,56},{1,57},{2,58},{3,59},{4,60},{5,61},{6,62},{7,63},{8,0},{9,1... | collective-permute-start | bytes 245768 | tf_op jit(solution)/shard_map/ppermute | solution.py:149
  30.1 4.5 %collective-permute-done.25 = bf16[320,128]{1,0:T(8,128)(2,1)S(1)} collective-permute-done((bf16[320,128]{1,0:T(8,128)(2,1)S(1)}, bf16[320,128]{1,0:T(8,128)(2,1)S(1)}, u32[]{:S(2)}, u32[]{:S(2)}) %collective-permute-start.25) | collective-permute-done | bytes 81952 | tf_op jit(solution)/shard_map/ppermute | solution.py:149
  34.7 2.7 %collective-permute-start.27 = (bf16[160,128]{1,0:T(8,128)(2,1)S(1)}, bf16[160,128]{1,0:T(8,128)(2,1)S(1)}, u32[]{:S(2)}, u32[]{:S(2)}) collective-permute-start(bf16[160,128]{1,0:T(8,128)(2,1)S(1)} %slice.85), channel_id=1, source_target_pairs={{0,56},{1,57},{2,58},{3,59},{4,60},{5,61},{6,62},{7,63},{8,0},{9,1... | collective-permute-start | bytes 122888 | tf_op jit(solution)/shard_map/ppermute | solution.py:149
  37.3 1.4 collective-permute-done.26
  39.0 0.3 collective-permute-start.29
  39.3 2.7 %collective-permute-start.28 = (bf16[2560,128]{1,0:T(8,128)(2,1)S(1)}, bf16[2560,128]{1,0:T(8,128)(2,1)S(1)}, u32[]{:S(2)}, u32[]{:S(2)}) collective-permute-start(bf16[2560,128]{1,0:T(8,128)(2,1)S(1)} %constant_dynamic-update-slice_fusion.5.refs_18_), channel_id=1, source_target_pairs={{0,6},{1,7},{2,0},{3,1},{4,2},{5,3},{6,4},{7,5},{8,14},{9,15},{10,... | collective-permute-start | bytes 1966088 | tf_op jit(solution)/shard_map/ppermute | solution.py:149
  42.0 2.7 %collective-permute-start.4 = (bf16[1280,128]{1,0:T(8,128)(2,1)}, bf16[1280,128]{1,0:T(8,128)(2,1)}, u32[]{:S(2)}, u32[]{:S(2)}) collective-permute-start(bf16[1280,128]{1,0:T(8,128)(2,1)} %collective-permute-done.3.refs_1_), channel_id=1, source_target_pairs={{0,56},{1,57},{2,58},{3,59},{4,60},{5,61},{6,62},{7,63},{8,0},{9,1... | collective-permute-start | bytes 983048 | tf_op jit(solution)/shard_map/ppermute | solution.py:149
  44.6 0.1 and_add_fusion
  44.8 0.7 copy-done.3
  45.5 7.1 %collective-permute-start.32 = (bf16[2560,128]{1,0:T(8,128)(2,1)S(1)}, bf16[2560,128]{1,0:T(8,128)(2,1)S(1)}, u32[]{:S(2)}, u32[]{:S(2)}) collective-permute-start(bf16[2560,128]{1,0:T(8,128)(2,1)S(1)} %constant_dynamic-update-slice_fusion.5.refs_18_), channel_id=1, source_target_pairs={{0,1},{1,0},{2,3},{3,2},{4,5},{5,4},{6,7},{7,6},{8,9},{9,8},{10,11... | collective-permute-start | bytes 1966088 | tf_op jit(solution)/shard_map/ppermute | solution.py:149
  52.7 2.7 %collective-permute-start.5 = (bf16[1280,128]{1,0:T(8,128)(2,1)}, bf16[1280,128]{1,0:T(8,128)(2,1)S(1)}, u32[]{:S(2)}, u32[]{:S(2)}) collective-permute-start(bf16[1280,128]{1,0:T(8,128)(2,1)} %collective-permute-done.4.refs_2_), channel_id=1, source_target_pairs={{0,56},{1,57},{2,58},{3,59},{4,60},{5,61},{6,62},{7,63},{8,0},{9,1... | collective-permute-start | bytes 983048 | tf_op jit(solution)/shard_map/ppermute | solution.py:149
  55.4 5.0 %collective-permute-start.12 = (bf16[1280,128]{1,0:T(8,128)(2,1)}, bf16[1280,128]{1,0:T(8,128)(2,1)}, u32[]{:S(2)}, u32[]{:S(2)}) collective-permute-start(bf16[1280,128]{1,0:T(8,128)(2,1)} %collective-permute-done.3.refs_1_), channel_id=1, source_target_pairs={{0,1},{1,0},{2,3},{3,2},{4,5},{5,4},{6,7},{7,6},{8,9},{9,8},{10,11... | collective-permute-start | bytes 983048 | tf_op jit(solution)/shard_map/ppermute | solution.py:149
  60.5 1.7 %collective-permute-done.8.refs_6_ = bf16[1280,128]{1,0:T(8,128)(2,1)S(1)} collective-permute-done((bf16[1280,128]{1,0:T(8,128)(2,1)S(1)}, bf16[1280,128]{1,0:T(8,128)(2,1)S(1)}, u32[]{:S(2)}, u32[]{:S(2)}) %collective-permute-start.8) | collective-permute-done | bytes 327712 | tf_op jit(solution)/shard_map/ppermute | solution.py:149
  62.2 1.7 %collective-permute-start.13 = (bf16[1280,128]{1,0:T(8,128)(2,1)}, bf16[1280,128]{1,0:T(8,128)(2,1)}, u32[]{:S(2)}, u32[]{:S(2)}) collective-permute-start(bf16[1280,128]{1,0:T(8,128)(2,1)} %collective-permute-done.4.refs_2_), channel_id=1, source_target_pairs={{0,1},{1,0},{2,3},{3,2},{4,5},{5,4},{6,7},{7,6},{8,9},{9,8},{10,11... | collective-permute-start | bytes 983048 | tf_op jit(solution)/shard_map/ppermute | solution.py:149
  63.9 0.6 pad_clamp_fusion
  64.5 1.8 %gather_fusion = s32[128]{0:T(128)} fusion(s32[16384]{0:T(1024)S(1)} %copy-done, s32[1024]{0:T(1024)} %pad_clamp_fusion), kind=kCustom, calls=%fused_computation | custom fusion | bytes 1536 | tf_op jit(solution)/shard_map/jit(_take)/gather | solution.py:192
  66.3 1.2 convert_bitcast_fusion
  67.7 2.7 %collective-permute-start.31 = (bf16[1280,128]{1,0:T(8,128)(2,1)S(1)}, bf16[1280,128]{1,0:T(8,128)(2,1)}, u32[]{:S(2)}, u32[]{:S(2)}) collective-permute-start(bf16[1280,128]{1,0:T(8,128)(2,1)S(1)} %slice.87), channel_id=1, source_target_pairs={{0,6},{1,7},{2,0},{3,1},{4,2},{5,3},{6,4},{7,5},{8,14},{9,15},{10,... | collective-permute-start | bytes 983048 | tf_op jit(solution)/shard_map/ppermute | solution.py:149
  70.5 2.6 %collective-permute-start.10 = (bf16[640,128]{1,0:T(8,128)(2,1)S(1)}, bf16[640,128]{1,0:T(8,128)(2,1)S(1)}, u32[]{:S(2)}, u32[]{:S(2)}) collective-permute-start(bf16[640,128]{1,0:T(8,128)(2,1)S(1)} %slice.83), channel_id=1, source_target_pairs={{0,56},{1,57},{2,58},{3,59},{4,60},{5,61},{6,62},{7,63},{8,0},{9,1... | collective-permute-start | bytes 491528 | tf_op jit(solution)/shard_map/ppermute | solution.py:149
  73.1 1.7 %collective-permute-start.33 = (bf16[2560,128]{1,0:T(8,128)(2,1)S(1)}, bf16[2560,128]{1,0:T(8,128)(2,1)}, u32[]{:S(2)}, u32[]{:S(2)}) collective-permute-start(bf16[2560,128]{1,0:T(8,128)(2,1)S(1)} %collective-permute-done.28.refs_19_), channel_id=1, source_target_pairs={{0,1},{1,0},{2,3},{3,2},{4,5},{5,4},{6,7},{7,6},{8,9},{9,8},{10,11... | collective-permute-start | bytes 1966088 | tf_op jit(solution)/shard_map/ppermute | solution.py:149
  74.8 1.6 %collective-permute-done.9.refs_4_ = bf16[640,128]{1,0:T(8,128)(2,1)S(1)} collective-permute-done((bf16[640,128]{1,0:T(8,128)(2,1)S(1)}, bf16[640,128]{1,0:T(8,128)(2,1)S(1)}, u32[]{:S(2)}, u32[]{:S(2)}) %collective-permute-start.9) | collective-permute-done | bytes 163872 | tf_op jit(solution)/shard_map/ppermute | solution.py:149
  76.4 1.8 %collective-permute-start.36 = (bf16[2560,128]{1,0:T(8,128)(2,1)S(1)}, bf16[2560,128]{1,0:T(8,128)(2,1)}, u32[]{:S(2)}, u32[]{:S(2)}) collective-permute-start(bf16[2560,128]{1,0:T(8,128)(2,1)S(1)} %collective-permute-done.29.refs_22_), channel_id=1, source_target_pairs={{0,1},{1,0},{2,3},{3,2},{4,5},{5,4},{6,7},{7,6},{8,9},{9,8},{10,11... | collective-permute-start | bytes 1966088 | tf_op jit(solution)/shard_map/ppermute | solution.py:149
  78.3 0.3 fusion
  78.7 0.5 collective-permute-start.15
  79.2 0.3 collective-permute-start.16
  79.5 0.6 copy-done.11
  80.1 0.5 add_select_fusion
  80.7 0.7 copy-done.13
  81.3 0.3 collective-permute-start.17
  81.7 0.7 copy-done.15
  82.3 0.2 collective-permute-start.34
  82.5 0.7 copy-done.7
  83.2 0.3 collective-permute-start.35
  83.7 1.4 copy.22
  85.2 0.8 broadcast_select_fusion.1.w0_ref
  86.1 1.0 copy-done.2
  87.1 1.0 copy-done.4
  88.0 1.0 copy-done.6
  89.0 1.0 copy-done.8
  90.0 0.9 copy-done.10
  90.9 0.9 copy-done.12
  91.8 0.9 copy-done.14
  92.7 0.9 copy-done.16
  93.6 30.9 %tile_sums.1 = f32[128,128]{1,0:T(8,128)S(1)} custom-call(s32[32768]{0:T(1024)S(1)} %bitcast.23, f32[128,128]{1,0:T(8,128)S(1)} %broadcast_select_fusion.1.w0_ref, f32[128,128]{1,0:T(8,128)S(1)} %get-tuple-element.13.w1_ref, bf16[1280,128]{1,0:T(8,128)(2,1)S(1)} %copy-done.2, bf16[1280,128]{1,0:T(8,128)(2,1)} %collective-permute-done.3.refs_1_, ...), custom_call_target="tpu_custom_call" | custom-call | tf_op jit(solution)/shard_map/tile_sums/pallas_call | solution.py:128
  124.7 0.7 copy-done.19
  125.4 0.5 fusion.5
  125.9 0.3 copy.23
  126.2 24.9 %all_to_all.5 = f32[256,1,1,256]{3,1,2,0:T(1,128)S(1)} all-to-all(f32[256,1,1,256]{3,1,2,0:T(1,128)S(1)} %bitcast.25), channel_id=1, replica_groups=mesh['grp'=4,'dev'=64] {'dev','grp'}, dimensions={0} | all-to-all | bytes 524288 | tf_op jit(solution)/shard_map/all_to_all | solution.py:31
  151.2 0.2 fusion.2
  151.4 0.5 fusion.3
  151.9 0.6 copy-done.23
  152.5 0.9 convolution_add_fusion
  (117 shorter events, 1.8 us)
Async XLA Ops:
  0.0 64.5 %copy-start = (s32[16384]{0:T(1024)S(1)}, s32[16384]{0:T(1024)}, u32[]{:S(2)}) copy-start(s32[16384]{0:T(1024)} %param.11) | copy-start | bytes 196612
  1.1 0.8 copy-start.21
  2.2 10.1 %collective-permute-start = (bf16[320,128]{1,0:T(8,128)(2,1)S(1)}, bf16[320,128]{1,0:T(8,128)(2,1)S(1)}, u32[]{:S(2)}, u32[]{:S(2)}) collective-permute-start(bf16[320,128]{1,0:T(8,128)(2,1)S(1)} %pad_maximum_fusion), channel_id=1, source_target_pairs={{0,6},{1,7},{2,0},{3,1},{4,2},{5,3},{6,4},{7,5},{8,14},{9,15},{10,... | collective-permute-start | bytes 245768 | tf_op jit(solution)/shard_map/ppermute | solution.py:149
  5.6 17.1 %collective-permute-start.20 = (bf16[320,128]{1,0:T(8,128)(2,1)S(1)}, bf16[320,128]{1,0:T(8,128)(2,1)S(1)}, u32[]{:S(2)}, u32[]{:S(2)}) collective-permute-start(bf16[320,128]{1,0:T(8,128)(2,1)S(1)} %pad_maximum_fusion.1), channel_id=1, source_target_pairs={{0,56},{1,57},{2,58},{3,59},{4,60},{5,61},{6,62},{7,63},{8,0},{9,1... | collective-permute-start | bytes 245768 | tf_op jit(solution)/shard_map/ppermute | solution.py:149
  11.2 13.2 %collective-permute-start.23 = (bf16[320,128]{1,0:T(8,128)(2,1)S(1)}, bf16[320,128]{1,0:T(8,128)(2,1)S(1)}, u32[]{:S(2)}, u32[]{:S(2)}) collective-permute-start(bf16[320,128]{1,0:T(8,128)(2,1)S(1)} %pad_maximum_fusion.1), channel_id=1, source_target_pairs={{0,8},{1,9},{2,10},{3,11},{4,12},{5,13},{6,14},{7,15},{8,16},{9,17... | collective-permute-start | bytes 245768 | tf_op jit(solution)/shard_map/ppermute | solution.py:149
  11.2 4.9 %collective-permute-start.1 = (bf16[320,128]{1,0:T(8,128)(2,1)S(1)}, bf16[320,128]{1,0:T(8,128)(2,1)S(1)}, u32[]{:S(2)}, u32[]{:S(2)}) collective-permute-start(bf16[320,128]{1,0:T(8,128)(2,1)S(1)} %pad_maximum_fusion), channel_id=1, source_target_pairs={{0,4},{1,5},{2,6},{3,7},{4,0},{5,1},{6,2},{7,3},{8,12},{9,13},{10,... | collective-permute-start | bytes 245768 | tf_op jit(solution)/shard_map/ppermute | solution.py:149
  11.7 5.5 %collective-permute-start.2 = (bf16[320,128]{1,0:T(8,128)(2,1)S(1)}, bf16[320,128]{1,0:T(8,128)(2,1)S(1)}, u32[]{:S(2)}, u32[]{:S(2)}) collective-permute-start(bf16[320,128]{1,0:T(8,128)(2,1)S(1)} %pad_maximum_fusion), channel_id=1, source_target_pairs={{0,2},{1,3},{2,4},{3,5},{4,6},{5,7},{6,0},{7,1},{8,10},{9,11},{10,... | collective-permute-start | bytes 245768 | tf_op jit(solution)/shard_map/ppermute | solution.py:149
  17.2 20.1 %copy-start.1 = (bf16[1280,128]{1,0:T(8,128)(2,1)}, bf16[1280,128]{1,0:T(8,128)(2,1)S(1)}, u32[]{:S(2)}) copy-start(bf16[1280,128]{1,0:T(8,128)(2,1)S(1)} %constant_dynamic-update-slice_fusion.refs_0_) | copy-start | bytes 983044
  17.2 21.6 %collective-permute-start.6 = (bf16[1280,128]{1,0:T(8,128)(2,1)S(1)}, bf16[1280,128]{1,0:T(8,128)(2,1)}, u32[]{:S(2)}, u32[]{:S(2)}) collective-permute-start(bf16[1280,128]{1,0:T(8,128)(2,1)S(1)} %constant_dynamic-update-slice_fusion.refs_0_), channel_id=1, source_target_pairs={{0,8},{1,9},{2,10},{3,11},{4,12},{5,13},{6,14},{7,15},{8,16},{9,17... | collective-permute-start | bytes 983048 | tf_op jit(solution)/shard_map/ppermute | solution.py:149
  17.3 24.6 %collective-permute-start.3 = (bf16[1280,128]{1,0:T(8,128)(2,1)S(1)}, bf16[1280,128]{1,0:T(8,128)(2,1)}, u32[]{:S(2)}, u32[]{:S(2)}) collective-permute-start(bf16[1280,128]{1,0:T(8,128)(2,1)S(1)} %constant_dynamic-update-slice_fusion.refs_0_), channel_id=1, source_target_pairs={{0,56},{1,57},{2,58},{3,59},{4,60},{5,61},{6,62},{7,63},{8,0},{9,1... | collective-permute-start | bytes 983048 | tf_op jit(solution)/shard_map/ppermute | solution.py:149
  20.0 24.7 %collective-permute-start.11 = (bf16[1280,128]{1,0:T(8,128)(2,1)S(1)}, bf16[1280,128]{1,0:T(8,128)(2,1)S(1)}, u32[]{:S(2)}, u32[]{:S(2)}) collective-permute-start(bf16[1280,128]{1,0:T(8,128)(2,1)S(1)} %constant_dynamic-update-slice_fusion.refs_0_), channel_id=1, source_target_pairs={{0,1},{1,0},{2,3},{3,2},{4,5},{5,4},{6,7},{7,6},{8,9},{9,8},{10,11... | collective-permute-start | bytes 983048 | tf_op jit(solution)/shard_map/ppermute | solution.py:149
  22.7 4.6 %collective-permute-start.21 = (bf16[320,128]{1,0:T(8,128)(2,1)S(1)}, bf16[320,128]{1,0:T(8,128)(2,1)S(1)}, u32[]{:S(2)}, u32[]{:S(2)}) collective-permute-start(bf16[320,128]{1,0:T(8,128)(2,1)S(1)} %collective-permute-done.20), channel_id=1, source_target_pairs={{0,56},{1,57},{2,58},{3,59},{4,60},{5,61},{6,62},{7,63},{8,0},{9,1... | collective-permute-start | bytes 245768 | tf_op jit(solution)/shard_map/ppermute | solution.py:149
  24.3 5.8 %collective-permute-start.24 = (bf16[320,128]{1,0:T(8,128)(2,1)S(1)}, bf16[320,128]{1,0:T(8,128)(2,1)S(1)}, u32[]{:S(2)}, u32[]{:S(2)}) collective-permute-start(bf16[320,128]{1,0:T(8,128)(2,1)S(1)} %collective-permute-done.23), channel_id=1, source_target_pairs={{0,8},{1,9},{2,10},{3,11},{4,12},{5,13},{6,14},{7,15},{8,16},{9,17... | collective-permute-start | bytes 245768 | tf_op jit(solution)/shard_map/ppermute | solution.py:149
  27.3 7.4 %collective-permute-start.22 = (bf16[320,128]{1,0:T(8,128)(2,1)S(1)}, bf16[320,128]{1,0:T(8,128)(2,1)S(1)}, u32[]{:S(2)}, u32[]{:S(2)}) collective-permute-start(bf16[320,128]{1,0:T(8,128)(2,1)S(1)} %collective-permute-done.21), channel_id=1, source_target_pairs={{0,56},{1,57},{2,58},{3,59},{4,60},{5,61},{6,62},{7,63},{8,0},{9,1... | collective-permute-start | bytes 245768 | tf_op jit(solution)/shard_map/ppermute | solution.py:149
  30.1 4.5 %collective-permute-start.25 = (bf16[320,128]{1,0:T(8,128)(2,1)S(1)}, bf16[320,128]{1,0:T(8,128)(2,1)S(1)}, u32[]{:S(2)}, u32[]{:S(2)}) collective-permute-start(bf16[320,128]{1,0:T(8,128)(2,1)S(1)} %collective-permute-done.24), channel_id=1, source_target_pairs={{0,8},{1,9},{2,10},{3,11},{4,12},{5,13},{6,14},{7,15},{8,16},{9,17... | collective-permute-start | bytes 245768 | tf_op jit(solution)/shard_map/ppermute | solution.py:149
  34.6 4.1 %collective-permute-start.26 = (bf16[160,128]{1,0:T(8,128)(2,1)S(1)}, bf16[160,128]{1,0:T(8,128)(2,1)S(1)}, u32[]{:S(2)}, u32[]{:S(2)}) collective-permute-start(bf16[160,128]{1,0:T(8,128)(2,1)S(1)} %slice.84), channel_id=1, source_target_pairs={{0,8},{1,9},{2,10},{3,11},{4,12},{5,13},{6,14},{7,15},{8,16},{9,17... | collective-permute-start | bytes 122888 | tf_op jit(solution)/shard_map/ppermute | solution.py:149
  34.7 4.1 %collective-permute-start.27 = (bf16[160,128]{1,0:T(8,128)(2,1)S(1)}, bf16[160,128]{1,0:T(8,128)(2,1)S(1)}, u32[]{:S(2)}, u32[]{:S(2)}) collective-permute-start(bf16[160,128]{1,0:T(8,128)(2,1)S(1)} %slice.85), channel_id=1, source_target_pairs={{0,56},{1,57},{2,58},{3,59},{4,60},{5,61},{6,62},{7,63},{8,0},{9,1... | collective-permute-start | bytes 122888 | tf_op jit(solution)/shard_map/ppermute | solution.py:149
  38.9 5.8 %copy-start.18 = (s32[128,128]{1,0:T(8,128)S(1)}, s32[128,128]{1,0:T(8,128)}, u32[]{:S(2)}) copy-start(s32[128,128]{1,0:T(8,128)} %param.7) | copy-start | bytes 196612
  38.9 5.7 %copy-start.20 = (s32[128,128]{1,0:T(8,128)S(1)}, s32[128,128]{1,0:T(8,128)}, u32[]{:S(2)}) copy-start(s32[128,128]{1,0:T(8,128)} %param.8) | copy-start | bytes 196612
  38.9 13.7 %collective-permute-start.7 = (bf16[1280,128]{1,0:T(8,128)(2,1)}, bf16[1280,128]{1,0:T(8,128)(2,1)S(1)}, u32[]{:S(2)}, u32[]{:S(2)}) collective-permute-start(bf16[1280,128]{1,0:T(8,128)(2,1)} %collective-permute-done.6.refs_8_), channel_id=1, source_target_pairs={{0,8},{1,9},{2,10},{3,11},{4,12},{5,13},{6,14},{7,15},{8,16},{9,17... | collective-permute-start | bytes 983048 | tf_op jit(solution)/shard_map/ppermute | solution.py:149
  39.0 13.6 %copy-start.17 = (f32[128,128]{1,0:T(8,128)S(1)}, f32[128,128]{1,0:T(8,128)}, u32[]{:S(2)}) copy-start(f32[128,128]{1,0:T(8,128)} %param.9) | copy-start | bytes 196612
  39.0 16.4 %collective-permute-start.29 = (bf16[2560,128]{1,0:T(8,128)(2,1)S(1)}, bf16[2560,128]{1,0:T(8,128)(2,1)S(1)}, u32[]{:S(2)}, u32[]{:S(2)}) collective-permute-start(bf16[2560,128]{1,0:T(8,128)(2,1)S(1)} %constant_dynamic-update-slice_fusion.5.refs_18_), channel_id=1, source_target_pairs={{0,2},{1,3},{2,4},{3,5},{4,6},{5,7},{6,0},{7,1},{8,10},{9,11},{10,... | collective-permute-start | bytes 1966088 | tf_op jit(solution)/shard_map/ppermute | solution.py:149
  39.3 21.2 %collective-permute-start.28 = (bf16[2560,128]{1,0:T(8,128)(2,1)S(1)}, bf16[2560,128]{1,0:T(8,128)(2,1)S(1)}, u32[]{:S(2)}, u32[]{:S(2)}) collective-permute-start(bf16[2560,128]{1,0:T(8,128)(2,1)S(1)} %constant_dynamic-update-slice_fusion.5.refs_18_), channel_id=1, source_target_pairs={{0,6},{1,7},{2,0},{3,1},{4,2},{5,3},{6,4},{7,5},{8,14},{9,15},{10,... | collective-permute-start | bytes 1966088 | tf_op jit(solution)/shard_map/ppermute | solution.py:149
  42.0 10.7 %collective-permute-start.4 = (bf16[1280,128]{1,0:T(8,128)(2,1)}, bf16[1280,128]{1,0:T(8,128)(2,1)}, u32[]{:S(2)}, u32[]{:S(2)}) collective-permute-start(bf16[1280,128]{1,0:T(8,128)(2,1)} %collective-permute-done.3.refs_1_), channel_id=1, source_target_pairs={{0,56},{1,57},{2,58},{3,59},{4,60},{5,61},{6,62},{7,63},{8,0},{9,1... | collective-permute-start | bytes 983048 | tf_op jit(solution)/shard_map/ppermute | solution.py:149
  44.7 10.7 %copy-start.27 = (s32[128]{0:T(128)S(1)}, s32[128]{0:T(128)}, u32[]{:S(2)}) copy-start(s32[128]{0:T(128)} %param.10) | copy-start | bytes 1540
  44.8 0.7 copy-start.3
  45.5 24.9 %collective-permute-start.32 = (bf16[2560,128]{1,0:T(8,128)(2,1)S(1)}, bf16[2560,128]{1,0:T(8,128)(2,1)S(1)}, u32[]{:S(2)}, u32[]{:S(2)}) collective-permute-start(bf16[2560,128]{1,0:T(8,128)(2,1)S(1)} %constant_dynamic-update-slice_fusion.5.refs_18_), channel_id=1, source_target_pairs={{0,1},{1,0},{2,3},{3,2},{4,5},{5,4},{6,7},{7,6},{8,9},{9,8},{10,11... | collective-permute-start | bytes 1966088 | tf_op jit(solution)/shard_map/ppermute | solution.py:149
  52.6 9.6 %copy-start.5 = (bf16[1280,128]{1,0:T(8,128)(2,1)}, bf16[1280,128]{1,0:T(8,128)(2,1)S(1)}, u32[]{:S(2)}) copy-start(bf16[1280,128]{1,0:T(8,128)(2,1)S(1)} %collective-permute-done.7.refs_7_) | copy-start | bytes 983044
  52.6 9.6 %collective-permute-start.8 = (bf16[1280,128]{1,0:T(8,128)(2,1)S(1)}, bf16[1280,128]{1,0:T(8,128)(2,1)S(1)}, u32[]{:S(2)}, u32[]{:S(2)}) collective-permute-start(bf16[1280,128]{1,0:T(8,128)(2,1)S(1)} %collective-permute-done.7.refs_7_), channel_id=1, source_target_pairs={{0,8},{1,9},{2,10},{3,11},{4,12},{5,13},{6,14},{7,15},{8,16},{9,17... | collective-permute-start | bytes 983048 | tf_op jit(solution)/shard_map/ppermute | solution.py:149
  52.7 13.7 %collective-permute-start.5 = (bf16[1280,128]{1,0:T(8,128)(2,1)}, bf16[1280,128]{1,0:T(8,128)(2,1)S(1)}, u32[]{:S(2)}, u32[]{:S(2)}) collective-permute-start(bf16[1280,128]{1,0:T(8,128)(2,1)} %collective-permute-done.4.refs_2_), channel_id=1, source_target_pairs={{0,56},{1,57},{2,58},{3,59},{4,60},{5,61},{6,62},{7,63},{8,0},{9,1... | collective-permute-start | bytes 983048 | tf_op jit(solution)/shard_map/ppermute | solution.py:149
  55.4 12.2 %collective-permute-start.12 = (bf16[1280,128]{1,0:T(8,128)(2,1)}, bf16[1280,128]{1,0:T(8,128)(2,1)}, u32[]{:S(2)}, u32[]{:S(2)}) collective-permute-start(bf16[1280,128]{1,0:T(8,128)(2,1)} %collective-permute-done.3.refs_1_), channel_id=1, source_target_pairs={{0,1},{1,0},{2,3},{3,2},{4,5},{5,4},{6,7},{7,6},{8,9},{9,8},{10,11... | collective-permute-start | bytes 983048 | tf_op jit(solution)/shard_map/ppermute | solution.py:149
  60.4 7.3 %collective-permute-start.19 = (bf16[1280,128]{1,0:T(8,128)(2,1)}, bf16[1280,128]{1,0:T(8,128)(2,1)}, u32[]{:S(2)}, u32[]{:S(2)}) collective-permute-start(bf16[1280,128]{1,0:T(8,128)(2,1)} %collective-permute-done.6.refs_8_), channel_id=1, source_target_pairs={{0,1},{1,0},{2,3},{3,2},{4,5},{5,4},{6,7},{7,6},{8,9},{9,8},{10,11... | collective-permute-start | bytes 983048 | tf_op jit(solution)/shard_map/ppermute | solution.py:149
  62.2 8.2 %collective-permute-start.13 = (bf16[1280,128]{1,0:T(8,128)(2,1)}, bf16[1280,128]{1,0:T(8,128)(2,1)}, u32[]{:S(2)}, u32[]{:S(2)}) collective-permute-start(bf16[1280,128]{1,0:T(8,128)(2,1)} %collective-permute-done.4.refs_2_), channel_id=1, source_target_pairs={{0,1},{1,0},{2,3},{3,2},{4,5},{5,4},{6,7},{7,6},{8,9},{9,8},{10,11... | collective-permute-start | bytes 983048 | tf_op jit(solution)/shard_map/ppermute | solution.py:149
  66.3 6.8 %collective-permute-start.18 = (bf16[1280,128]{1,0:T(8,128)(2,1)}, bf16[1280,128]{1,0:T(8,128)(2,1)}, u32[]{:S(2)}, u32[]{:S(2)}) collective-permute-start(bf16[1280,128]{1,0:T(8,128)(2,1)} %copy-done.5), channel_id=1, source_target_pairs={{0,1},{1,0},{2,3},{3,2},{4,5},{5,4},{6,7},{7,6},{8,9},{9,8},{10,11... | collective-permute-start | bytes 983048 | tf_op jit(solution)/shard_map/ppermute | solution.py:149
  67.6 5.5 %copy-start.24 = (s32[128]{0:T(128)S(1)}, s32[128]{0:T(128)}, u32[]{:S(2)}) copy-start(s32[128]{0:T(128)} %get-tuple-element.17) | copy-start | bytes 1540
  67.6 11.0 %collective-permute-start.30 = (bf16[1280,128]{1,0:T(8,128)(2,1)S(1)}, bf16[1280,128]{1,0:T(8,128)(2,1)}, u32[]{:S(2)}, u32[]{:S(2)}) collective-permute-start(bf16[1280,128]{1,0:T(8,128)(2,1)S(1)} %slice.86), channel_id=1, source_target_pairs={{0,2},{1,3},{2,4},{3,5},{4,6},{5,7},{6,0},{7,1},{8,10},{9,11},{10,... | collective-permute-start | bytes 983048 | tf_op jit(solution)/shard_map/ppermute | solution.py:149
  67.7 11.4 %collective-permute-start.31 = (bf16[1280,128]{1,0:T(8,128)(2,1)S(1)}, bf16[1280,128]{1,0:T(8,128)(2,1)}, u32[]{:S(2)}, u32[]{:S(2)}) collective-permute-start(bf16[1280,128]{1,0:T(8,128)(2,1)S(1)} %slice.87), channel_id=1, source_target_pairs={{0,6},{1,7},{2,0},{3,1},{4,2},{5,3},{6,4},{7,5},{8,14},{9,15},{10,... | collective-permute-start | bytes 983048 | tf_op jit(solution)/shard_map/ppermute | solution.py:149
  70.4 6.0 %collective-permute-start.9 = (bf16[640,128]{1,0:T(8,128)(2,1)S(1)}, bf16[640,128]{1,0:T(8,128)(2,1)S(1)}, u32[]{:S(2)}, u32[]{:S(2)}) collective-permute-start(bf16[640,128]{1,0:T(8,128)(2,1)S(1)} %slice.82), channel_id=1, source_target_pairs={{0,8},{1,9},{2,10},{3,11},{4,12},{5,13},{6,14},{7,15},{8,16},{9,17... | collective-permute-start | bytes 491528 | tf_op jit(solution)/shard_map/ppermute | solution.py:149
  70.5 7.7 %collective-permute-start.10 = (bf16[640,128]{1,0:T(8,128)(2,1)S(1)}, bf16[640,128]{1,0:T(8,128)(2,1)S(1)}, u32[]{:S(2)}, u32[]{:S(2)}) collective-permute-start(bf16[640,128]{1,0:T(8,128)(2,1)S(1)} %slice.83), channel_id=1, source_target_pairs={{0,56},{1,57},{2,58},{3,59},{4,60},{5,61},{6,62},{7,63},{8,0},{9,1... | collective-permute-start | bytes 491528 | tf_op jit(solution)/shard_map/ppermute | solution.py:149
  73.1 7.1 %copy-start.22 = (pred[128]{0:T(512)(128)(4,1)}, pred[128]{0:T(512)(128)(4,1)S(1)}, u32[]{:S(2)}) copy-start(pred[128]{0:T(512)(128)(4,1)S(1)} %get-tuple-element.19) | copy-start | bytes 388
  73.1 13.0 %collective-permute-start.33 = (bf16[2560,128]{1,0:T(8,128)(2,1)S(1)}, bf16[2560,128]{1,0:T(8,128)(2,1)}, u32[]{:S(2)}, u32[]{:S(2)}) collective-permute-start(bf16[2560,128]{1,0:T(8,128)(2,1)S(1)} %collective-permute-done.28.refs_19_), channel_id=1, source_target_pairs={{0,1},{1,0},{2,3},{3,2},{4,5},{5,4},{6,7},{7,6},{8,9},{9,8},{10,11... | collective-permute-start | bytes 1966088 | tf_op jit(solution)/shard_map/ppermute | solution.py:149
  76.4 7.3 %copy-start.9 = (bf16[640,128]{1,0:T(8,128)(2,1)}, bf16[640,128]{1,0:T(8,128)(2,1)S(1)}, u32[]{:S(2)}) copy-start(bf16[640,128]{1,0:T(8,128)(2,1)S(1)} %collective-permute-done.9.refs_4_) | copy-start | bytes 491524
  76.4 9.7 %collective-permute-start.36 = (bf16[2560,128]{1,0:T(8,128)(2,1)S(1)}, bf16[2560,128]{1,0:T(8,128)(2,1)}, u32[]{:S(2)}, u32[]{:S(2)}) collective-permute-start(bf16[2560,128]{1,0:T(8,128)(2,1)S(1)} %collective-permute-done.29.refs_22_), channel_id=1, source_target_pairs={{0,1},{1,0},{2,3},{3,2},{4,5},{5,4},{6,7},{7,6},{8,9},{9,8},{10,11... | collective-permute-start | bytes 1966088 | tf_op jit(solution)/shard_map/ppermute | solution.py:149
  78.2 4.3 %collective-permute-start.14 = (bf16[1280,128]{1,0:T(8,128)(2,1)S(1)}, bf16[1280,128]{1,0:T(8,128)(2,1)S(1)}, u32[]{:S(2)}, u32[]{:S(2)}) collective-permute-start(bf16[1280,128]{1,0:T(8,128)(2,1)S(1)} %collective-permute-done.5.refs_3_), channel_id=1, source_target_pairs={{0,1},{1,0},{2,3},{3,2},{4,5},{5,4},{6,7},{7,6},{8,9},{9,8},{10,11... | collective-permute-start | bytes 983048 | tf_op jit(solution)/shard_map/ppermute | solution.py:149
  78.7 2.0 %collective-permute-start.15 = (bf16[640,128]{1,0:T(8,128)(2,1)S(1)}, bf16[640,128]{1,0:T(8,128)(2,1)S(1)}, u32[]{:S(2)}, u32[]{:S(2)}) collective-permute-start(bf16[640,128]{1,0:T(8,128)(2,1)S(1)} %collective-permute-done.9.refs_4_), channel_id=1, source_target_pairs={{0,1},{1,0},{2,3},{3,2},{4,5},{5,4},{6,7},{7,6},{8,9},{9,8},{10,11... | collective-permute-start | bytes 491528 | tf_op jit(solution)/shard_map/ppermute | solution.py:149
  79.2 2.5 %collective-permute-start.16 = (bf16[640,128]{1,0:T(8,128)(2,1)S(1)}, bf16[640,128]{1,0:T(8,128)(2,1)S(1)}, u32[]{:S(2)}, u32[]{:S(2)}) collective-permute-start(bf16[640,128]{1,0:T(8,128)(2,1)S(1)} %collective-permute-done.10.refs_5_), channel_id=1, source_target_pairs={{0,1},{1,0},{2,3},{3,2},{4,5},{5,4},{6,7},{7,6},{8,9},{9,8},{10,11... | collective-permute-start | bytes 491528 | tf_op jit(solution)/shard_map/ppermute | solution.py:149
  79.5 0.7 copy-start.11
  80.7 0.7 copy-start.13
  81.3 4.7 %collective-permute-start.17 = (bf16[1280,128]{1,0:T(8,128)(2,1)S(1)}, bf16[1280,128]{1,0:T(8,128)(2,1)}, u32[]{:S(2)}, u32[]{:S(2)}) collective-permute-start(bf16[1280,128]{1,0:T(8,128)(2,1)S(1)} %collective-permute-done.8.refs_6_), channel_id=1, source_target_pairs={{0,1},{1,0},{2,3},{3,2},{4,5},{5,4},{6,7},{7,6},{8,9},{9,8},{10,11... | collective-permute-start | bytes 983048 | tf_op jit(solution)/shard_map/ppermute | solution.py:149
  81.7 0.7 copy-start.15
  82.3 3.7 %collective-permute-start.34 = (bf16[1280,128]{1,0:T(8,128)(2,1)}, bf16[1280,128]{1,0:T(8,128)(2,1)}, u32[]{:S(2)}, u32[]{:S(2)}) collective-permute-start(bf16[1280,128]{1,0:T(8,128)(2,1)} %collective-permute-done.30.refs_20_), channel_id=1, source_target_pairs={{0,1},{1,0},{2,3},{3,2},{4,5},{5,4},{6,7},{7,6},{8,9},{9,8},{10,11... | collective-permute-start | bytes 983048 | tf_op jit(solution)/shard_map/ppermute | solution.py:149
  82.5 0.7 copy-start.7
  83.2 2.8 %collective-permute-start.35 = (bf16[1280,128]{1,0:T(8,128)(2,1)}, bf16[1280,128]{1,0:T(8,128)(2,1)}, u32[]{:S(2)}, u32[]{:S(2)}) collective-permute-start(bf16[1280,128]{1,0:T(8,128)(2,1)} %collective-permute-done.31.refs_21_), channel_id=1, source_target_pairs={{0,1},{1,0},{2,3},{3,2},{4,5},{5,4},{6,7},{7,6},{8,9},{9,8},{10,11... | collective-permute-start | bytes 983048 | tf_op jit(solution)/shard_map/ppermute | solution.py:149
  86.1 1.0 copy-start.2
  87.1 1.0 copy-start.4
  88.0 1.0 copy-start.6
  89.0 1.0 copy-start.8
  90.0 0.9 copy-start.10
  90.9 0.9 copy-start.12
  91.8 0.9 copy-start.14
  92.7 0.9 copy-start.16
  124.5 0.8 copy-start.19
  124.6 0.8 copy-start.26
  151.9 0.6 copy-start.23
  (1 other events, 0.6 us)

commit v3 on v2

--- a/solution.py
+++ b/solution.py
@@ -107,11 +107,16 @@
 
 
 def slot_of(dev, color):
-    me = lax.axis_index("dev")
+    me, grp = lax.axis_index("dev"), lax.axis_index("grp")
     dz = ((dev >> 3) - (me >> 3)) & 7
     dx = ((dev >> 1) - (me >> 1)) & 3
-    other = (dev ^ me) & 1
-    return (color * 2 + other) * 32 + jnp.where(color == 1, dx * 8 + dz, dz * 4 + dx)
+    ahead = (dz >= 1) & (dz <= 4)
+    pair = jnp.where(ahead, dz - 1, (8 - dz) & 7)
+    which = ahead.astype(jnp.int32)
+    first = dx * 8 + ((pair - grp) & 3) * 2 + which
+    second = ((3 - pair - grp) & 3) * 8 + dx * 2 + which
+    far_side = (color ^ me) & 1
+    return (far_side * 32 + jnp.where(color == 0, first, second)) * 2 + ((dev ^ color) & 1)
 
 
 def tile_sums(pieces, nz_user, nz_sub, nz_value):
@@ -137,39 +142,51 @@
             pltpu.SMEM((2 * CH,), jnp.int32),
             pltpu.SemaphoreType.DMA((2,)),
         ],
-        compiler_params=pltpu.CompilerParams(vmem_limit_bytes=44 * 2**20),
+        compiler_params=pltpu.CompilerParams(vmem_limit_bytes=32 * 2**20),
         name="tile_sums",
     )(idx, w0, w1, *pieces)
     return out[:, :64] + out[:, 64:]
 
 
-def sent(value, dz, dx, dc=0):
-    devs = lax.axis_size("dev")
-    pairs = [(d, ((d // 8 + dz) % 8) * 8 + ((d % 8 // 2 + dx) % 4) * 2 + ((d % 2) ^ dc)) for d in range(devs)]
-    return lax.ppermute(value, "dev", pairs)
-
-
-def along_z(block):
+def fetched(value, source):
+    grps, devs = lax.axis_size("grp"), lax.axis_size("dev")
+    pairs = []
+    for g in range(grps):
+        for d in range(devs):
+            sg, sz, sx, sc = source(g, d // 8, d % 8 // 2, d % 2)
+            pairs.append(((sg % 4) * devs + (sz % 8) * 8 + (sx % 4) * 2 + sc, g * devs + d))
+    return lax.ppermute(value, ("grp", "dev"), pairs)
+
+
+def swapped(value):
+    return fetched(value, lambda g, z, x, c: (g, z, x, 1 - c))
+
+
+def pair_of(g, c):
+    return 3 - g if c else g
+
+
+def near(step):
+    return lambda g, z, x, c: (g, z, x + step, c) if c else (g + step, z, x, c)
+
+
+def wide(step):
+    return lambda g, z, x, c: (g + step, z, x, c) if c else (g, z, x + step, c)
+
+
+def gathered(halves):
+    core = lax.axis_index("dev") & 1
+    keep = jnp.where(core == 0, halves[0], halves[1])
+    give = jnp.where(core == 0, halves[1], halves[0])
+    unit = jnp.concatenate([keep, swapped(give)], axis=0)
+    back = fetched(unit, lambda g, z, x, c: (g, z - pair_of(g, c), x, c))
+    ahead = fetched(unit, lambda g, z, x, c: (g, z + pair_of(g, c) + 1, x, c))
+    pair = jnp.concatenate([back, ahead], axis=0)
+    block = jnp.concatenate([pair] + [fetched(pair, near(k)) for k in (1, 2, 3)], axis=0)
     half = block.shape[0] // 2
-    up, down = [], []
-    p = m = block
-    for _ in range(3):
-        p, m = sent(p, 1, 0), sent(m, -1, 0)
-        up.append(p)
-        down.append(m)
-    return [block] + down + [sent(p[:half], 1, 0), sent(m[half:], -1, 0)] + up[::-1]
-
-
-def gathered(mine_a, mine_b):
-    block_a = jnp.concatenate([mine_a, sent(mine_a, 0, -1), sent(mine_a, 0, 2), sent(mine_a, 0, 1)], axis=0)
-    pieces_a = along_z(block_a)
-    block_b = jnp.concatenate(along_z(mine_b), axis=0)
-    half = block_b.shape[0] // 2
-    p, m = sent(block_b, 0, 1), sent(block_b, 0, -1)
-    pieces_b = [block_b, m, sent(p[:half], 0, 1), sent(m[half:], 0, -1), p]
-    other_a = [sent(v, 0, 0, 1) for v in pieces_a]
-    other_b = [sent(v, 0, 0, 1) for v in pieces_b]
-    return pieces_a + other_a + pieces_b + other_b
+    right, left = fetched(block, wide(1)), fetched(block, wide(-1))
+    pieces = [block, right, fetched(right[:half], wide(1)), fetched(left[half:], wide(-1)), left]
+    return pieces + [swapped(p) for p in pieces]
 
 
 def packed(factor):
@@ -182,7 +199,7 @@
     users, subs = packed(user_factor), packed(sub_factor)
     mine_a = jnp.concatenate([users[:SHARD_U], subs[:SHARD_S]], axis=0)
     mine_b = jnp.concatenate([users[SHARD_U:], subs[SHARD_S:]], axis=0)
-    tile_rows = tile_sums(gathered(mine_a, mine_b), nz_user, nz_sub, nz_value)
+    tile_rows = tile_sums(gathered((mine_a, mine_b)), nz_user, nz_sub, nz_value)
     tile_count, rank_width = tile_rows.shape
     grp_size = lax.axis_size("grp")
     dev_size = lax.axis_size("dev")

time: 154 us -> 136 us (0.88)
  starting transfers between devices: 55.8 us -> 38.4 us
  waiting for transfers between devices: 17 us -> 27.9 us
  local copies, waits for them, and re-layouts: 18.2 us -> 9.84 us
  blocking collectives: 24.9 us -> 23.3 us
    ppermute x37 -> x15, starting transfers between devices: 55.8 us -> 38.4 us  [fetched(): return lax.ppermute(value, ('grp', 'dev'), pairs)]
    ppermute x37 -> x15, waiting for transfers between devices: 17 us -> 27.9 us  [fetched(): return lax.ppermute(value, ('grp', 'dev'), pairs)]
    unnamed x68 -> x18, local copies, waits for them, and re-layouts: 14.4 us -> 4.21 us
    slice x6 -> x2, local copies, waits for them, and re-layouts: 0.08 us -> 1.77 us  [the longest x1 0.89 us: gathered(): right[:half]]
    all_to_all x1, blocking collectives: 24.9 us -> 23.3 us  [exchange_both(): lax.all_to_all(pieces, axis, split_axis=0, concat_axis=0, tiled=True)]
  transfers between devices with their start and end apart: 37 -> 15, of which waited for: 7 -> 7; matrix products, arithmetic and copies ran while one was open for 5% -> 6% of each run, Pallas kernels for 0% -> 0%
where the time goes in v3:
time: 136 us; the launch traced here: 135 us
  starting transfers between devices  38.4 us (28%)
  Pallas kernels  31.1 us (23%)
  waiting for transfers between devices  27.9 us (21%)
  blocking collectives  23.3 us (17%)
  local copies, waits for them, and re-layouts  9.84 us (7%)
  other arithmetic  2.51 us (2%)
  matrix products  2.15 us (2%)
    ppermute x15, starting transfers between devices, fetched(): return lax.ppermute(value, ('grp', 'dev'), pairs)  38.4 us
    pallas_call x1, Pallas kernels, tile_sums(): pl.pallas_call(functools.partial(tile_kernel, counts, tiles), out_shape=j...  31.1 us
    ppermute x15, waiting for transfers between devices, fetched(): return lax.ppermute(value, ('grp', 'dev'), pairs)  27.9 us
    all_to_all x1, blocking collectives, exchange_both(): lax.all_to_all(pieces, axis, split_axis=0, concat_axis=0, tiled=True)  23.3 us
    unnamed x18, local copies, waits for them, and re-layouts  4.21 us
  transfers between devices with their start and end apart: 15, of which 7 were waited for; matrix products, arithmetic and copies ran while one was open for 6% of the time, Pallas kernels for 0%

profile of v3, /device:TPU:1, one launch (start us, length us, event | category | flops | bytes accessed | tf_op | source)
XLA Modules:
  0.0 135.4 jit_solution(15581915879071305937)
XLA Ops:
  0.0 0.0 copy-start
  0.0 1.1 copy.20
  1.1 0.9 copy.21
  2.0 0.1 fusion.28
  2.1 0.1 fusion.54
  2.2 0.1 broadcast_select_fusion.1
  2.4 3.3 %collective-permute-start = (bf16[320,128]{1,0:T(8,128)(2,1)S(1)}, bf16[320,128]{1,0:T(8,128)(2,1)S(1)}, u32[]{:S(2)}, u32[]{:S(2)}) collective-permute-start(bf16[320,128]{1,0:T(8,128)(2,1)S(1)} %broadcast_select_fusion), channel_id=1, source_target_pairs={{1,0},{0,1},{3,2},{2,3},{5,4},{4,5},{7,6},{6,7},{9,8},{8,9},{11,10... | collective-permute-start | bytes 245768 | tf_op jit(solution)/shard_map/ppermute | solution.py:158
  5.7 0.9 collective-permute-done
  6.6 4.5 %collective-permute-start.1 = (bf16[640,128]{1,0:T(8,128)(2,1)S(1)}, bf16[640,128]{1,0:T(8,128)(2,1)S(1)}, u32[]{:S(2)}, u32[]{:S(2)}) collective-permute-start(bf16[640,128]{1,0:T(8,128)(2,1)S(1)} %pad_maximum_fusion), channel_id=1, source_target_pairs={{0,0},{41,1},{2,2},{43,3},{4,4},{45,5},{6,6},{47,7},{8,8},{49,9},{... | collective-permute-start | bytes 491528 | tf_op jit(solution)/shard_map/ppermute | solution.py:158
  11.1 4.3 %collective-permute-start.2 = (bf16[640,128]{1,0:T(8,128)(2,1)S(1)}, bf16[640,128]{1,0:T(8,128)(2,1)S(1)}, u32[]{:S(2)}, u32[]{:S(2)}) collective-permute-start(bf16[640,128]{1,0:T(8,128)(2,1)S(1)} %pad_maximum_fusion), channel_id=1, source_target_pairs={{8,0},{33,1},{10,2},{35,3},{12,4},{37,5},{14,6},{39,7},{16,8},{41,... | collective-permute-start | bytes 491528 | tf_op jit(solution)/shard_map/ppermute | solution.py:158
  15.4 0.7 collective-permute-done.1
  16.2 0.7 constant_dynamic-update-slice_fusion.1
  16.8 5.8 %collective-permute-done.2 = bf16[640,128]{1,0:T(8,128)(2,1)S(1)} collective-permute-done((bf16[640,128]{1,0:T(8,128)(2,1)S(1)}, bf16[640,128]{1,0:T(8,128)(2,1)S(1)}, u32[]{:S(2)}, u32[]{:S(2)}) %collective-permute-start.2) | collective-permute-done | bytes 163872 | tf_op jit(solution)/shard_map/ppermute | solution.py:158
  22.7 0.7 constant_dynamic-update-slice_fusion
  23.4 2.5 %collective-permute-start.3 = (bf16[1280,128]{1,0:T(8,128)(2,1)S(1)}, bf16[1280,128]{1,0:T(8,128)(2,1)S(1)}, u32[]{:S(2)}, u32[]{:S(2)}) collective-permute-start(bf16[1280,128]{1,0:T(8,128)(2,1)S(1)} %get-tuple-element.16), channel_id=1, source_target_pairs={{64,0},{3,1},{66,2},{5,3},{68,4},{7,5},{70,6},{1,7},{72,8},{11,9},... | collective-permute-start | bytes 983048 | tf_op jit(solution)/shard_map/ppermute | solution.py:158
  25.8 0.5 collective-permute-start.4
  26.4 0.6 collective-permute-start.5
  27.0 6.4 %collective-permute-done.3 = bf16[1280,128]{1,0:T(8,128)(2,1)S(1)} collective-permute-done((bf16[1280,128]{1,0:T(8,128)(2,1)S(1)}, bf16[1280,128]{1,0:T(8,128)(2,1)S(1)}, u32[]{:S(2)}, u32[]{:S(2)}) %collective-permute-start.3) | collective-permute-done | bytes 327712 | tf_op jit(solution)/shard_map/ppermute | solution.py:158
  33.4 0.7 constant_dynamic-update-slice_fusion.4
  34.1 0.0 collective-permute-done.4
  34.1 0.8 constant_dynamic-update-slice_fusion.3
  34.9 2.2 %collective-permute-done.5 = bf16[1280,128]{1,0:T(8,128)(2,1)S(1)} collective-permute-done((bf16[1280,128]{1,0:T(8,128)(2,1)S(1)}, bf16[1280,128]{1,0:T(8,128)(2,1)S(1)}, u32[]{:S(2)}, u32[]{:S(2)}) %collective-permute-start.5) | collective-permute-done | bytes 327712 | tf_op jit(solution)/shard_map/ppermute | solution.py:158
  37.1 0.8 constant_dynamic-update-slice_fusion.2.refs_0_
  37.9 0.0 collective-permute-start.6
  37.9 1.5 %collective-permute-start.8 = (bf16[5120,128]{1,0:T(8,128)(2,1)}, bf16[5120,128]{1,0:T(8,128)(2,1)S(1)}, u32[]{:S(2)}, u32[]{:S(2)}) collective-permute-start(bf16[5120,128]{1,0:T(8,128)(2,1)} %constant_dynamic-update-slice_fusion.2.refs_0_), channel_id=1, source_target_pairs={{6,0},{193,1},{0,2},{195,3},{2,4},{197,5},{4,6},{199,7},{14,8},{20... | collective-permute-start | bytes 3932168 | tf_op jit(solution)/shard_map/ppermute | solution.py:158
  39.3 0.0 copy-done.2
  39.3 0.0 copy-done.4
  39.3 0.2 fusion.19
  39.5 0.1 add_bitcast_fusion
  39.7 0.0 copy-done.5
  39.7 4.3 %collective-permute-start.10 = (bf16[5120,128]{1,0:T(8,128)(2,1)}, bf16[5120,128]{1,0:T(8,128)(2,1)}, u32[]{:S(2)}, u32[]{:S(2)}) collective-permute-start(bf16[5120,128]{1,0:T(8,128)(2,1)} %constant_dynamic-update-slice_fusion.2.refs_0_), channel_id=1, source_target_pairs={{1,0},{0,1},{3,2},{2,3},{5,4},{4,5},{7,6},{6,7},{9,8},{8,9},{11,10... | collective-permute-start | bytes 3932168 | tf_op jit(solution)/shard_map/ppermute | solution.py:158
  44.0 10.8 %collective-permute-done.6.refs_1_ = bf16[5120,128]{1,0:T(8,128)(2,1)S(1)} collective-permute-done((bf16[5120,128]{1,0:T(8,128)(2,1)}, bf16[5120,128]{1,0:T(8,128)(2,1)S(1)}, u32[]{:S(2)}, u32[]{:S(2)}) %collective-permute-start.6) | collective-permute-done | bytes 1310752 | tf_op jit(solution)/shard_map/ppermute | solution.py:158
  54.8 0.9 slice.66
  55.7 1.2 collective-permute-start.7
  56.9 0.0 collective-permute-done.8.refs_4_
  56.9 0.9 slice.67
  57.8 0.3 collective-permute-start.9
  58.1 6.3 %collective-permute-start.11 = (bf16[5120,128]{1,0:T(8,128)(2,1)S(1)}, bf16[5120,128]{1,0:T(8,128)(2,1)}, u32[]{:S(2)}, u32[]{:S(2)}) collective-permute-start(bf16[5120,128]{1,0:T(8,128)(2,1)S(1)} %collective-permute-done.6.refs_1_), channel_id=1, source_target_pairs={{1,0},{0,1},{3,2},{2,3},{5,4},{4,5},{7,6},{6,7},{9,8},{8,9},{11,10... | collective-permute-start | bytes 3932168 | tf_op jit(solution)/shard_map/ppermute | solution.py:158
  64.4 0.0 collective-permute-start.14
  64.4 1.1 gather_fusion
  65.5 0.7 convert_bitcast_fusion
  66.2 0.7 copy.22
  66.9 0.1 pad.2.clone
  67.0 0.3 fusion
  67.4 0.0 collective-permute-done.7.refs_2_
  67.4 4.5 %collective-permute-start.12 = (bf16[2560,128]{1,0:T(8,128)(2,1)S(1)}, bf16[2560,128]{1,0:T(8,128)(2,1)S(1)}, u32[]{:S(2)}, u32[]{:S(2)}) collective-permute-start(bf16[2560,128]{1,0:T(8,128)(2,1)S(1)} %collective-permute-done.7.refs_2_), channel_id=1, source_target_pairs={{1,0},{0,1},{3,2},{2,3},{5,4},{4,5},{7,6},{6,7},{9,8},{8,9},{11,10... | collective-permute-start | bytes 1966088 | tf_op jit(solution)/shard_map/ppermute | solution.py:158
  71.9 0.0 collective-permute-done.9.refs_3_
  71.9 4.6 %collective-permute-start.13 = (bf16[2560,128]{1,0:T(8,128)(2,1)}, bf16[2560,128]{1,0:T(8,128)(2,1)S(1)}, u32[]{:S(2)}, u32[]{:S(2)}) collective-permute-start(bf16[2560,128]{1,0:T(8,128)(2,1)} %collective-permute-done.9.refs_3_), channel_id=1, source_target_pairs={{1,0},{0,1},{3,2},{2,3},{5,4},{4,5},{7,6},{6,7},{9,8},{8,9},{11,10... | collective-permute-start | bytes 1966088 | tf_op jit(solution)/shard_map/ppermute | solution.py:158
  76.5 0.9 broadcast_select_fusion.2
  77.4 0.0 collective-permute-done.10.refs_5_
  77.4 0.0 collective-permute-done.12.refs_7_
  77.4 1.0 collective-permute-done.13.refs_8_
  78.4 0.0 collective-permute-done.11.refs_6_
  78.4 0.0 collective-permute-done.14.refs_9_
  78.4 31.1 %tile_sums.1 = f32[128,128]{1,0:T(8,128)S(1)} custom-call(s32[32768]{0:T(1024)S(1)} %bitcast.23, f32[128,128]{1,0:T(8,128)S(1)} %broadcast_select_fusion.3.w0_ref, f32[128,128]{1,0:T(8,128)S(1)} %get-tuple-element.7.w1_ref, bf16[5120,128]{1,0:T(8,128)(2,1)} %constant_dynamic-update-slice_fusion.2.refs_0_, ...), custom_call_target="tpu_custom_call" | custom-call | tf_op jit(solution)/shard_map/tile_sums/pallas_call | solution.py:133
  109.5 0.1 slice_add_fusion
  109.6 0.5 fusion.5
  110.1 0.1 reshape_reshape.6
  110.2 0.3 copy.23
  110.5 23.3 %all_to_all.5 = f32[256,1,1,256]{3,1,2,0:T(1,128)S(1)} all-to-all(f32[256,1,1,256]{3,1,2,0:T(1,128)S(1)} %bitcast.25), channel_id=1, replica_groups=mesh['grp'=4,'dev'=64] {'dev','grp'}, dimensions={0} | all-to-all | bytes 524288 | tf_op jit(solution)/shard_map/all_to_all | solution.py:31
  133.8 0.1 copy.28
  133.8 0.2 fusion.2
  134.1 0.5 fusion.3
  134.5 0.9 convolution_add_fusion
  (20 shorter events, 0.1 us)
Async XLA Ops:
  0.0 64.4 %copy-start = (s32[16384]{0:T(1024)S(1)}, s32[16384]{0:T(1024)}, u32[]{:S(2)}) copy-start(s32[16384]{0:T(1024)} %param.11) | copy-start | bytes 196612
  2.4 4.2 %collective-permute-start = (bf16[320,128]{1,0:T(8,128)(2,1)S(1)}, bf16[320,128]{1,0:T(8,128)(2,1)S(1)}, u32[]{:S(2)}, u32[]{:S(2)}) collective-permute-start(bf16[320,128]{1,0:T(8,128)(2,1)S(1)} %broadcast_select_fusion), channel_id=1, source_target_pairs={{1,0},{0,1},{3,2},{2,3},{5,4},{4,5},{7,6},{6,7},{9,8},{8,9},{11,10... | collective-permute-start | bytes 245768 | tf_op jit(solution)/shard_map/ppermute | solution.py:158
  6.6 9.6 %collective-permute-start.1 = (bf16[640,128]{1,0:T(8,128)(2,1)S(1)}, bf16[640,128]{1,0:T(8,128)(2,1)S(1)}, u32[]{:S(2)}, u32[]{:S(2)}) collective-permute-start(bf16[640,128]{1,0:T(8,128)(2,1)S(1)} %pad_maximum_fusion), channel_id=1, source_target_pairs={{0,0},{41,1},{2,2},{43,3},{4,4},{45,5},{6,6},{47,7},{8,8},{49,9},{... | collective-permute-start | bytes 491528 | tf_op jit(solution)/shard_map/ppermute | solution.py:158
  11.1 11.5 %collective-permute-start.2 = (bf16[640,128]{1,0:T(8,128)(2,1)S(1)}, bf16[640,128]{1,0:T(8,128)(2,1)S(1)}, u32[]{:S(2)}, u32[]{:S(2)}) collective-permute-start(bf16[640,128]{1,0:T(8,128)(2,1)S(1)} %pad_maximum_fusion), channel_id=1, source_target_pairs={{8,0},{33,1},{10,2},{35,3},{12,4},{37,5},{14,6},{39,7},{16,8},{41,... | collective-permute-start | bytes 491528 | tf_op jit(solution)/shard_map/ppermute | solution.py:158
  16.8 22.5 %copy-start.2 = (s32[128,128]{1,0:T(8,128)S(1)}, s32[128,128]{1,0:T(8,128)}, u32[]{:S(2)}) copy-start(s32[128,128]{1,0:T(8,128)} %param.7) | copy-start | bytes 196612
  16.8 22.5 %copy-start.4 = (s32[128,128]{1,0:T(8,128)S(1)}, s32[128,128]{1,0:T(8,128)}, u32[]{:S(2)}) copy-start(s32[128,128]{1,0:T(8,128)} %param.8) | copy-start | bytes 196612
  23.4 10.0 %collective-permute-start.3 = (bf16[1280,128]{1,0:T(8,128)(2,1)S(1)}, bf16[1280,128]{1,0:T(8,128)(2,1)S(1)}, u32[]{:S(2)}, u32[]{:S(2)}) collective-permute-start(bf16[1280,128]{1,0:T(8,128)(2,1)S(1)} %get-tuple-element.16), channel_id=1, source_target_pairs={{64,0},{3,1},{66,2},{5,3},{68,4},{7,5},{70,6},{1,7},{72,8},{11,9},... | collective-permute-start | bytes 983048 | tf_op jit(solution)/shard_map/ppermute | solution.py:158
  25.8 8.3 %collective-permute-start.4 = (bf16[1280,128]{1,0:T(8,128)(2,1)S(1)}, bf16[1280,128]{1,0:T(8,128)(2,1)S(1)}, u32[]{:S(2)}, u32[]{:S(2)}) collective-permute-start(bf16[1280,128]{1,0:T(8,128)(2,1)S(1)} %get-tuple-element.16), channel_id=1, source_target_pairs={{128,0},{5,1},{130,2},{7,3},{132,4},{1,5},{134,6},{3,7},{136,8},{1... | collective-permute-start | bytes 983048 | tf_op jit(solution)/shard_map/ppermute | solution.py:158
  26.4 10.7 %collective-permute-start.5 = (bf16[1280,128]{1,0:T(8,128)(2,1)S(1)}, bf16[1280,128]{1,0:T(8,128)(2,1)S(1)}, u32[]{:S(2)}, u32[]{:S(2)}) collective-permute-start(bf16[1280,128]{1,0:T(8,128)(2,1)S(1)} %get-tuple-element.16), channel_id=1, source_target_pairs={{192,0},{7,1},{194,2},{1,3},{196,4},{3,5},{198,6},{5,7},{200,8},{1... | collective-permute-start | bytes 983048 | tf_op jit(solution)/shard_map/ppermute | solution.py:158
  33.4 6.3 %copy-start.5 = (s32[128]{0:T(128)S(1)}, s32[128]{0:T(128)}, u32[]{:S(2)}) copy-start(s32[128]{0:T(128)} %param.10) | copy-start | bytes 1540
  37.9 17.0 %collective-permute-start.6 = (bf16[5120,128]{1,0:T(8,128)(2,1)}, bf16[5120,128]{1,0:T(8,128)(2,1)S(1)}, u32[]{:S(2)}, u32[]{:S(2)}) collective-permute-start(bf16[5120,128]{1,0:T(8,128)(2,1)} %constant_dynamic-update-slice_fusion.2.refs_0_), channel_id=1, source_target_pairs={{2,0},{65,1},{4,2},{67,3},{6,4},{69,5},{0,6},{71,7},{10,8},{73,9},... | collective-permute-start | bytes 3932168 | tf_op jit(solution)/shard_map/ppermute | solution.py:158
  37.9 19.1 %collective-permute-start.8 = (bf16[5120,128]{1,0:T(8,128)(2,1)}, bf16[5120,128]{1,0:T(8,128)(2,1)S(1)}, u32[]{:S(2)}, u32[]{:S(2)}) collective-permute-start(bf16[5120,128]{1,0:T(8,128)(2,1)} %constant_dynamic-update-slice_fusion.2.refs_0_), channel_id=1, source_target_pairs={{6,0},{193,1},{0,2},{195,3},{2,4},{197,5},{4,6},{199,7},{14,8},{20... | collective-permute-start | bytes 3932168 | tf_op jit(solution)/shard_map/ppermute | solution.py:158
  39.7 37.7 %collective-permute-start.10 = (bf16[5120,128]{1,0:T(8,128)(2,1)}, bf16[5120,128]{1,0:T(8,128)(2,1)}, u32[]{:S(2)}, u32[]{:S(2)}) collective-permute-start(bf16[5120,128]{1,0:T(8,128)(2,1)} %constant_dynamic-update-slice_fusion.2.refs_0_), channel_id=1, source_target_pairs={{1,0},{0,1},{3,2},{2,3},{5,4},{4,5},{7,6},{6,7},{9,8},{8,9},{11,10... | collective-permute-start | bytes 3932168 | tf_op jit(solution)/shard_map/ppermute | solution.py:158
  55.7 20.8 %copy-start.1 = (f32[128,128]{1,0:T(8,128)S(1)}, f32[128,128]{1,0:T(8,128)}, u32[]{:S(2)}) copy-start(f32[128,128]{1,0:T(8,128)} %param.9) | copy-start | bytes 196612
  55.7 11.7 %collective-permute-start.7 = (bf16[2560,128]{1,0:T(8,128)(2,1)}, bf16[2560,128]{1,0:T(8,128)(2,1)S(1)}, u32[]{:S(2)}, u32[]{:S(2)}) collective-permute-start(bf16[2560,128]{1,0:T(8,128)(2,1)} %slice.66), channel_id=1, source_target_pairs={{2,0},{65,1},{4,2},{67,3},{6,4},{69,5},{0,6},{71,7},{10,8},{73,9},... | collective-permute-start | bytes 1966088 | tf_op jit(solution)/shard_map/ppermute | solution.py:158
  57.8 14.1 %collective-permute-start.9 = (bf16[2560,128]{1,0:T(8,128)(2,1)}, bf16[2560,128]{1,0:T(8,128)(2,1)}, u32[]{:S(2)}, u32[]{:S(2)}) collective-permute-start(bf16[2560,128]{1,0:T(8,128)(2,1)} %slice.67), channel_id=1, source_target_pairs={{6,0},{193,1},{0,2},{195,3},{2,4},{197,5},{4,6},{199,7},{14,8},{20... | collective-permute-start | bytes 1966088 | tf_op jit(solution)/shard_map/ppermute | solution.py:158
  58.1 20.3 %collective-permute-start.11 = (bf16[5120,128]{1,0:T(8,128)(2,1)S(1)}, bf16[5120,128]{1,0:T(8,128)(2,1)}, u32[]{:S(2)}, u32[]{:S(2)}) collective-permute-start(bf16[5120,128]{1,0:T(8,128)(2,1)S(1)} %collective-permute-done.6.refs_1_), channel_id=1, source_target_pairs={{1,0},{0,1},{3,2},{2,3},{5,4},{4,5},{7,6},{6,7},{9,8},{8,9},{11,10... | collective-permute-start | bytes 3932168 | tf_op jit(solution)/shard_map/ppermute | solution.py:158
  64.4 14.1 %collective-permute-start.14 = (bf16[5120,128]{1,0:T(8,128)(2,1)S(1)}, bf16[5120,128]{1,0:T(8,128)(2,1)}, u32[]{:S(2)}, u32[]{:S(2)}) collective-permute-start(bf16[5120,128]{1,0:T(8,128)(2,1)S(1)} %collective-permute-done.8.refs_4_), channel_id=1, source_target_pairs={{1,0},{0,1},{3,2},{2,3},{5,4},{4,5},{7,6},{6,7},{9,8},{8,9},{11,10... | collective-permute-start | bytes 3932168 | tf_op jit(solution)/shard_map/ppermute | solution.py:158
  67.4 10.0 %collective-permute-start.12 = (bf16[2560,128]{1,0:T(8,128)(2,1)S(1)}, bf16[2560,128]{1,0:T(8,128)(2,1)S(1)}, u32[]{:S(2)}, u32[]{:S(2)}) collective-permute-start(bf16[2560,128]{1,0:T(8,128)(2,1)S(1)} %collective-permute-done.7.refs_2_), channel_id=1, source_target_pairs={{1,0},{0,1},{3,2},{2,3},{5,4},{4,5},{7,6},{6,7},{9,8},{8,9},{11,10... | collective-permute-start | bytes 1966088 | tf_op jit(solution)/shard_map/ppermute | solution.py:158
  71.9 6.5 %collective-permute-start.13 = (bf16[2560,128]{1,0:T(8,128)(2,1)}, bf16[2560,128]{1,0:T(8,128)(2,1)S(1)}, u32[]{:S(2)}, u32[]{:S(2)}) collective-permute-start(bf16[2560,128]{1,0:T(8,128)(2,1)} %collective-permute-done.9.refs_3_), channel_id=1, source_target_pairs={{1,0},{0,1},{3,2},{2,3},{5,4},{4,5},{7,6},{6,7},{9,8},{8,9},{11,10... | collective-permute-start | bytes 1966088 | tf_op jit(solution)/shard_map/ppermute | solution.py:158
  78.4 31.2 %copy-start.3 = (f32[128,1]{1,0:T(8,128)S(1)}, f32[128,1]{1,0:T(8,128)}, u32[]{:S(2)}) copy-start(f32[128,1]{1,0:T(8,128)} %copy.22) | copy-start | bytes 1540

commit v4 on v3

--- a/solution.py
+++ b/solution.py
@@ -50,7 +50,8 @@
 
 def tile_kernel(counts, tiles, idx_hbm, w0_ref, w1_ref, *refs):
     f32 = jnp.float32
-    pieces, (out_ref, utab, stab, bufa, bufb, isem) = refs[: len(counts)], refs[len(counts) :]
+    n = len(counts)
+    pieces, (out_ref, utab, stab, stage, bufa, bufb, sem, isem) = refs[:n], refs[n:]
     bufs = (bufa, bufb)
     steps = tiles // (2 * NT)
 
@@ -59,24 +60,30 @@
 
     icopy(0, 0).start()
     icopy(1, 1).start()
+    starts = [sum(counts[:k]) for k in range(n)]
+
+    def tcopy(k):
+        rows = pl.ds(starts[k] * SHARD, counts[k] * SHARD)
+        return pltpu.make_async_copy(pieces[k], stage.at[rows, :], sem.at[k])
+
+    for k in range(n):
+        tcopy(k).start()
     low = lax.broadcasted_iota(jnp.int32, (SHARD_S, 128), 1) < 64
-    first_slot = 0
-    for piece, count in zip(pieces, counts):
-
-        def conv(i, carry, piece=piece, first_slot=first_slot):
-            src = pl.multiple_of(i * SHARD, SHARD_S)
-            slot = first_slot + i
-            urow = pl.multiple_of(slot * SHARD_U, SHARD_U)
-            srow = pl.multiple_of(slot * 2 * SHARD_S, 2 * SHARD_S)
-            utab[pl.ds(urow, SHARD_U), :] = piece[pl.ds(src, SHARD_U), :].astype(f32)
-            x = piece[pl.ds(src + SHARD_U, SHARD_S), :].astype(f32)
-            r = pltpu.roll(x, 64, 1)
-            stab[pl.ds(srow, SHARD_S), :] = jnp.where(low, x, r)
-            stab[pl.ds(srow + SHARD_S, SHARD_S), :] = jnp.where(low, r, x)
-            return carry
-
-        lax.fori_loop(0, count, conv, 0)
-        first_slot += count
+
+    def conv(slot, carry):
+        src = pl.multiple_of(slot * SHARD, SHARD_S)
+        urow = pl.multiple_of(slot * SHARD_U, SHARD_U)
+        srow = pl.multiple_of(slot * 2 * SHARD_S, 2 * SHARD_S)
+        utab[pl.ds(urow, SHARD_U), :] = stage[pl.ds(src, SHARD_U), :].astype(f32)
+        x = stage[pl.ds(src + SHARD_U, SHARD_S), :].astype(f32)
+        r = pltpu.roll(x, 64, 1)
+        stab[pl.ds(srow, SHARD_S), :] = jnp.where(low, x, r)
+        stab[pl.ds(srow + SHARD_S, SHARD_S), :] = jnp.where(low, r, x)
+        return carry
+
+    for k in range(n):
+        tcopy(k).wait()
+        lax.fori_loop(starts[k], starts[k] + counts[k], conv, 0)
 
     def tile(buf, j, t):
         w0 = w0_ref[pl.ds(t, 1), :]
@@ -113,8 +120,8 @@
     ahead = (dz >= 1) & (dz <= 4)
     pair = jnp.where(ahead, dz - 1, (8 - dz) & 7)
     which = ahead.astype(jnp.int32)
-    first = dx * 8 + ((pair - grp) & 3) * 2 + which
-    second = ((3 - pair - grp) & 3) * 8 + dx * 2 + which
+    first = which * 16 + dx * 4 + ((pair - grp) & 3)
+    second = which * 16 + ((3 - pair - grp) & 3) * 4 + dx
     far_side = (color ^ me) & 1
     return (far_side * 32 + jnp.where(color == 0, first, second)) * 2 + ((dev ^ color) & 1)
 
@@ -133,16 +140,19 @@
     out = pl.pallas_call(
         functools.partial(tile_kernel, counts, tiles),
         out_shape=jax.ShapeDtypeStruct((tiles, 128), jnp.float32),
-        in_specs=[pl.BlockSpec(memory_space=pltpu.HBM), vmem, vmem] + [vmem] * len(pieces),
+        in_specs=[pl.BlockSpec(memory_space=pltpu.HBM), vmem, vmem]
+        + [pl.BlockSpec(memory_space=pltpu.HBM)] * len(pieces),
         out_specs=vmem,
         scratch_shapes=[
             pltpu.VMEM((slots * SHARD_U, 128), jnp.float32),
             pltpu.VMEM((slots * 2 * SHARD_S, 128), jnp.float32),
+            pltpu.VMEM((slots * SHARD, 128), jnp.bfloat16),
             pltpu.SMEM((2 * CH,), jnp.int32),
             pltpu.SMEM((2 * CH,), jnp.int32),
+            pltpu.SemaphoreType.DMA((len(pieces),)),
             pltpu.SemaphoreType.DMA((2,)),
         ],
-        compiler_params=pltpu.CompilerParams(vmem_limit_bytes=32 * 2**20),
+        compiler_params=pltpu.CompilerParams(vmem_limit_bytes=44 * 2**20),
         name="tile_sums",
     )(idx, w0, w1, *pieces)
     return out[:, :64] + out[:, 64:]
@@ -181,11 +191,11 @@
     unit = jnp.concatenate([keep, swapped(give)], axis=0)
     back = fetched(unit, lambda g, z, x, c: (g, z - pair_of(g, c), x, c))
     ahead = fetched(unit, lambda g, z, x, c: (g, z + pair_of(g, c) + 1, x, c))
-    pair = jnp.concatenate([back, ahead], axis=0)
-    block = jnp.concatenate([pair] + [fetched(pair, near(k)) for k in (1, 2, 3)], axis=0)
-    half = block.shape[0] // 2
-    right, left = fetched(block, wide(1)), fetched(block, wide(-1))
-    pieces = [block, right, fetched(right[:half], wide(1)), fetched(left[half:], wide(-1)), left]
+    a = jnp.concatenate([back] + [fetched(back, near(k)) for k in (1, 2, 3)], axis=0)
+    right_a, left_a = fetched(a, wide(1)), fetched(a, wide(-1))
+    b = jnp.concatenate([ahead] + [fetched(ahead, near(k)) for k in (1, 2, 3)], axis=0)
+    left_b, right_b = fetched(b, wide(-1)), fetched(b, wide(1))
+    pieces = [a, right_a, fetched(right_a, wide(1)), left_a, b, right_b, fetched(left_b, wide(-1)), left_b]
     return pieces + [swapped(p) for p in pieces]
 
 

time: 136 us -> 125 us (0.919)
  waiting for transfers between devices: 27.9 us -> 16.4 us
  local copies, waits for them, and re-layouts: 9.84 us -> 5.95 us
  starting transfers between devices: 38.4 us -> 42.1 us
  blocking collectives: 23.3 us -> 25.2 us
    ppermute x15 -> x23, waiting for transfers between devices: 27.9 us -> 16.4 us  [fetched(): return lax.ppermute(value, ('grp', 'dev'), pairs)]
    ppermute x15 -> x23, starting transfers between devices: 38.4 us -> 42.1 us  [fetched(): return lax.ppermute(value, ('grp', 'dev'), pairs)]
    all_to_all x1, blocking collectives: 23.3 us -> 25.2 us  [exchange_both(): lax.all_to_all(pieces, axis, split_axis=0, concat_axis=0, tiled=True)]
    slice x2 -> x0, local copies, waits for them, and re-layouts: 1.77 us -> none  [the longest x1 0.89 us: gathered(): right[:half]]
    concatenate x2, local copies, waits for them, and re-layouts: 1.46 us -> 0.05 us  [the longest x1 0.02 us: gathered(): jnp.concatenate([ahead] + [fetched(ahead, near(k)) for k in (1, 2, 3)], a...]
    unnamed x18 -> x25, local copies, waits for them, and re-layouts: 4.21 us -> 3.49 us
  transfers between devices with their start and end apart: 15 -> 23, of which waited for: 7 -> 7; matrix products, arithmetic and copies ran while one was open for 6% -> 3% of each run, Pallas kernels for 0% -> 0%
where the time goes in v4:
time: 125 us; the launch traced here: 124 us
  starting transfers between devices  42.1 us (34%)
  Pallas kernels  30.5 us (24%)
  blocking collectives  25.2 us (20%)
  waiting for transfers between devices  16.4 us (13%)
  local copies, waits for them, and re-layouts  5.95 us (5%)
  matrix products  2.15 us (2%)
  other arithmetic  1.66 us (1%)
    ppermute x23, starting transfers between devices, fetched(): return lax.ppermute(value, ('grp', 'dev'), pairs)  42.1 us
    pallas_call x1, Pallas kernels, tile_sums(): pl.pallas_call(functools.partial(tile_kernel, counts, tiles), out_shape=j...  30.5 us
    all_to_all x1, blocking collectives, exchange_both(): lax.all_to_all(pieces, axis, split_axis=0, concat_axis=0, tiled=True)  25.2 us
    ppermute x23, waiting for transfers between devices, fetched(): return lax.ppermute(value, ('grp', 'dev'), pairs)  16.4 us
    unnamed x25, local copies, waits for them, and re-layouts  3.49 us
  transfers between devices with their start and end apart: 23, of which 7 were waited for; matrix products, arithmetic and copies ran while one was open for 3% of the time, Pallas kernels for 0%

profile of v4, /device:TPU:1, one launch (start us, length us, event | category | flops | bytes accessed | tf_op | source)
XLA Modules:
  0.0 124.4 jit_solution(11454756640967999913)
XLA Ops:
  0.0 1.1 copy.20
  1.1 0.0 copy-start.6
  1.2 0.7 copy-done.6
  1.9 0.1 copy.21
  2.0 0.1 fusion.32
  2.1 0.1 fusion.56
  2.2 0.1 broadcast_select_fusion.1
  2.3 3.3 %collective-permute-start = (bf16[320,128]{1,0:T(8,128)(2,1)S(1)}, bf16[320,128]{1,0:T(8,128)(2,1)S(1)}, u32[]{:S(2)}, u32[]{:S(2)}) collective-permute-start(bf16[320,128]{1,0:T(8,128)(2,1)S(1)} %broadcast_select_fusion), channel_id=1, source_target_pairs={{1,0},{0,1},{3,2},{2,3},{5,4},{4,5},{7,6},{6,7},{9,8},{8,9},{11,10... | collective-permute-start | bytes 245768 | tf_op jit(solution)/shard_map/ppermute | solution.py:168
  5.6 0.9 collective-permute-done
  6.6 5.3 %collective-permute-start.8 = (bf16[640,128]{1,0:T(8,128)(2,1)S(1)}, bf16[640,128]{1,0:T(8,128)(2,1)S(1)}, u32[]{:S(2)}, u32[]{:S(2)}) collective-permute-start(bf16[640,128]{1,0:T(8,128)(2,1)S(1)} %pad_maximum_fusion), channel_id=1, source_target_pairs={{8,0},{33,1},{10,2},{35,3},{12,4},{37,5},{14,6},{39,7},{16,8},{41,... | collective-permute-start | bytes 491528 | tf_op jit(solution)/shard_map/ppermute | solution.py:168
  11.8 3.5 %collective-permute-start.1 = (bf16[640,128]{1,0:T(8,128)(2,1)S(1)}, bf16[640,128]{1,0:T(8,128)(2,1)S(1)}, u32[]{:S(2)}, u32[]{:S(2)}) collective-permute-start(bf16[640,128]{1,0:T(8,128)(2,1)S(1)} %pad_maximum_fusion), channel_id=1, source_target_pairs={{0,0},{41,1},{2,2},{43,3},{4,4},{45,5},{6,6},{47,7},{8,8},{49,9},{... | collective-permute-start | bytes 491528 | tf_op jit(solution)/shard_map/ppermute | solution.py:168
  15.4 2.6 %collective-permute-start.9 = (bf16[640,128]{1,0:T(8,128)(2,1)S(1)}, bf16[640,128]{1,0:T(8,128)(2,1)S(1)}, u32[]{:S(2)}, u32[]{:S(2)}) collective-permute-start(bf16[640,128]{1,0:T(8,128)(2,1)S(1)} %collective-permute-done.8), channel_id=1, source_target_pairs={{64,0},{3,1},{66,2},{5,3},{68,4},{7,5},{70,6},{1,7},{72,8},{11,9},... | collective-permute-start | bytes 491528 | tf_op jit(solution)/shard_map/ppermute | solution.py:168
  18.0 0.6 collective-permute-start.10
  18.6 0.6 collective-permute-start.11
  19.2 4.8 %collective-permute-done.1 = bf16[640,128]{1,0:T(8,128)(2,1)S(1)} collective-permute-done((bf16[640,128]{1,0:T(8,128)(2,1)S(1)}, bf16[640,128]{1,0:T(8,128)(2,1)S(1)}, u32[]{:S(2)}, u32[]{:S(2)}) %collective-permute-start.1) | collective-permute-done | bytes 163872 | tf_op jit(solution)/shard_map/ppermute | solution.py:168
  24.0 2.6 %collective-permute-start.2 = (bf16[640,128]{1,0:T(8,128)(2,1)S(1)}, bf16[640,128]{1,0:T(8,128)(2,1)S(1)}, u32[]{:S(2)}, u32[]{:S(2)}) collective-permute-start(bf16[640,128]{1,0:T(8,128)(2,1)S(1)} %collective-permute-done.1), channel_id=1, source_target_pairs={{64,0},{3,1},{66,2},{5,3},{68,4},{7,5},{70,6},{1,7},{72,8},{11,9},... | collective-permute-start | bytes 491528 | tf_op jit(solution)/shard_map/ppermute | solution.py:168
  26.6 0.5 collective-permute-start.3
  27.1 0.0 collective-permute-done.9
  27.1 0.6 collective-permute-start.4
  27.8 3.9 %collective-permute-start.13 = (bf16[2560,128]{1,0:T(8,128)(2,1)S(1)}, bf16[2560,128]{1,0:T(8,128)(2,1)S(1)}, u32[]{:S(2)}, u32[]{:S(2)}) collective-permute-start(bf16[2560,128]{1,0:T(8,128)(2,1)S(1)} %constant_dynamic-update-slice_fusion.4.refs_4_), channel_id=1, source_target_pairs={{6,0},{193,1},{0,2},{195,3},{2,4},{197,5},{4,6},{199,7},{14,8},{20... | collective-permute-start | bytes 1966088 | tf_op jit(solution)/shard_map/ppermute | solution.py:168
  31.7 0.0 collective-permute-done.2
  31.7 3.0 %collective-permute-start.19 = (bf16[2560,128]{1,0:T(8,128)(2,1)S(1)}, bf16[2560,128]{1,0:T(8,128)(2,1)S(1)}, u32[]{:S(2)}, u32[]{:S(2)}) collective-permute-start(bf16[2560,128]{1,0:T(8,128)(2,1)S(1)} %constant_dynamic-update-slice_fusion.4.refs_4_), channel_id=1, source_target_pairs={{1,0},{0,1},{3,2},{2,3},{5,4},{4,5},{7,6},{6,7},{9,8},{8,9},{11,10... | collective-permute-start | bytes 1966088 | tf_op jit(solution)/shard_map/ppermute | solution.py:168
  34.7 0.0 collective-permute-done.3
  34.8 0.0 copy-start.3
  34.8 0.0 copy-start.5
  34.8 0.0 collective-permute-done.4
  34.8 2.6 %collective-permute-start.5 = (bf16[2560,128]{1,0:T(8,128)(2,1)S(1)}, bf16[2560,128]{1,0:T(8,128)(2,1)}, u32[]{:S(2)}, u32[]{:S(2)}) collective-permute-start(bf16[2560,128]{1,0:T(8,128)(2,1)S(1)} %constant_dynamic-update-slice_fusion.refs_0_), channel_id=1, source_target_pairs={{2,0},{65,1},{4,2},{67,3},{6,4},{69,5},{0,6},{71,7},{10,8},{73,9},... | collective-permute-start | bytes 1966088 | tf_op jit(solution)/shard_map/ppermute | solution.py:168
  37.4 0.2 fusion.20
  37.6 0.1 add_bitcast_fusion
  37.8 0.0 copy-start.7
  37.8 0.6 copy-done.7
  38.4 3.9 %collective-permute-done.13.refs_7_ = bf16[2560,128]{1,0:T(8,128)(2,1)S(1)} collective-permute-done((bf16[2560,128]{1,0:T(8,128)(2,1)S(1)}, bf16[2560,128]{1,0:T(8,128)(2,1)S(1)}, u32[]{:S(2)}, u32[]{:S(2)}) %collective-permute-start.13) | collective-permute-done | bytes 655392 | tf_op jit(solution)/shard_map/ppermute | solution.py:168
  42.4 0.9 collective-permute-start.15
  43.3 0.0 collective-permute-done.12.refs_5_
  43.3 0.6 collective-permute-start.14
  43.8 0.0 collective-permute-done.19.refs_12_
  43.8 1.2 collective-permute-start.20
  45.1 3.5 %collective-permute-done.5.refs_1_ = bf16[2560,128]{1,0:T(8,128)(2,1)} collective-permute-done((bf16[2560,128]{1,0:T(8,128)(2,1)S(1)}, bf16[2560,128]{1,0:T(8,128)(2,1)}, u32[]{:S(2)}, u32[]{:S(2)}) %collective-permute-start.5) | collective-permute-done | bytes 655392 | tf_op jit(solution)/shard_map/ppermute | solution.py:168
  48.6 1.8 %collective-permute-start.6 = (bf16[2560,128]{1,0:T(8,128)(2,1)}, bf16[2560,128]{1,0:T(8,128)(2,1)}, u32[]{:S(2)}, u32[]{:S(2)}) collective-permute-start(bf16[2560,128]{1,0:T(8,128)(2,1)} %collective-permute-done.5.refs_1_), channel_id=1, source_target_pairs={{2,0},{65,1},{4,2},{67,3},{6,4},{69,5},{0,6},{71,7},{10,8},{73,9},... | collective-permute-start | bytes 1966088 | tf_op jit(solution)/shard_map/ppermute | solution.py:168
  50.4 1.1 gather_fusion
  51.6 0.7 convert_bitcast_fusion
  52.2 0.8 copy.22
  53.0 0.1 pad.2.clone
  53.1 0.3 fusion
  53.4 0.0 collective-permute-done.7.refs_3_
  53.4 3.3 %collective-permute-start.22 = (bf16[2560,128]{1,0:T(8,128)(2,1)S(1)}, bf16[2560,128]{1,0:T(8,128)(2,1)S(1)}, u32[]{:S(2)}, u32[]{:S(2)}) collective-permute-start(bf16[2560,128]{1,0:T(8,128)(2,1)S(1)} %collective-permute-done.13.refs_7_), channel_id=1, source_target_pairs={{1,0},{0,1},{3,2},{2,3},{5,4},{4,5},{7,6},{6,7},{9,8},{8,9},{11,10... | collective-permute-start | bytes 1966088 | tf_op jit(solution)/shard_map/ppermute | solution.py:168
  56.7 0.1 collective-permute-start.16
  56.9 4.6 %collective-permute-start.18 = (bf16[2560,128]{1,0:T(8,128)(2,1)}, bf16[2560,128]{1,0:T(8,128)(2,1)S(1)}, u32[]{:S(2)}, u32[]{:S(2)}) collective-permute-start(bf16[2560,128]{1,0:T(8,128)(2,1)} %collective-permute-done.7.refs_3_), channel_id=1, source_target_pairs={{1,0},{0,1},{3,2},{2,3},{5,4},{4,5},{7,6},{6,7},{9,8},{8,9},{11,10... | collective-permute-start | bytes 1966088 | tf_op jit(solution)/shard_map/ppermute | solution.py:168
  61.5 0.0 collective-permute-start.21
  61.5 0.6 collective-permute-start.17
  62.1 1.3 %collective-permute-done.18.refs_11_ = bf16[2560,128]{1,0:T(8,128)(2,1)S(1)} collective-permute-done((bf16[2560,128]{1,0:T(8,128)(2,1)}, bf16[2560,128]{1,0:T(8,128)(2,1)S(1)}, u32[]{:S(2)}, u32[]{:S(2)}) %collective-permute-start.18) | collective-permute-done | bytes 655392 | tf_op jit(solution)/shard_map/ppermute | solution.py:168
  63.4 0.9 collective-permute-done.21.refs_14_
  64.3 0.9 collective-permute-done.17.refs_10_
  65.3 30.5 %tile_sums.1 = f32[128,128]{1,0:T(8,128)S(1)} custom-call(s32[32768]{0:T(1024)S(1)} %bitcast.23, f32[128,128]{1,0:T(8,128)S(1)} %broadcast_select_fusion.3.w0_ref, f32[128,128]{1,0:T(8,128)S(1)} %get-tuple-element.7.w1_ref, bf16[2560,128]{1,0:T(8,128)(2,1)S(1)} %constant_dynamic-update-slice_fusion.refs_0_, ...), custom_call_target="tpu_custom_call" | custom-call | tf_op jit(solution)/shard_map/tile_sums/pallas_call | solution.py:140
  95.8 0.1 slice_add_fusion
  95.9 0.7 copy-done.4
  96.6 0.5 fusion.5
  97.1 0.1 reshape_reshape.6
  97.2 0.3 copy.23
  97.4 25.2 %all_to_all.5 = f32[256,1,1,256]{3,1,2,0:T(1,128)S(1)} all-to-all(f32[256,1,1,256]{3,1,2,0:T(1,128)S(1)} %bitcast.25), channel_id=1, replica_groups=mesh['grp'=4,'dev'=64] {'dev','grp'}, dimensions={0} | all-to-all | bytes 524288 | tf_op jit(solution)/shard_map/all_to_all | solution.py:31
  122.7 0.1 copy.28
  122.8 0.2 fusion.2
  123.0 0.5 fusion.3
  123.5 0.9 convolution_add_fusion
  (41 shorter events, 0.4 us)
Async XLA Ops:
  0.0 50.4 %copy-start = (s32[16384]{0:T(1024)S(1)}, s32[16384]{0:T(1024)}, u32[]{:S(2)}) copy-start(s32[16384]{0:T(1024)} %param.11) | copy-start | bytes 196612
  1.1 0.8 copy-start.6
  2.3 4.2 %collective-permute-start = (bf16[320,128]{1,0:T(8,128)(2,1)S(1)}, bf16[320,128]{1,0:T(8,128)(2,1)S(1)}, u32[]{:S(2)}, u32[]{:S(2)}) collective-permute-start(bf16[320,128]{1,0:T(8,128)(2,1)S(1)} %broadcast_select_fusion), channel_id=1, source_target_pairs={{1,0},{0,1},{3,2},{2,3},{5,4},{4,5},{7,6},{6,7},{9,8},{8,9},{11,10... | collective-permute-start | bytes 245768 | tf_op jit(solution)/shard_map/ppermute | solution.py:168
  6.6 8.8 %collective-permute-start.8 = (bf16[640,128]{1,0:T(8,128)(2,1)S(1)}, bf16[640,128]{1,0:T(8,128)(2,1)S(1)}, u32[]{:S(2)}, u32[]{:S(2)}) collective-permute-start(bf16[640,128]{1,0:T(8,128)(2,1)S(1)} %pad_maximum_fusion), channel_id=1, source_target_pairs={{8,0},{33,1},{10,2},{35,3},{12,4},{37,5},{14,6},{39,7},{16,8},{41,... | collective-permute-start | bytes 491528 | tf_op jit(solution)/shard_map/ppermute | solution.py:168
  11.8 12.2 %collective-permute-start.1 = (bf16[640,128]{1,0:T(8,128)(2,1)S(1)}, bf16[640,128]{1,0:T(8,128)(2,1)S(1)}, u32[]{:S(2)}, u32[]{:S(2)}) collective-permute-start(bf16[640,128]{1,0:T(8,128)(2,1)S(1)} %pad_maximum_fusion), channel_id=1, source_target_pairs={{0,0},{41,1},{2,2},{43,3},{4,4},{45,5},{6,6},{47,7},{8,8},{49,9},{... | collective-permute-start | bytes 491528 | tf_op jit(solution)/shard_map/ppermute | solution.py:168
  15.4 11.7 %collective-permute-start.9 = (bf16[640,128]{1,0:T(8,128)(2,1)S(1)}, bf16[640,128]{1,0:T(8,128)(2,1)S(1)}, u32[]{:S(2)}, u32[]{:S(2)}) collective-permute-start(bf16[640,128]{1,0:T(8,128)(2,1)S(1)} %collective-permute-done.8), channel_id=1, source_target_pairs={{64,0},{3,1},{66,2},{5,3},{68,4},{7,5},{70,6},{1,7},{72,8},{11,9},... | collective-permute-start | bytes 491528 | tf_op jit(solution)/shard_map/ppermute | solution.py:168
  18.0 9.8 %collective-permute-start.10 = (bf16[640,128]{1,0:T(8,128)(2,1)S(1)}, bf16[640,128]{1,0:T(8,128)(2,1)S(1)}, u32[]{:S(2)}, u32[]{:S(2)}) collective-permute-start(bf16[640,128]{1,0:T(8,128)(2,1)S(1)} %collective-permute-done.8), channel_id=1, source_target_pairs={{128,0},{5,1},{130,2},{7,3},{132,4},{1,5},{134,6},{3,7},{136,8},{1... | collective-permute-start | bytes 491528 | tf_op jit(solution)/shard_map/ppermute | solution.py:168
  18.6 9.2 %collective-permute-start.11 = (bf16[640,128]{1,0:T(8,128)(2,1)S(1)}, bf16[640,128]{1,0:T(8,128)(2,1)S(1)}, u32[]{:S(2)}, u32[]{:S(2)}) collective-permute-start(bf16[640,128]{1,0:T(8,128)(2,1)S(1)} %collective-permute-done.8), channel_id=1, source_target_pairs={{192,0},{7,1},{194,2},{1,3},{196,4},{3,5},{198,6},{5,7},{200,8},{1... | collective-permute-start | bytes 491528 | tf_op jit(solution)/shard_map/ppermute | solution.py:168
  24.0 7.7 %collective-permute-start.2 = (bf16[640,128]{1,0:T(8,128)(2,1)S(1)}, bf16[640,128]{1,0:T(8,128)(2,1)S(1)}, u32[]{:S(2)}, u32[]{:S(2)}) collective-permute-start(bf16[640,128]{1,0:T(8,128)(2,1)S(1)} %collective-permute-done.1), channel_id=1, source_target_pairs={{64,0},{3,1},{66,2},{5,3},{68,4},{7,5},{70,6},{1,7},{72,8},{11,9},... | collective-permute-start | bytes 491528 | tf_op jit(solution)/shard_map/ppermute | solution.py:168
  26.6 8.1 %collective-permute-start.3 = (bf16[640,128]{1,0:T(8,128)(2,1)S(1)}, bf16[640,128]{1,0:T(8,128)(2,1)S(1)}, u32[]{:S(2)}, u32[]{:S(2)}) collective-permute-start(bf16[640,128]{1,0:T(8,128)(2,1)S(1)} %collective-permute-done.1), channel_id=1, source_target_pairs={{128,0},{5,1},{130,2},{7,3},{132,4},{1,5},{134,6},{3,7},{136,8},{1... | collective-permute-start | bytes 491528 | tf_op jit(solution)/shard_map/ppermute | solution.py:168
  27.1 7.7 %collective-permute-start.4 = (bf16[640,128]{1,0:T(8,128)(2,1)S(1)}, bf16[640,128]{1,0:T(8,128)(2,1)S(1)}, u32[]{:S(2)}, u32[]{:S(2)}) collective-permute-start(bf16[640,128]{1,0:T(8,128)(2,1)S(1)} %collective-permute-done.1), channel_id=1, source_target_pairs={{192,0},{7,1},{194,2},{1,3},{196,4},{3,5},{198,6},{5,7},{200,8},{1... | collective-permute-start | bytes 491528 | tf_op jit(solution)/shard_map/ppermute | solution.py:168
  27.8 14.5 %collective-permute-start.13 = (bf16[2560,128]{1,0:T(8,128)(2,1)S(1)}, bf16[2560,128]{1,0:T(8,128)(2,1)S(1)}, u32[]{:S(2)}, u32[]{:S(2)}) collective-permute-start(bf16[2560,128]{1,0:T(8,128)(2,1)S(1)} %constant_dynamic-update-slice_fusion.4.refs_4_), channel_id=1, source_target_pairs={{6,0},{193,1},{0,2},{195,3},{2,4},{197,5},{4,6},{199,7},{14,8},{20... | collective-permute-start | bytes 1966088 | tf_op jit(solution)/shard_map/ppermute | solution.py:168
  31.7 11.5 %collective-permute-start.12 = (bf16[2560,128]{1,0:T(8,128)(2,1)S(1)}, bf16[2560,128]{1,0:T(8,128)(2,1)S(1)}, u32[]{:S(2)}, u32[]{:S(2)}) collective-permute-start(bf16[2560,128]{1,0:T(8,128)(2,1)S(1)} %constant_dynamic-update-slice_fusion.4.refs_4_), channel_id=1, source_target_pairs={{2,0},{65,1},{4,2},{67,3},{6,4},{69,5},{0,6},{71,7},{10,8},{73,9},... | collective-permute-start | bytes 1966088 | tf_op jit(solution)/shard_map/ppermute | solution.py:168
  31.7 12.1 %collective-permute-start.19 = (bf16[2560,128]{1,0:T(8,128)(2,1)S(1)}, bf16[2560,128]{1,0:T(8,128)(2,1)S(1)}, u32[]{:S(2)}, u32[]{:S(2)}) collective-permute-start(bf16[2560,128]{1,0:T(8,128)(2,1)S(1)} %constant_dynamic-update-slice_fusion.4.refs_4_), channel_id=1, source_target_pairs={{1,0},{0,1},{3,2},{2,3},{5,4},{4,5},{7,6},{6,7},{9,8},{8,9},{11,10... | collective-permute-start | bytes 1966088 | tf_op jit(solution)/shard_map/ppermute | solution.py:168
  34.8 2.7 %copy-start.3 = (s32[128,128]{1,0:T(8,128)S(1)}, s32[128,128]{1,0:T(8,128)}, u32[]{:S(2)}) copy-start(s32[128,128]{1,0:T(8,128)} %param.7) | copy-start | bytes 196612
  34.8 2.7 %copy-start.5 = (s32[128,128]{1,0:T(8,128)S(1)}, s32[128,128]{1,0:T(8,128)}, u32[]{:S(2)}) copy-start(s32[128,128]{1,0:T(8,128)} %param.8) | copy-start | bytes 196612
  34.8 13.7 %collective-permute-start.5 = (bf16[2560,128]{1,0:T(8,128)(2,1)S(1)}, bf16[2560,128]{1,0:T(8,128)(2,1)}, u32[]{:S(2)}, u32[]{:S(2)}) collective-permute-start(bf16[2560,128]{1,0:T(8,128)(2,1)S(1)} %constant_dynamic-update-slice_fusion.refs_0_), channel_id=1, source_target_pairs={{2,0},{65,1},{4,2},{67,3},{6,4},{69,5},{0,6},{71,7},{10,8},{73,9},... | collective-permute-start | bytes 1966088 | tf_op jit(solution)/shard_map/ppermute | solution.py:168
  37.8 0.7 copy-start.7
  38.4 15.0 %collective-permute-start.7 = (bf16[2560,128]{1,0:T(8,128)(2,1)S(1)}, bf16[2560,128]{1,0:T(8,128)(2,1)}, u32[]{:S(2)}, u32[]{:S(2)}) collective-permute-start(bf16[2560,128]{1,0:T(8,128)(2,1)S(1)} %constant_dynamic-update-slice_fusion.refs_0_), channel_id=1, source_target_pairs={{6,0},{193,1},{0,2},{195,3},{2,4},{197,5},{4,6},{199,7},{14,8},{20... | collective-permute-start | bytes 1966088 | tf_op jit(solution)/shard_map/ppermute | solution.py:168
  42.4 14.4 %collective-permute-start.15 = (bf16[2560,128]{1,0:T(8,128)(2,1)S(1)}, bf16[2560,128]{1,0:T(8,128)(2,1)}, u32[]{:S(2)}, u32[]{:S(2)}) collective-permute-start(bf16[2560,128]{1,0:T(8,128)(2,1)S(1)} %constant_dynamic-update-slice_fusion.refs_0_), channel_id=1, source_target_pairs={{1,0},{0,1},{3,2},{2,3},{5,4},{4,5},{7,6},{6,7},{9,8},{8,9},{11,10... | collective-permute-start | bytes 1966088 | tf_op jit(solution)/shard_map/ppermute | solution.py:168
  43.3 13.6 %collective-permute-start.14 = (bf16[2560,128]{1,0:T(8,128)(2,1)S(1)}, bf16[2560,128]{1,0:T(8,128)(2,1)}, u32[]{:S(2)}, u32[]{:S(2)}) collective-permute-start(bf16[2560,128]{1,0:T(8,128)(2,1)S(1)} %collective-permute-done.13.refs_7_), channel_id=1, source_target_pairs={{6,0},{193,1},{0,2},{195,3},{2,4},{197,5},{4,6},{199,7},{14,8},{20... | collective-permute-start | bytes 1966088 | tf_op jit(solution)/shard_map/ppermute | solution.py:168
  43.8 17.6 %collective-permute-start.20 = (bf16[2560,128]{1,0:T(8,128)(2,1)S(1)}, bf16[2560,128]{1,0:T(8,128)(2,1)}, u32[]{:S(2)}, u32[]{:S(2)}) collective-permute-start(bf16[2560,128]{1,0:T(8,128)(2,1)S(1)} %collective-permute-done.12.refs_5_), channel_id=1, source_target_pairs={{1,0},{0,1},{3,2},{2,3},{5,4},{4,5},{7,6},{6,7},{9,8},{8,9},{11,10... | collective-permute-start | bytes 1966088 | tf_op jit(solution)/shard_map/ppermute | solution.py:168
  48.6 12.9 %collective-permute-start.6 = (bf16[2560,128]{1,0:T(8,128)(2,1)}, bf16[2560,128]{1,0:T(8,128)(2,1)}, u32[]{:S(2)}, u32[]{:S(2)}) collective-permute-start(bf16[2560,128]{1,0:T(8,128)(2,1)} %collective-permute-done.5.refs_1_), channel_id=1, source_target_pairs={{2,0},{65,1},{4,2},{67,3},{6,4},{69,5},{0,6},{71,7},{10,8},{73,9},... | collective-permute-start | bytes 1966088 | tf_op jit(solution)/shard_map/ppermute | solution.py:168
  53.1 9.0 %copy-start.2 = (f32[128,128]{1,0:T(8,128)S(1)}, f32[128,128]{1,0:T(8,128)}, u32[]{:S(2)}) copy-start(f32[128,128]{1,0:T(8,128)} %param.9) | copy-start | bytes 196612
  53.4 8.7 %collective-permute-start.22 = (bf16[2560,128]{1,0:T(8,128)(2,1)S(1)}, bf16[2560,128]{1,0:T(8,128)(2,1)S(1)}, u32[]{:S(2)}, u32[]{:S(2)}) collective-permute-start(bf16[2560,128]{1,0:T(8,128)(2,1)S(1)} %collective-permute-done.13.refs_7_), channel_id=1, source_target_pairs={{1,0},{0,1},{3,2},{2,3},{5,4},{4,5},{7,6},{6,7},{9,8},{8,9},{11,10... | collective-permute-start | bytes 1966088 | tf_op jit(solution)/shard_map/ppermute | solution.py:168
  56.7 5.4 %collective-permute-start.16 = (bf16[2560,128]{1,0:T(8,128)(2,1)}, bf16[2560,128]{1,0:T(8,128)(2,1)S(1)}, u32[]{:S(2)}, u32[]{:S(2)}) collective-permute-start(bf16[2560,128]{1,0:T(8,128)(2,1)} %collective-permute-done.5.refs_1_), channel_id=1, source_target_pairs={{1,0},{0,1},{3,2},{2,3},{5,4},{4,5},{7,6},{6,7},{9,8},{8,9},{11,10... | collective-permute-start | bytes 1966088 | tf_op jit(solution)/shard_map/ppermute | solution.py:168
  56.9 6.5 %collective-permute-start.18 = (bf16[2560,128]{1,0:T(8,128)(2,1)}, bf16[2560,128]{1,0:T(8,128)(2,1)S(1)}, u32[]{:S(2)}, u32[]{:S(2)}) collective-permute-start(bf16[2560,128]{1,0:T(8,128)(2,1)} %collective-permute-done.7.refs_3_), channel_id=1, source_target_pairs={{1,0},{0,1},{3,2},{2,3},{5,4},{4,5},{7,6},{6,7},{9,8},{8,9},{11,10... | collective-permute-start | bytes 1966088 | tf_op jit(solution)/shard_map/ppermute | solution.py:168
  61.5 2.9 %collective-permute-start.21 = (bf16[2560,128]{1,0:T(8,128)(2,1)}, bf16[2560,128]{1,0:T(8,128)(2,1)S(1)}, u32[]{:S(2)}, u32[]{:S(2)}) collective-permute-start(bf16[2560,128]{1,0:T(8,128)(2,1)} %collective-permute-done.14.refs_6_), channel_id=1, source_target_pairs={{1,0},{0,1},{3,2},{2,3},{5,4},{4,5},{7,6},{6,7},{9,8},{8,9},{11,10... | collective-permute-start | bytes 1966088 | tf_op jit(solution)/shard_map/ppermute | solution.py:168
  61.5 3.8 %collective-permute-start.17 = (bf16[2560,128]{1,0:T(8,128)(2,1)}, bf16[2560,128]{1,0:T(8,128)(2,1)S(1)}, u32[]{:S(2)}, u32[]{:S(2)}) collective-permute-start(bf16[2560,128]{1,0:T(8,128)(2,1)} %collective-permute-done.6.refs_2_), channel_id=1, source_target_pairs={{1,0},{0,1},{3,2},{2,3},{5,4},{4,5},{7,6},{6,7},{9,8},{8,9},{11,10... | collective-permute-start | bytes 1966088 | tf_op jit(solution)/shard_map/ppermute | solution.py:168
  62.1 3.2 %copy-start.1 = (bf16[2560,128]{1,0:T(8,128)(2,1)}, bf16[2560,128]{1,0:T(8,128)(2,1)S(1)}, u32[]{:S(2)}) copy-start(bf16[2560,128]{1,0:T(8,128)(2,1)S(1)} %collective-permute-done.22.refs_15_) | copy-start | bytes 1966084
  95.8 0.8 copy-start.4

commit v5 on v4

--- a/solution.py
+++ b/solution.py
@@ -33,7 +33,7 @@
     return joined_along(pieces, concats[1])
 
 
-NT = 8
+NT = 4
 CH = NT * 128
 SHARD_U = 256
 SHARD_S = 64
@@ -48,42 +48,51 @@
     return out
 
 
-def tile_kernel(counts, tiles, idx_hbm, w0_ref, w1_ref, *refs):
+def tile_kernel(counts, range_ref, idx_hbm, w0_ref, w1_ref, *refs):
     f32 = jnp.float32
     n = len(counts)
-    pieces, (out_ref, utab, stab, stage, bufa, bufb, sem, isem) = refs[:n], refs[n:]
-    bufs = (bufa, bufb)
-    steps = tiles // (2 * NT)
+    pieces, (out_ref, utab, stab, stage, buf0, buf1, buf2, buf3, sem, isem) = refs[:n], refs[n:]
+    bufs = (buf0, buf1, buf2, buf3)
+    nb = len(bufs)
+    c0, c1 = range_ref[0], range_ref[1]
+    group0, group1 = c0 // nb, (c1 + nb - 1) // nb
 
     def icopy(c, b):
-        return pltpu.make_async_copy(idx_hbm.at[pl.ds(c * 2 * CH, 2 * CH)], bufs[b], isem.at[b])
-
-    icopy(0, 0).start()
-    icopy(1, 1).start()
-    starts = [sum(counts[:k]) for k in range(n)]
-
-    def tcopy(k):
-        rows = pl.ds(starts[k] * SHARD, counts[k] * SHARD)
-        return pltpu.make_async_copy(pieces[k], stage.at[rows, :], sem.at[k])
+        rows = pl.ds(pl.multiple_of(c * 2 * CH, 2 * CH), 2 * CH)
+        return pltpu.make_async_copy(idx_hbm.at[rows], bufs[b], isem.at[b])
+
+    for b in range(nb):
+        c = group0 * nb + b
+
+        @pl.when((c >= c0) & (c < c1))
+        def _():
+            icopy(c, b).start()
+
+    per = counts[0]
+
+    def tcopy(source, k):
+        rows = pl.ds(pl.multiple_of(k * per * SHARD, per * SHARD), per * SHARD)
+        return pltpu.make_async_copy(source, stage.at[rows, :], sem.at[k])
 
     for k in range(n):
-        tcopy(k).start()
+        tcopy(pieces[k], k).start()
+    out_ref[...] = jnp.zeros_like(out_ref)
     low = lax.broadcasted_iota(jnp.int32, (SHARD_S, 128), 1) < 64
 
-    def conv(slot, carry):
-        src = pl.multiple_of(slot * SHARD, SHARD_S)
-        urow = pl.multiple_of(slot * SHARD_U, SHARD_U)
-        srow = pl.multiple_of(slot * 2 * SHARD_S, 2 * SHARD_S)
-        utab[pl.ds(urow, SHARD_U), :] = stage[pl.ds(src, SHARD_U), :].astype(f32)
-        x = stage[pl.ds(src + SHARD_U, SHARD_S), :].astype(f32)
-        r = pltpu.roll(x, 64, 1)
-        stab[pl.ds(srow, SHARD_S), :] = jnp.where(low, x, r)
-        stab[pl.ds(srow + SHARD_S, SHARD_S), :] = jnp.where(low, r, x)
+    def conv(k, carry):
+        tcopy(pieces[0], k).wait()
+        src = pl.multiple_of(k * per * SHARD, per * SHARD)
+        urow = pl.multiple_of(k * per * SHARD_U, per * SHARD_U)
+        srow = pl.multiple_of(k * per * 2 * SHARD_S, per * 2 * SHARD_S)
+        for e in range(per):
+            utab[pl.ds(urow + e * SHARD_U, SHARD_U), :] = stage[pl.ds(src + e * SHARD, SHARD_U), :].astype(f32)
+            x = stage[pl.ds(src + e * SHARD + SHARD_U, SHARD_S), :].astype(f32)
+            r = pltpu.roll(x, 64, 1)
+            stab[pl.ds(srow + e * 2 * SHARD_S, SHARD_S), :] = jnp.where(low, x, r)
+            stab[pl.ds(srow + (e * 2 + 1) * SHARD_S, SHARD_S), :] = jnp.where(low, r, x)
         return carry
 
-    for k in range(n):
-        tcopy(k).wait()
-        lax.fori_loop(starts[k], starts[k] + counts[k], conv, 0)
+    lax.fori_loop(0, n, conv, 0)
 
     def tile(buf, j, t):
         w0 = w0_ref[pl.ds(t, 1), :]
@@ -98,19 +107,22 @@
         out_ref[pl.ds(t, 1), :] = jnp.sum(acc, axis=0, keepdims=True)
 
     def body(i, carry):
-        for b in range(2):
-            c = i * 2 + b
-            icopy(c, b).wait()
-            for j in range(NT):
-                tile(bufs[b], j, c * NT + j)
-
-            @pl.when(i < steps - 1)
+        for b in range(nb):
+            c = i * nb + b
+
+            @pl.when((c >= c0) & (c < c1))
             def _():
-                icopy(c + 2, b).start()
+                icopy(c, b).wait()
+                for j in range(NT):
+                    tile(bufs[b], j, c * NT + j)
+
+            @pl.when(c + nb < c1)
+            def _():
+                icopy(c + nb, b).start()
 
         return carry
 
-    lax.fori_loop(0, steps, body, 0)
+    lax.fori_loop(group0, group1, body, 0)
 
 
 def slot_of(dev, color):
@@ -126,35 +138,36 @@
     return (far_side * 32 + jnp.where(color == 0, first, second)) * 2 + ((dev ^ color) & 1)
 
 
-def tile_sums(pieces, nz_user, nz_sub, nz_value):
-    tiles, width = nz_user.shape
-    counts = tuple(p.shape[0] // SHARD for p in pieces)
-    slots = sum(counts)
+def tile_inputs(nz_user, nz_sub, nz_value):
     user_row = slot_of(nz_user >> 10, (nz_user >> 8) & 1) * SHARD_U + (nz_user & 255)
     sub_row = (slot_of(nz_sub >> 8, (nz_sub >> 6) & 1) * 2 + ((nz_sub >> 7) & 1)) * SHARD_S + (nz_sub & 63)
     high = ((nz_user >> 9) & 1) == 1
     w1 = jnp.where(high, nz_value, 0.0)
     w0 = jnp.where(high, 0.0, nz_value)
-    idx = jnp.concatenate([user_row.reshape(-1, 1, CH), sub_row.reshape(-1, 1, CH)], axis=1).reshape(-1)
+    return jnp.concatenate([user_row.astype(jnp.float32), sub_row.astype(jnp.float32), w0, w1], axis=1)
+
+
+def tile_sums(pieces, span, idx, w0, w1, name):
+    tiles = w0.shape[0]
+    counts = tuple(p.shape[0] // SHARD for p in pieces)
+    slots = sum(counts)
     vmem = pl.BlockSpec(memory_space=pltpu.VMEM)
+    hbm = pl.BlockSpec(memory_space=pltpu.HBM)
     out = pl.pallas_call(
-        functools.partial(tile_kernel, counts, tiles),
+        functools.partial(tile_kernel, counts),
         out_shape=jax.ShapeDtypeStruct((tiles, 128), jnp.float32),
-        in_specs=[pl.BlockSpec(memory_space=pltpu.HBM), vmem, vmem]
-        + [pl.BlockSpec(memory_space=pltpu.HBM)] * len(pieces),
+        in_specs=[pl.BlockSpec(memory_space=pltpu.SMEM), hbm, vmem, vmem] + [hbm] * len(pieces),
         out_specs=vmem,
         scratch_shapes=[
             pltpu.VMEM((slots * SHARD_U, 128), jnp.float32),
             pltpu.VMEM((slots * 2 * SHARD_S, 128), jnp.float32),
             pltpu.VMEM((slots * SHARD, 128), jnp.bfloat16),
-            pltpu.SMEM((2 * CH,), jnp.int32),
-            pltpu.SMEM((2 * CH,), jnp.int32),
-            pltpu.SemaphoreType.DMA((len(pieces),)),
-            pltpu.SemaphoreType.DMA((2,)),
-        ],
+        ]
+        + [pltpu.SMEM((2 * CH,), jnp.int32)] * 4
+        + [pltpu.SemaphoreType.DMA((len(pieces),)), pltpu.SemaphoreType.DMA((4,))],
         compiler_params=pltpu.CompilerParams(vmem_limit_bytes=44 * 2**20),
-        name="tile_sums",
-    )(idx, w0, w1, *pieces)
+        name=name,
+    )(span, idx, w0, w1, *pieces)
     return out[:, :64] + out[:, 64:]
 
 
@@ -209,26 +222,46 @@
     users, subs = packed(user_factor), packed(sub_factor)
     mine_a = jnp.concatenate([users[:SHARD_U], subs[:SHARD_S]], axis=0)
     mine_b = jnp.concatenate([users[SHARD_U:], subs[SHARD_S:]], axis=0)
-    tile_rows = tile_sums(gathered((mine_a, mine_b)), nz_user, nz_sub, nz_value)
-    tile_count, rank_width = tile_rows.shape
+    pieces = gathered((mine_a, mine_b))
+    tile_count = nz_user.shape[0]
+    rank_width = user_factor.shape[0]
     grp_size = lax.axis_size("grp")
     dev_size = lax.axis_size("dev")
     devices_all = grp_size * dev_size
     words_total = word_owner.shape[0]
     words_local = words_total // devices_all
-    out_rows = jnp.take(word_owner, tile_word)
     self_index = lax.axis_index("grp") * dev_size + lax.axis_index("dev")
+    tile_ids = jnp.arange(tile_count, dtype=jnp.int32)
+    rows_given = jnp.take(word_owner, tile_word)
+    remote = (rows_given // words_local != self_index).astype(jnp.int32)
+    remote_before = jnp.sum(jnp.where(tile_ids[:, None] < tile_ids[None, :], remote[:, None], 0), axis=0)
+    remote_count = jnp.sum(remote)
+    place = jnp.where(remote == 1, remote_before, remote_count + tile_ids - remote_before)
+    order = (tile_ids[:, None] == place[None, :]).astype(jnp.float32)
+    inputs = jnp.concatenate(
+        [tile_inputs(nz_user, nz_sub, nz_value), rows_given.astype(jnp.float32)[:, None]], axis=1
+    )
+    inputs = jnp.dot(order, inputs, precision=lax.Precision.HIGHEST, preferred_element_type=jnp.float32)
+    width = nz_user.shape[1]
+    idx = inputs[:, : 2 * width].astype(jnp.int32).reshape(-1, NT, 2, width)
+    idx = jnp.swapaxes(idx, 1, 2).reshape(-1)
+    w0, w1 = inputs[:, 2 * width : 3 * width], inputs[:, 3 * width : 4 * width]
+    out_rows = inputs[:, 4 * width].astype(jnp.int32)
+    chunks = tile_count // NT
+    first_span = jnp.stack([jnp.zeros_like(remote_count), (remote_count + NT - 1) // NT])
+    second_span = jnp.stack([remote_count // NT, jnp.full_like(remote_count, chunks)])
+    tile_rows = tile_sums(pieces, first_span, idx, w0, w1, "remote_tiles")
+    own_rows = tile_sums(pieces, second_span, idx, w0, w1, "own_tiles")
     owner_dev = out_rows // words_local
     local_row = out_rows - owner_dev * words_local
     owned = owner_dev == self_index
     columns = jnp.arange(words_local, dtype=jnp.int32)
     own_table = (owned[:, None] & (local_row[:, None] == columns[None, :])).astype(jnp.float32)
-    own_part = jnp.einsum("tr,tk->rk", tile_rows, own_table, precision=lax.Precision.HIGHEST)
+    own_part = jnp.einsum("tr,tk->rk", own_rows, own_table, precision=lax.Precision.HIGHEST)
     peer_ids = jnp.arange(devices_all, dtype=jnp.int32)
     outgoing = (jnp.logical_not(owned)[:, None] & (owner_dev[:, None] == peer_ids[None, :])).astype(
         jnp.float32
     )
-    tile_ids = jnp.arange(tile_count, dtype=jnp.int32)
     earlier_table = (tile_ids[:, None] > tile_ids[None, :]).astype(jnp.float32)
     earlier = jnp.dot(
         earlier_table, outgoing, precision=lax.Precision.HIGHEST, preferred_element_type=jnp.float32

time: 125 us -> 138 us (1.10)
  the two profiles are of different devices: /device:TPU:1 before, /device:TPU:41 now
where the time goes in v5:
time: 138 us; the launch traced here: 137 us
  starting transfers between devices  56 us (41%)
  Pallas kernels  29.3 us (21%)
  local copies, waits for them, and re-layouts  20.8 us (15%)
  waiting for transfers between devices  17.2 us (12%)
  other arithmetic  6.34 us (5%)
  between operations  3.71 us (3%)
  matrix products  3.31 us (2%)
    ppermute x23, starting transfers between devices, fetched(): return lax.ppermute(value, ('grp', 'dev'), pairs)  37.4 us
    pallas_call x2, Pallas kernels, tile_sums(): pl.pallas_call(functools.partial(tile_kernel, counts), out_shape=jax.Shap...  29.3 us
    all_to_all x1, starting transfers between devices, exchange_both(): lax.all_to_all(pieces, axis, split_axis=0, concat_axis=0, tiled=True)  18.6 us
    ppermute x23, waiting for transfers between devices, fetched(): return lax.ppermute(value, ('grp', 'dev'), pairs)  17.2 us
    unnamed x47, local copies, waits for them, and re-layouts  8.68 us
    another operation x2, local copies, waits for them, and re-layouts, cut_along(): value.reshape(*shape[:dim], peers, shape[dim] // peers, *shape[dim + 1:])  3.64 us
  transfers between devices with their start and end apart: 24, of which 5 were waited for; matrix products, arithmetic and copies ran while one was open for 12% of the time, Pallas kernels for 15%

profile of v5, /device:TPU:41, one launch (start us, length us, event | category | flops | bytes accessed | tf_op | source)
XLA Modules:
  0.0 136.7 jit_solution(10988902061856790700)
XLA Ops:
  0.0 0.9 copy.32
  1.0 0.2 copy.31
  1.3 0.1 broadcast_select_fusion.1
  1.5 0.8 collective-permute-start
  2.3 0.7 copy-done.17
  2.9 1.1 gather_fusion
  4.2 0.7 copy-done.13
  5.1 0.7 copy-done.10
  5.8 0.6 fusion.71
  6.5 0.1 copy.26
  6.6 5.6 %collective-permute-start.8 = (bf16[640,128]{1,0:T(8,128)(2,1)S(1)}, bf16[640,128]{1,0:T(8,128)(2,1)S(1)}, u32[]{:S(2)}, u32[]{:S(2)}) collective-permute-start(bf16[640,128]{1,0:T(8,128)(2,1)S(1)} %pad_maximum_fusion), channel_id=1, source_target_pairs={{8,0},{33,1},{10,2},{35,3},{12,4},{37,5},{14,6},{39,7},{16,8},{41,... | collective-permute-start | bytes 491528 | tf_op jit(solution)/shard_map/ppermute | solution.py:181
  12.2 1.9 %collective-permute-start.1 = (bf16[640,128]{1,0:T(8,128)(2,1)S(1)}, bf16[640,128]{1,0:T(8,128)(2,1)S(1)}, u32[]{:S(2)}, u32[]{:S(2)}) collective-permute-start(bf16[640,128]{1,0:T(8,128)(2,1)S(1)} %pad_maximum_fusion), channel_id=1, source_target_pairs={{0,0},{41,1},{2,2},{43,3},{4,4},{45,5},{6,6},{47,7},{8,8},{49,9},{... | collective-permute-start | bytes 491528 | tf_op jit(solution)/shard_map/ppermute | solution.py:181
  14.2 7.6 %collective-permute-done.8 = bf16[640,128]{1,0:T(8,128)(2,1)S(1)} collective-permute-done((bf16[640,128]{1,0:T(8,128)(2,1)S(1)}, bf16[640,128]{1,0:T(8,128)(2,1)S(1)}, u32[]{:S(2)}, u32[]{:S(2)}) %collective-permute-start.8) | collective-permute-done | bytes 163872 | tf_op jit(solution)/shard_map/ppermute | solution.py:181
  21.8 1.2 collective-permute-start.11
  23.0 2.5 %collective-permute-start.10 = (bf16[640,128]{1,0:T(8,128)(2,1)S(1)}, bf16[640,128]{1,0:T(8,128)(2,1)S(1)}, u32[]{:S(2)}, u32[]{:S(2)}) collective-permute-start(bf16[640,128]{1,0:T(8,128)(2,1)S(1)} %collective-permute-done.8), channel_id=1, source_target_pairs={{128,0},{5,1},{130,2},{7,3},{132,4},{1,5},{134,6},{3,7},{136,8},{1... | collective-permute-start | bytes 491528 | tf_op jit(solution)/shard_map/ppermute | solution.py:181
  25.4 1.2 collective-permute-start.9
  26.6 0.3 collective-permute-start.4
  26.9 0.9 collective-permute-start.3
  27.8 2.1 %collective-permute-done.9 = bf16[640,128]{1,0:T(8,128)(2,1)S(1)} collective-permute-done((bf16[640,128]{1,0:T(8,128)(2,1)S(1)}, bf16[640,128]{1,0:T(8,128)(2,1)S(1)}, u32[]{:S(2)}, u32[]{:S(2)}) %collective-permute-start.9) | collective-permute-done | bytes 163872 | tf_op jit(solution)/shard_map/ppermute | solution.py:181
  29.9 2.2 %collective-permute-start.2 = (bf16[640,128]{1,0:T(8,128)(2,1)S(1)}, bf16[640,128]{1,0:T(8,128)(2,1)S(1)}, u32[]{:S(2)}, u32[]{:S(2)}) collective-permute-start(bf16[640,128]{1,0:T(8,128)(2,1)S(1)} %collective-permute-done.1), channel_id=1, source_target_pairs={{64,0},{3,1},{66,2},{5,3},{68,4},{7,5},{70,6},{1,7},{72,8},{11,9},... | collective-permute-start | bytes 491528 | tf_op jit(solution)/shard_map/ppermute | solution.py:181
  32.3 0.2 collective-permute-start.13
  32.5 2.1 %collective-permute-done.2 = bf16[640,128]{1,0:T(8,128)(2,1)S(1)} collective-permute-done((bf16[640,128]{1,0:T(8,128)(2,1)S(1)}, bf16[640,128]{1,0:T(8,128)(2,1)S(1)}, u32[]{:S(2)}, u32[]{:S(2)}) %collective-permute-start.2) | collective-permute-done | bytes 163872 | tf_op jit(solution)/shard_map/ppermute | solution.py:181
  34.7 2.7 %collective-permute-start.5 = (bf16[2560,128]{1,0:T(8,128)(2,1)S(1)}, bf16[2560,128]{1,0:T(8,128)(2,1)}, u32[]{:S(2)}, u32[]{:S(2)}) collective-permute-start(bf16[2560,128]{1,0:T(8,128)(2,1)S(1)} %constant_dynamic-update-slice_fusion.1.refs_0_), channel_id=1, source_target_pairs={{2,0},{65,1},{4,2},{67,3},{6,4},{69,5},{0,6},{71,7},{10,8},{73,9},... | collective-permute-start | bytes 1966088 | tf_op jit(solution)/shard_map/ppermute | solution.py:181
  37.5 0.7 compare_select_fusion.1
  38.2 0.4 fusion.55
  38.6 0.7 copy-done.5
  39.3 0.1 copy.40
  39.5 2.3 %collective-permute-start.15 = (bf16[2560,128]{1,0:T(8,128)(2,1)S(1)}, bf16[2560,128]{1,0:T(8,128)(2,1)}, u32[]{:S(2)}, u32[]{:S(2)}) collective-permute-start(bf16[2560,128]{1,0:T(8,128)(2,1)S(1)} %constant_dynamic-update-slice_fusion.1.refs_0_), channel_id=1, source_target_pairs={{1,0},{0,1},{3,2},{2,3},{5,4},{4,5},{7,6},{6,7},{9,8},{8,9},{11,10... | collective-permute-start | bytes 1966088 | tf_op jit(solution)/shard_map/ppermute | solution.py:181
  41.8 1.7 %collective-permute-start.7 = (bf16[2560,128]{1,0:T(8,128)(2,1)S(1)}, bf16[2560,128]{1,0:T(8,128)(2,1)}, u32[]{:S(2)}, u32[]{:S(2)}) collective-permute-start(bf16[2560,128]{1,0:T(8,128)(2,1)S(1)} %constant_dynamic-update-slice_fusion.1.refs_0_), channel_id=1, source_target_pairs={{6,0},{193,1},{0,2},{195,3},{2,4},{197,5},{4,6},{199,7},{14,8},{20... | collective-permute-start | bytes 1966088 | tf_op jit(solution)/shard_map/ppermute | solution.py:181
  43.5 1.1 collective-permute-start.22
  44.6 1.6 %collective-permute-start.14 = (bf16[2560,128]{1,0:T(8,128)(2,1)S(1)}, bf16[2560,128]{1,0:T(8,128)(2,1)}, u32[]{:S(2)}, u32[]{:S(2)}) collective-permute-start(bf16[2560,128]{1,0:T(8,128)(2,1)S(1)} %collective-permute-done.13.refs_7_), channel_id=1, source_target_pairs={{6,0},{193,1},{0,2},{195,3},{2,4},{197,5},{4,6},{199,7},{14,8},{20... | collective-permute-start | bytes 1966088 | tf_op jit(solution)/shard_map/ppermute | solution.py:181
  46.2 5.3 %collective-permute-done.5.refs_1_ = bf16[2560,128]{1,0:T(8,128)(2,1)} collective-permute-done((bf16[2560,128]{1,0:T(8,128)(2,1)S(1)}, bf16[2560,128]{1,0:T(8,128)(2,1)}, u32[]{:S(2)}, u32[]{:S(2)}) %collective-permute-start.5) | collective-permute-done | bytes 655392 | tf_op jit(solution)/shard_map/ppermute | solution.py:181
  51.4 0.3 collective-permute-start.6
  51.8 0.7 fusion.69
  53.2 0.7 add_convert_fusion
  53.8 0.3 fusion
  54.2 0.7 copy.34
  54.9 5.8 %collective-permute-start.16 = (bf16[2560,128]{1,0:T(8,128)(2,1)}, bf16[2560,128]{1,0:T(8,128)(2,1)}, u32[]{:S(2)}, u32[]{:S(2)}) collective-permute-start(bf16[2560,128]{1,0:T(8,128)(2,1)} %collective-permute-done.5.refs_1_), channel_id=1, source_target_pairs={{1,0},{0,1},{3,2},{2,3},{5,4},{4,5},{7,6},{6,7},{9,8},{8,9},{11,10... | collective-permute-start | bytes 1966088 | tf_op jit(solution)/shard_map/ppermute | solution.py:181
  60.8 0.4 collective-permute-start.18
  61.3 0.2 collective-permute-done.6.refs_2_
  61.5 4.5 %collective-permute-start.17 = (bf16[2560,128]{1,0:T(8,128)(2,1)}, bf16[2560,128]{1,0:T(8,128)(2,1)}, u32[]{:S(2)}, u32[]{:S(2)}) collective-permute-start(bf16[2560,128]{1,0:T(8,128)(2,1)} %collective-permute-done.6.refs_2_), channel_id=1, source_target_pairs={{1,0},{0,1},{3,2},{2,3},{5,4},{4,5},{7,6},{6,7},{9,8},{8,9},{11,10... | collective-permute-start | bytes 1966088 | tf_op jit(solution)/shard_map/ppermute | solution.py:181
  66.0 1.5 %fusion.72 = (f32[128,128]{0,1:T(8,128)S(1)}, f32[128,128]{0,1:T(8,128)}) fusion(f32[128,513]{0,1:T(8,128)} %copy-done.5), kind=kLoop, calls=%fused_computation.139 | loop fusion | bytes 262144 | tf_op jit(solution)/shard_map/slice | solution.py:248
  67.6 0.9 slice_convert_fusion.1
  68.5 0.7 copy.27
  69.2 1.6 %reshape.73 = s32[32,4,2,128]{3,2,1,0:T(2,128)} reshape(s32[128,256]{1,0:T(8,128)} %copy.27) | data formatting | bytes 262144 | tf_op jit(solution)/shard_map/reshape | solution.py:246
  70.8 0.9 copy.28
  71.8 1.6 %copy.38.w0_ref = f32[128,128]{1,0:T(8,128)} copy(f32[128,128]{0,1:T(8,128)} %get-tuple-element.17) | data formatting | bytes 131072
  73.3 0.6 pad.2.clone
  74.1 1.6 %fusion.65 = (s32[128]{0:T(128)}, s32[128]{0:T(128)S(1)}) fusion(f32[128,1]{1,0:T(8,128)} %copy-done.6, pred[128,1]{1,0:T(8,128)(4,1)S(1)} %get-tuple-element.11, s32[128,1]{1,0:T(8,128)} %copy.34), kind=kLoop, calls=%fused_computation.120 | loop fusion | flops 2688 | bytes 2176 | tf_op jit(solution)/shard_map/sub | solution.py:256
  75.7 8.3 %remote_tiles.1 = f32[128,128]{1,0:T(8,128)S(1)} custom-call(s32[2]{0:T(128)S(1)} %pad_add_fusion.1.range_ref, s32[32768]{0:T(1024)S(1)} %bitcast.24, f32[128,128]{1,0:T(8,128)S(1)} %copy-done.1, f32[128,128]{1,0:T(8,128)S(1)} %copy.39.w1_ref, bf16[2560,128]{1,0:T(8,128)(2,1)S(1)} %constant_dynamic-update-slice_fusion.1.refs_0_, ...), custom_call_target="tpu_custom_call" | custom-call | tf_op jit(solution)/shard_map/remote_tiles/pallas_call | solution.py:156
  84.1 0.7 copy-done.11
  84.8 1.2 fusion.5
  86.0 1.7 %reshape_reshape.6 = f32[4,64,1,256]{3,1,0,2:T(8,128)} reshape(f32[512,128]{1,0:T(8,128)} %fusion.5) | data formatting | bytes 524288 | tf_op jit(solution)/shard_map/reshape;reshape | solution.py:15
  87.7 1.9 %copy.35 = f32[4,64,1,256]{3,2,0,1:T(1,128)} copy(f32[4,64,1,256]{3,1,0,2:T(8,128)} %reshape_reshape.6) | data formatting | bytes 524288 | tf_op jit(solution)/shard_map/reshape;reshape | solution.py:15
  89.6 18.6 %all-to-all-start = ((f32[256,1,1,256]{3,1,2,0:T(1,128)}), f32[256,1,1,256]{3,1,2,0:T(1,128)}, u32[]{:S(2)}, u32[]{:S(2)}) async-start(f32[256,1,1,256]{3,1,2,0:T(1,128)} %bitcast.26), calls=%async_computation | async-start | bytes 524288 | tf_op jit(solution)/shard_map/all_to_all | solution.py:31
  110.9 0.8 copy-done.2
  111.7 21.0 %own_tiles.1 = f32[128,128]{1,0:T(8,128)S(1)} custom-call(s32[2]{0:T(128)S(1)} %pad_add_fusion.range_ref, s32[32768]{0:T(1024)S(1)} %bitcast.25, f32[128,128]{1,0:T(8,128)S(1)} %copy-done.2, f32[128,128]{1,0:T(8,128)S(1)} %copy.39.w1_ref, bf16[2560,128]{1,0:T(8,128)(2,1)S(1)} %constant_dynamic-update-slice_fusion.1.refs_0_, ...), custom_call_target="tpu_custom_call" | custom-call | tf_op jit(solution)/shard_map/own_tiles/pallas_call | solution.py:156
  132.7 0.6 copy-done.3
  133.3 1.0 copy.42
  134.4 0.2 fusion.2
  134.6 0.5 fusion.3
  135.1 0.4 copy-done.4
  135.5 0.3 copy-done.14
  135.8 0.9 convolution_add_fusion
  (80 shorter events, 1.5 us)
Async XLA Ops:
  0.0 2.9 %copy-start = (s32[16384]{0:T(1024)S(1)}, s32[16384]{0:T(1024)}, u32[]{:S(2)}) copy-start(s32[16384]{0:T(1024)} %param.11) | copy-start | bytes 196612
  0.0 1.0 copy-start.12
  1.5 5.1 %collective-permute-start = (bf16[320,128]{1,0:T(8,128)(2,1)S(1)}, bf16[320,128]{1,0:T(8,128)(2,1)S(1)}, u32[]{:S(2)}, u32[]{:S(2)}) collective-permute-start(bf16[320,128]{1,0:T(8,128)(2,1)S(1)} %broadcast_select_fusion), channel_id=1, source_target_pairs={{1,0},{0,1},{3,2},{2,3},{5,4},{4,5},{7,6},{6,7},{9,8},{8,9},{11,10... | collective-permute-start | bytes 245768 | tf_op jit(solution)/shard_map/ppermute | solution.py:181
  2.3 0.7 copy-start.17
  2.9 1.2 copy-start.9
  4.1 0.8 copy-start.13
  5.0 0.8 copy-start.10
  6.6 15.2 %collective-permute-start.8 = (bf16[640,128]{1,0:T(8,128)(2,1)S(1)}, bf16[640,128]{1,0:T(8,128)(2,1)S(1)}, u32[]{:S(2)}, u32[]{:S(2)}) collective-permute-start(bf16[640,128]{1,0:T(8,128)(2,1)S(1)} %pad_maximum_fusion), channel_id=1, source_target_pairs={{8,0},{33,1},{10,2},{35,3},{12,4},{37,5},{14,6},{39,7},{16,8},{41,... | collective-permute-start | bytes 491528 | tf_op jit(solution)/shard_map/ppermute | solution.py:181
  12.2 14.3 %collective-permute-start.1 = (bf16[640,128]{1,0:T(8,128)(2,1)S(1)}, bf16[640,128]{1,0:T(8,128)(2,1)S(1)}, u32[]{:S(2)}, u32[]{:S(2)}) collective-permute-start(bf16[640,128]{1,0:T(8,128)(2,1)S(1)} %pad_maximum_fusion), channel_id=1, source_target_pairs={{0,0},{41,1},{2,2},{43,3},{4,4},{45,5},{6,6},{47,7},{8,8},{49,9},{... | collective-permute-start | bytes 491528 | tf_op jit(solution)/shard_map/ppermute | solution.py:181
  14.2 12.7 %copy-start.7 = (f32[128,513]{1,0:T(8,128)}, f32[128,513]{1,0:T(8,128)S(1)}, u32[]{:S(2)}) copy-start(f32[128,513]{1,0:T(8,128)S(1)} %select_dynamic-update-slice_fusion) | copy-start | bytes 787972
  21.8 10.4 %collective-permute-start.11 = (bf16[640,128]{1,0:T(8,128)(2,1)S(1)}, bf16[640,128]{1,0:T(8,128)(2,1)S(1)}, u32[]{:S(2)}, u32[]{:S(2)}) collective-permute-start(bf16[640,128]{1,0:T(8,128)(2,1)S(1)} %collective-permute-done.8), channel_id=1, source_target_pairs={{192,0},{7,1},{194,2},{1,3},{196,4},{3,5},{198,6},{5,7},{200,8},{1... | collective-permute-start | bytes 491528 | tf_op jit(solution)/shard_map/ppermute | solution.py:181
  23.0 9.2 %collective-permute-start.10 = (bf16[640,128]{1,0:T(8,128)(2,1)S(1)}, bf16[640,128]{1,0:T(8,128)(2,1)S(1)}, u32[]{:S(2)}, u32[]{:S(2)}) collective-permute-start(bf16[640,128]{1,0:T(8,128)(2,1)S(1)} %collective-permute-done.8), channel_id=1, source_target_pairs={{128,0},{5,1},{130,2},{7,3},{132,4},{1,5},{134,6},{3,7},{136,8},{1... | collective-permute-start | bytes 491528 | tf_op jit(solution)/shard_map/ppermute | solution.py:181
  25.4 4.5 %collective-permute-start.9 = (bf16[640,128]{1,0:T(8,128)(2,1)S(1)}, bf16[640,128]{1,0:T(8,128)(2,1)S(1)}, u32[]{:S(2)}, u32[]{:S(2)}) collective-permute-start(bf16[640,128]{1,0:T(8,128)(2,1)S(1)} %collective-permute-done.8), channel_id=1, source_target_pairs={{64,0},{3,1},{66,2},{5,3},{68,4},{7,5},{70,6},{1,7},{72,8},{11,9},... | collective-permute-start | bytes 491528 | tf_op jit(solution)/shard_map/ppermute | solution.py:181
  26.6 8.1 %collective-permute-start.4 = (bf16[640,128]{1,0:T(8,128)(2,1)S(1)}, bf16[640,128]{1,0:T(8,128)(2,1)S(1)}, u32[]{:S(2)}, u32[]{:S(2)}) collective-permute-start(bf16[640,128]{1,0:T(8,128)(2,1)S(1)} %collective-permute-done.1), channel_id=1, source_target_pairs={{192,0},{7,1},{194,2},{1,3},{196,4},{3,5},{198,6},{5,7},{200,8},{1... | collective-permute-start | bytes 491528 | tf_op jit(solution)/shard_map/ppermute | solution.py:181
  26.9 7.7 %collective-permute-start.3 = (bf16[640,128]{1,0:T(8,128)(2,1)S(1)}, bf16[640,128]{1,0:T(8,128)(2,1)S(1)}, u32[]{:S(2)}, u32[]{:S(2)}) collective-permute-start(bf16[640,128]{1,0:T(8,128)(2,1)S(1)} %collective-permute-done.1), channel_id=1, source_target_pairs={{128,0},{5,1},{130,2},{7,3},{132,4},{1,5},{134,6},{3,7},{136,8},{1... | collective-permute-start | bytes 491528 | tf_op jit(solution)/shard_map/ppermute | solution.py:181
  29.9 4.7 %collective-permute-start.2 = (bf16[640,128]{1,0:T(8,128)(2,1)S(1)}, bf16[640,128]{1,0:T(8,128)(2,1)S(1)}, u32[]{:S(2)}, u32[]{:S(2)}) collective-permute-start(bf16[640,128]{1,0:T(8,128)(2,1)S(1)} %collective-permute-done.1), channel_id=1, source_target_pairs={{64,0},{3,1},{66,2},{5,3},{68,4},{7,5},{70,6},{1,7},{72,8},{11,9},... | collective-permute-start | bytes 491528 | tf_op jit(solution)/shard_map/ppermute | solution.py:181
  32.2 9.6 %collective-permute-start.19 = (bf16[2560,128]{1,0:T(8,128)(2,1)S(1)}, bf16[2560,128]{1,0:T(8,128)(2,1)S(1)}, u32[]{:S(2)}, u32[]{:S(2)}) collective-permute-start(bf16[2560,128]{1,0:T(8,128)(2,1)S(1)} %constant_dynamic-update-slice_fusion.5.refs_4_), channel_id=1, source_target_pairs={{1,0},{0,1},{3,2},{2,3},{5,4},{4,5},{7,6},{6,7},{9,8},{8,9},{11,10... | collective-permute-start | bytes 1966088 | tf_op jit(solution)/shard_map/ppermute | solution.py:181
  32.3 11.2 %collective-permute-start.13 = (bf16[2560,128]{1,0:T(8,128)(2,1)S(1)}, bf16[2560,128]{1,0:T(8,128)(2,1)S(1)}, u32[]{:S(2)}, u32[]{:S(2)}) collective-permute-start(bf16[2560,128]{1,0:T(8,128)(2,1)S(1)} %constant_dynamic-update-slice_fusion.5.refs_4_), channel_id=1, source_target_pairs={{6,0},{193,1},{0,2},{195,3},{2,4},{197,5},{4,6},{199,7},{14,8},{20... | collective-permute-start | bytes 1966088 | tf_op jit(solution)/shard_map/ppermute | solution.py:181
  34.6 10.0 %collective-permute-start.12 = (bf16[2560,128]{1,0:T(8,128)(2,1)S(1)}, bf16[2560,128]{1,0:T(8,128)(2,1)S(1)}, u32[]{:S(2)}, u32[]{:S(2)}) collective-permute-start(bf16[2560,128]{1,0:T(8,128)(2,1)S(1)} %constant_dynamic-update-slice_fusion.5.refs_4_), channel_id=1, source_target_pairs={{2,0},{65,1},{4,2},{67,3},{6,4},{69,5},{0,6},{71,7},{10,8},{73,9},... | collective-permute-start | bytes 1966088 | tf_op jit(solution)/shard_map/ppermute | solution.py:181
  34.6 2.8 %copy-start.8 = (f32[128,513]{1,0:T(8,128)S(1)}, f32[128,513]{1,0:T(8,128)}, u32[]{:S(2)}) copy-start(f32[128,513]{1,0:T(8,128)} %copy-done.7) | copy-start | bytes 787972
  34.7 16.7 %collective-permute-start.5 = (bf16[2560,128]{1,0:T(8,128)(2,1)S(1)}, bf16[2560,128]{1,0:T(8,128)(2,1)}, u32[]{:S(2)}, u32[]{:S(2)}) collective-permute-start(bf16[2560,128]{1,0:T(8,128)(2,1)S(1)} %constant_dynamic-update-slice_fusion.1.refs_0_), channel_id=1, source_target_pairs={{2,0},{65,1},{4,2},{67,3},{6,4},{69,5},{0,6},{71,7},{10,8},{73,9},... | collective-permute-start | bytes 1966088 | tf_op jit(solution)/shard_map/ppermute | solution.py:181
  38.6 0.7 copy-start.5
  39.5 14.4 %copy-start.6 = (f32[128,1]{1,0:T(8,128)}, f32[128,1]{1,0:T(8,128)S(1)}, u32[]{:S(2)}) copy-start(f32[128,1]{1,0:T(8,128)S(1)} %copy.40) | copy-start | bytes 1540
  39.5 15.5 %collective-permute-start.15 = (bf16[2560,128]{1,0:T(8,128)(2,1)S(1)}, bf16[2560,128]{1,0:T(8,128)(2,1)}, u32[]{:S(2)}, u32[]{:S(2)}) collective-permute-start(bf16[2560,128]{1,0:T(8,128)(2,1)S(1)} %constant_dynamic-update-slice_fusion.1.refs_0_), channel_id=1, source_target_pairs={{1,0},{0,1},{3,2},{2,3},{5,4},{4,5},{7,6},{6,7},{9,8},{8,9},{11,10... | collective-permute-start | bytes 1966088 | tf_op jit(solution)/shard_map/ppermute | solution.py:181
  41.8 18.9 %collective-permute-start.7 = (bf16[2560,128]{1,0:T(8,128)(2,1)S(1)}, bf16[2560,128]{1,0:T(8,128)(2,1)}, u32[]{:S(2)}, u32[]{:S(2)}) collective-permute-start(bf16[2560,128]{1,0:T(8,128)(2,1)S(1)} %constant_dynamic-update-slice_fusion.1.refs_0_), channel_id=1, source_target_pairs={{6,0},{193,1},{0,2},{195,3},{2,4},{197,5},{4,6},{199,7},{14,8},{20... | collective-permute-start | bytes 1966088 | tf_op jit(solution)/shard_map/ppermute | solution.py:181
  43.5 17.3 %collective-permute-start.22 = (bf16[2560,128]{1,0:T(8,128)(2,1)S(1)}, bf16[2560,128]{1,0:T(8,128)(2,1)}, u32[]{:S(2)}, u32[]{:S(2)}) collective-permute-start(bf16[2560,128]{1,0:T(8,128)(2,1)S(1)} %collective-permute-done.13.refs_7_), channel_id=1, source_target_pairs={{1,0},{0,1},{3,2},{2,3},{5,4},{4,5},{7,6},{6,7},{9,8},{8,9},{11,10... | collective-permute-start | bytes 1966088 | tf_op jit(solution)/shard_map/ppermute | solution.py:181
  44.6 16.6 %collective-permute-start.14 = (bf16[2560,128]{1,0:T(8,128)(2,1)S(1)}, bf16[2560,128]{1,0:T(8,128)(2,1)}, u32[]{:S(2)}, u32[]{:S(2)}) collective-permute-start(bf16[2560,128]{1,0:T(8,128)(2,1)S(1)} %collective-permute-done.13.refs_7_), channel_id=1, source_target_pairs={{6,0},{193,1},{0,2},{195,3},{2,4},{197,5},{4,6},{199,7},{14,8},{20... | collective-permute-start | bytes 1966088 | tf_op jit(solution)/shard_map/ppermute | solution.py:181
  51.4 10.0 %collective-permute-start.6 = (bf16[2560,128]{1,0:T(8,128)(2,1)}, bf16[2560,128]{1,0:T(8,128)(2,1)}, u32[]{:S(2)}, u32[]{:S(2)}) collective-permute-start(bf16[2560,128]{1,0:T(8,128)(2,1)} %collective-permute-done.5.refs_1_), channel_id=1, source_target_pairs={{2,0},{65,1},{4,2},{67,3},{6,4},{69,5},{0,6},{71,7},{10,8},{73,9},... | collective-permute-start | bytes 1966088 | tf_op jit(solution)/shard_map/ppermute | solution.py:181
  54.9 20.7 %collective-permute-start.16 = (bf16[2560,128]{1,0:T(8,128)(2,1)}, bf16[2560,128]{1,0:T(8,128)(2,1)}, u32[]{:S(2)}, u32[]{:S(2)}) collective-permute-start(bf16[2560,128]{1,0:T(8,128)(2,1)} %collective-permute-done.5.refs_1_), channel_id=1, source_target_pairs={{1,0},{0,1},{3,2},{2,3},{5,4},{4,5},{7,6},{6,7},{9,8},{8,9},{11,10... | collective-permute-start | bytes 1966088 | tf_op jit(solution)/shard_map/ppermute | solution.py:181
  60.7 14.9 %collective-permute-start.20 = (bf16[2560,128]{1,0:T(8,128)(2,1)S(1)}, bf16[2560,128]{1,0:T(8,128)(2,1)}, u32[]{:S(2)}, u32[]{:S(2)}) collective-permute-start(bf16[2560,128]{1,0:T(8,128)(2,1)S(1)} %collective-permute-done.12.refs_5_), channel_id=1, source_target_pairs={{1,0},{0,1},{3,2},{2,3},{5,4},{4,5},{7,6},{6,7},{9,8},{8,9},{11,10... | collective-permute-start | bytes 1966088 | tf_op jit(solution)/shard_map/ppermute | solution.py:181
  60.8 14.8 %collective-permute-start.18 = (bf16[2560,128]{1,0:T(8,128)(2,1)}, bf16[2560,128]{1,0:T(8,128)(2,1)}, u32[]{:S(2)}, u32[]{:S(2)}) collective-permute-start(bf16[2560,128]{1,0:T(8,128)(2,1)} %collective-permute-done.7.refs_3_), channel_id=1, source_target_pairs={{1,0},{0,1},{3,2},{2,3},{5,4},{4,5},{7,6},{6,7},{9,8},{8,9},{11,10... | collective-permute-start | bytes 1966088 | tf_op jit(solution)/shard_map/ppermute | solution.py:181
  61.2 14.4 %collective-permute-start.21 = (bf16[2560,128]{1,0:T(8,128)(2,1)}, bf16[2560,128]{1,0:T(8,128)(2,1)}, u32[]{:S(2)}, u32[]{:S(2)}) collective-permute-start(bf16[2560,128]{1,0:T(8,128)(2,1)} %collective-permute-done.14.refs_6_), channel_id=1, source_target_pairs={{1,0},{0,1},{3,2},{2,3},{5,4},{4,5},{7,6},{6,7},{9,8},{8,9},{11,10... | collective-permute-start | bytes 1966088 | tf_op jit(solution)/shard_map/ppermute | solution.py:181
  61.5 14.1 %collective-permute-start.17 = (bf16[2560,128]{1,0:T(8,128)(2,1)}, bf16[2560,128]{1,0:T(8,128)(2,1)}, u32[]{:S(2)}, u32[]{:S(2)}) collective-permute-start(bf16[2560,128]{1,0:T(8,128)(2,1)} %collective-permute-done.6.refs_2_), channel_id=1, source_target_pairs={{1,0},{0,1},{3,2},{2,3},{5,4},{4,5},{7,6},{6,7},{9,8},{8,9},{11,10... | collective-permute-start | bytes 1966088 | tf_op jit(solution)/shard_map/ppermute | solution.py:181
  74.1 1.6 %copy-start.1 = (f32[128,128]{1,0:T(8,128)S(1)}, f32[128,128]{1,0:T(8,128)}, u32[]{:S(2)}) copy-start(f32[128,128]{1,0:T(8,128)} %copy.38.w0_ref) | copy-start | bytes 196612
  84.0 0.8 copy-start.11
  84.1 0.7 copy-start.16
  89.6 43.7 %all-to-all-start = ((f32[256,1,1,256]{3,1,2,0:T(1,128)}), f32[256,1,1,256]{3,1,2,0:T(1,128)}, u32[]{:S(2)}, u32[]{:S(2)}) async-start(f32[256,1,1,256]{3,1,2,0:T(1,128)} %bitcast.26), calls=%async_computation | async-start | bytes 524288 | tf_op jit(solution)/shard_map/all_to_all | solution.py:31
  110.9 0.8 copy-start.2
  132.7 0.6 copy-start.3
  134.6 0.8 copy-start.4
  135.1 0.7 copy-start.14
  135.1 0.7 copy-start.15

commit v6 on v4

--- a/solution.py
+++ b/solution.py
@@ -60,30 +60,30 @@
 
     icopy(0, 0).start()
     icopy(1, 1).start()
-    starts = [sum(counts[:k]) for k in range(n)]
-
-    def tcopy(k):
-        rows = pl.ds(starts[k] * SHARD, counts[k] * SHARD)
-        return pltpu.make_async_copy(pieces[k], stage.at[rows, :], sem.at[k])
+    per = counts[0]
+
+    def tcopy(source, k):
+        rows = pl.ds(pl.multiple_of(k * per * SHARD, per * SHARD), per * SHARD)
+        return pltpu.make_async_copy(source, stage.at[rows, :], sem.at[k])
 
     for k in range(n):
-        tcopy(k).start()
+        tcopy(pieces[k], k).start()
     low = lax.broadcasted_iota(jnp.int32, (SHARD_S, 128), 1) < 64
 
-    def conv(slot, carry):
-        src = pl.multiple_of(slot * SHARD, SHARD_S)
-        urow = pl.multiple_of(slot * SHARD_U, SHARD_U)
-        srow = pl.multiple_of(slot * 2 * SHARD_S, 2 * SHARD_S)
-        utab[pl.ds(urow, SHARD_U), :] = stage[pl.ds(src, SHARD_U), :].astype(f32)
-        x = stage[pl.ds(src + SHARD_U, SHARD_S), :].astype(f32)
-        r = pltpu.roll(x, 64, 1)
-        stab[pl.ds(srow, SHARD_S), :] = jnp.where(low, x, r)
-        stab[pl.ds(srow + SHARD_S, SHARD_S), :] = jnp.where(low, r, x)
+    def conv(k, carry):
+        tcopy(pieces[0], k).wait()
+        src = pl.multiple_of(k * per * SHARD, per * SHARD)
+        urow = pl.multiple_of(k * per * SHARD_U, per * SHARD_U)
+        srow = pl.multiple_of(k * per * 2 * SHARD_S, per * 2 * SHARD_S)
+        for e in range(per):
+            utab[pl.ds(urow + e * SHARD_U, SHARD_U), :] = stage[pl.ds(src + e * SHARD, SHARD_U), :].astype(f32)
+            x = stage[pl.ds(src + e * SHARD + SHARD_U, SHARD_S), :].astype(f32)
+            r = pltpu.roll(x, 64, 1)
+            stab[pl.ds(srow + e * 2 * SHARD_S, SHARD_S), :] = jnp.where(low, x, r)
+            stab[pl.ds(srow + (e * 2 + 1) * SHARD_S, SHARD_S), :] = jnp.where(low, r, x)
         return carry
 
-    for k in range(n):
-        tcopy(k).wait()
-        lax.fori_loop(starts[k], starts[k] + counts[k], conv, 0)
+    lax.fori_loop(0, n, conv, 0)
 
     def tile(buf, j, t):
         w0 = w0_ref[pl.ds(t, 1), :]

time: 125 us -> 117 us (0.936)
  Pallas kernels: 30.5 us -> 23.1 us
    pallas_call x1, Pallas kernels: 30.5 us -> 23.1 us  [tile_sums(): pl.pallas_call(functools.partial(tile_kernel, counts, tiles), out_shape=j...]
where the time goes in v6:
time: 117 us
  starting transfers between devices  42.1 us (36%)
  blocking collectives  25.2 us (22%)
  Pallas kernels  23.1 us (20%)
  waiting for transfers between devices  16.4 us (14%)
  local copies, waits for them, and re-layouts  5.95 us (5%)
  matrix products  2.15 us (2%)
  other arithmetic  1.66 us (1%)
    ppermute x23, starting transfers between devices, fetched(): return lax.ppermute(value, ('grp', 'dev'), pairs)  42.1 us
    all_to_all x1, blocking collectives, exchange_both(): lax.all_to_all(pieces, axis, split_axis=0, concat_axis=0, tiled=True)  25.2 us
    pallas_call x1, Pallas kernels, tile_sums(): pl.pallas_call(functools.partial(tile_kernel, counts, tiles), out_shape=j...  23.1 us
    ppermute x23, waiting for transfers between devices, fetched(): return lax.ppermute(value, ('grp', 'dev'), pairs)  16.4 us
    unnamed x25, local copies, waits for them, and re-layouts  3.49 us
  transfers between devices with their start and end apart: 23, of which 7 were waited for; matrix products, arithmetic and copies ran while one was open for 3% of the time, Pallas kernels for 0%

profile of v6, /device:TPU:1, one launch (start us, length us, event | category | flops | bytes accessed | tf_op | source)
XLA Modules:
  0.0 116.9 jit_solution(2984410243490227351)
XLA Ops:
  0.0 1.1 copy.20
  1.1 0.0 copy-start.6
  1.2 0.7 copy-done.6
  1.9 0.1 copy.21
  2.0 0.1 fusion.32
  2.1 0.1 fusion.56
  2.2 0.1 broadcast_select_fusion.1
  2.3 3.3 %collective-permute-start = (bf16[320,128]{1,0:T(8,128)(2,1)S(1)}, bf16[320,128]{1,0:T(8,128)(2,1)S(1)}, u32[]{:S(2)}, u32[]{:S(2)}) collective-permute-start(bf16[320,128]{1,0:T(8,128)(2,1)S(1)} %broadcast_select_fusion), channel_id=1, source_target_pairs={{1,0},{0,1},{3,2},{2,3},{5,4},{4,5},{7,6},{6,7},{9,8},{8,9},{11,10... | collective-permute-start | bytes 245768 | tf_op jit(solution)/shard_map/ppermute | solution.py:168
  5.6 0.9 collective-permute-done
  6.6 5.3 %collective-permute-start.8 = (bf16[640,128]{1,0:T(8,128)(2,1)S(1)}, bf16[640,128]{1,0:T(8,128)(2,1)S(1)}, u32[]{:S(2)}, u32[]{:S(2)}) collective-permute-start(bf16[640,128]{1,0:T(8,128)(2,1)S(1)} %pad_maximum_fusion), channel_id=1, source_target_pairs={{8,0},{33,1},{10,2},{35,3},{12,4},{37,5},{14,6},{39,7},{16,8},{41,... | collective-permute-start | bytes 491528 | tf_op jit(solution)/shard_map/ppermute | solution.py:168
  11.8 3.5 %collective-permute-start.1 = (bf16[640,128]{1,0:T(8,128)(2,1)S(1)}, bf16[640,128]{1,0:T(8,128)(2,1)S(1)}, u32[]{:S(2)}, u32[]{:S(2)}) collective-permute-start(bf16[640,128]{1,0:T(8,128)(2,1)S(1)} %pad_maximum_fusion), channel_id=1, source_target_pairs={{0,0},{41,1},{2,2},{43,3},{4,4},{45,5},{6,6},{47,7},{8,8},{49,9},{... | collective-permute-start | bytes 491528 | tf_op jit(solution)/shard_map/ppermute | solution.py:168
  15.4 0.0 collective-permute-done.8
  15.4 2.6 %collective-permute-start.9 = (bf16[640,128]{1,0:T(8,128)(2,1)S(1)}, bf16[640,128]{1,0:T(8,128)(2,1)S(1)}, u32[]{:S(2)}, u32[]{:S(2)}) collective-permute-start(bf16[640,128]{1,0:T(8,128)(2,1)S(1)} %collective-permute-done.8), channel_id=1, source_target_pairs={{64,0},{3,1},{66,2},{5,3},{68,4},{7,5},{70,6},{1,7},{72,8},{11,9},... | collective-permute-start | bytes 491528 | tf_op jit(solution)/shard_map/ppermute | solution.py:168
  18.0 0.6 collective-permute-start.10
  18.6 0.6 collective-permute-start.11
  19.2 4.8 %collective-permute-done.1 = bf16[640,128]{1,0:T(8,128)(2,1)S(1)} collective-permute-done((bf16[640,128]{1,0:T(8,128)(2,1)S(1)}, bf16[640,128]{1,0:T(8,128)(2,1)S(1)}, u32[]{:S(2)}, u32[]{:S(2)}) %collective-permute-start.1) | collective-permute-done | bytes 163872 | tf_op jit(solution)/shard_map/ppermute | solution.py:168
  24.0 2.6 %collective-permute-start.2 = (bf16[640,128]{1,0:T(8,128)(2,1)S(1)}, bf16[640,128]{1,0:T(8,128)(2,1)S(1)}, u32[]{:S(2)}, u32[]{:S(2)}) collective-permute-start(bf16[640,128]{1,0:T(8,128)(2,1)S(1)} %collective-permute-done.1), channel_id=1, source_target_pairs={{64,0},{3,1},{66,2},{5,3},{68,4},{7,5},{70,6},{1,7},{72,8},{11,9},... | collective-permute-start | bytes 491528 | tf_op jit(solution)/shard_map/ppermute | solution.py:168
  26.6 0.5 collective-permute-start.3
  27.1 0.0 collective-permute-done.9
  27.1 0.6 collective-permute-start.4
  27.7 0.0 collective-permute-done.10
  27.8 0.0 collective-permute-done.11
  27.8 3.9 %collective-permute-start.13 = (bf16[2560,128]{1,0:T(8,128)(2,1)S(1)}, bf16[2560,128]{1,0:T(8,128)(2,1)S(1)}, u32[]{:S(2)}, u32[]{:S(2)}) collective-permute-start(bf16[2560,128]{1,0:T(8,128)(2,1)S(1)} %constant_dynamic-update-slice_fusion.4.refs_4_), channel_id=1, source_target_pairs={{6,0},{193,1},{0,2},{195,3},{2,4},{197,5},{4,6},{199,7},{14,8},{20... | collective-permute-start | bytes 1966088 | tf_op jit(solution)/shard_map/ppermute | solution.py:168
  31.7 0.0 collective-permute-start.12
  31.7 3.0 %collective-permute-start.19 = (bf16[2560,128]{1,0:T(8,128)(2,1)S(1)}, bf16[2560,128]{1,0:T(8,128)(2,1)S(1)}, u32[]{:S(2)}, u32[]{:S(2)}) collective-permute-start(bf16[2560,128]{1,0:T(8,128)(2,1)S(1)} %constant_dynamic-update-slice_fusion.4.refs_4_), channel_id=1, source_target_pairs={{1,0},{0,1},{3,2},{2,3},{5,4},{4,5},{7,6},{6,7},{9,8},{8,9},{11,10... | collective-permute-start | bytes 1966088 | tf_op jit(solution)/shard_map/ppermute | solution.py:168
  34.8 0.0 copy-start.3
  34.8 0.0 copy-start.5
  34.8 2.6 %collective-permute-start.5 = (bf16[2560,128]{1,0:T(8,128)(2,1)S(1)}, bf16[2560,128]{1,0:T(8,128)(2,1)}, u32[]{:S(2)}, u32[]{:S(2)}) collective-permute-start(bf16[2560,128]{1,0:T(8,128)(2,1)S(1)} %constant_dynamic-update-slice_fusion.refs_0_), channel_id=1, source_target_pairs={{2,0},{65,1},{4,2},{67,3},{6,4},{69,5},{0,6},{71,7},{10,8},{73,9},... | collective-permute-start | bytes 1966088 | tf_op jit(solution)/shard_map/ppermute | solution.py:168
  37.4 0.2 fusion.20
  37.6 0.1 add_bitcast_fusion
  37.8 0.0 copy-start.7
  37.8 0.6 copy-done.7
  38.4 0.0 collective-permute-start.7
  38.4 3.9 %collective-permute-done.13.refs_7_ = bf16[2560,128]{1,0:T(8,128)(2,1)S(1)} collective-permute-done((bf16[2560,128]{1,0:T(8,128)(2,1)S(1)}, bf16[2560,128]{1,0:T(8,128)(2,1)S(1)}, u32[]{:S(2)}, u32[]{:S(2)}) %collective-permute-start.13) | collective-permute-done | bytes 655392 | tf_op jit(solution)/shard_map/ppermute | solution.py:168
  42.4 0.9 collective-permute-start.15
  43.3 0.6 collective-permute-start.14
  43.8 0.0 collective-permute-done.19.refs_12_
  43.8 1.2 %collective-permute-start.20 = (bf16[2560,128]{1,0:T(8,128)(2,1)S(1)}, bf16[2560,128]{1,0:T(8,128)(2,1)}, u32[]{:S(2)}, u32[]{:S(2)}) collective-permute-start(bf16[2560,128]{1,0:T(8,128)(2,1)S(1)} %collective-permute-done.12.refs_5_), channel_id=1, source_target_pairs={{1,0},{0,1},{3,2},{2,3},{5,4},{4,5},{7,6},{6,7},{9,8},{8,9},{11,10... | collective-permute-start | bytes 1966088 | tf_op jit(solution)/shard_map/ppermute | solution.py:168
  45.1 3.5 %collective-permute-done.5.refs_1_ = bf16[2560,128]{1,0:T(8,128)(2,1)} collective-permute-done((bf16[2560,128]{1,0:T(8,128)(2,1)S(1)}, bf16[2560,128]{1,0:T(8,128)(2,1)}, u32[]{:S(2)}, u32[]{:S(2)}) %collective-permute-start.5) | collective-permute-done | bytes 655392 | tf_op jit(solution)/shard_map/ppermute | solution.py:168
  48.6 1.8 %collective-permute-start.6 = (bf16[2560,128]{1,0:T(8,128)(2,1)}, bf16[2560,128]{1,0:T(8,128)(2,1)}, u32[]{:S(2)}, u32[]{:S(2)}) collective-permute-start(bf16[2560,128]{1,0:T(8,128)(2,1)} %collective-permute-done.5.refs_1_), channel_id=1, source_target_pairs={{2,0},{65,1},{4,2},{67,3},{6,4},{69,5},{0,6},{71,7},{10,8},{73,9},... | collective-permute-start | bytes 1966088 | tf_op jit(solution)/shard_map/ppermute | solution.py:168
  50.4 1.1 gather_fusion
  51.6 0.7 convert_bitcast_fusion
  52.2 0.8 copy.22
  53.0 0.1 pad.2.clone
  53.1 0.3 fusion
  53.4 3.3 %collective-permute-start.22 = (bf16[2560,128]{1,0:T(8,128)(2,1)S(1)}, bf16[2560,128]{1,0:T(8,128)(2,1)S(1)}, u32[]{:S(2)}, u32[]{:S(2)}) collective-permute-start(bf16[2560,128]{1,0:T(8,128)(2,1)S(1)} %collective-permute-done.13.refs_7_), channel_id=1, source_target_pairs={{1,0},{0,1},{3,2},{2,3},{5,4},{4,5},{7,6},{6,7},{9,8},{8,9},{11,10... | collective-permute-start | bytes 1966088 | tf_op jit(solution)/shard_map/ppermute | solution.py:168
  56.7 0.1 collective-permute-start.16
  56.9 4.6 %collective-permute-start.18 = (bf16[2560,128]{1,0:T(8,128)(2,1)}, bf16[2560,128]{1,0:T(8,128)(2,1)S(1)}, u32[]{:S(2)}, u32[]{:S(2)}) collective-permute-start(bf16[2560,128]{1,0:T(8,128)(2,1)} %collective-permute-done.7.refs_3_), channel_id=1, source_target_pairs={{1,0},{0,1},{3,2},{2,3},{5,4},{4,5},{7,6},{6,7},{9,8},{8,9},{11,10... | collective-permute-start | bytes 1966088 | tf_op jit(solution)/shard_map/ppermute | solution.py:168
  61.5 0.0 collective-permute-start.21
  61.5 0.6 collective-permute-start.17
  62.1 1.3 %collective-permute-done.18.refs_11_ = bf16[2560,128]{1,0:T(8,128)(2,1)S(1)} collective-permute-done((bf16[2560,128]{1,0:T(8,128)(2,1)}, bf16[2560,128]{1,0:T(8,128)(2,1)S(1)}, u32[]{:S(2)}, u32[]{:S(2)}) %collective-permute-start.18) | collective-permute-done | bytes 655392 | tf_op jit(solution)/shard_map/ppermute | solution.py:168
  63.4 0.9 collective-permute-done.21.refs_14_
  64.3 0.9 collective-permute-done.17.refs_10_
  65.3 23.1 %tile_sums.1 = f32[128,128]{1,0:T(8,128)S(1)} custom-call(s32[32768]{0:T(1024)S(1)} %bitcast.23, f32[128,128]{1,0:T(8,128)S(1)} %broadcast_select_fusion.3.w0_ref, f32[128,128]{1,0:T(8,128)S(1)} %get-tuple-element.7.w1_ref, bf16[2560,128]{1,0:T(8,128)(2,1)S(1)} %constant_dynamic-update-slice_fusion.refs_0_, ...), custom_call_target="tpu_custom_call" | custom-call | tf_op jit(solution)/shard_map/tile_sums/pallas_call | solution.py:140
  88.3 0.1 slice_add_fusion
  88.4 0.7 copy-done.4
  89.2 0.5 fusion.5
  89.6 0.1 reshape_reshape.6
  89.7 0.3 copy.23
  90.0 25.2 %all_to_all.5 = f32[256,1,1,256]{3,1,2,0:T(1,128)S(1)} all-to-all(f32[256,1,1,256]{3,1,2,0:T(1,128)S(1)} %bitcast.25), channel_id=1, replica_groups=mesh['grp'=4,'dev'=64] {'dev','grp'}, dimensions={0} | all-to-all | bytes 524288 | tf_op jit(solution)/shard_map/all_to_all | solution.py:31
  115.2 0.1 copy.28
  115.3 0.2 fusion.2
  115.6 0.5 fusion.3
  116.0 0.9 convolution_add_fusion
  (41 shorter events, 0.4 us)
Async XLA Ops:
  0.0 50.4 %copy-start = (s32[16384]{0:T(1024)S(1)}, s32[16384]{0:T(1024)}, u32[]{:S(2)}) copy-start(s32[16384]{0:T(1024)} %param.11) | copy-start | bytes 196612
  1.1 0.8 copy-start.6
  2.3 4.2 %collective-permute-start = (bf16[320,128]{1,0:T(8,128)(2,1)S(1)}, bf16[320,128]{1,0:T(8,128)(2,1)S(1)}, u32[]{:S(2)}, u32[]{:S(2)}) collective-permute-start(bf16[320,128]{1,0:T(8,128)(2,1)S(1)} %broadcast_select_fusion), channel_id=1, source_target_pairs={{1,0},{0,1},{3,2},{2,3},{5,4},{4,5},{7,6},{6,7},{9,8},{8,9},{11,10... | collective-permute-start | bytes 245768 | tf_op jit(solution)/shard_map/ppermute | solution.py:168
  6.6 8.8 %collective-permute-start.8 = (bf16[640,128]{1,0:T(8,128)(2,1)S(1)}, bf16[640,128]{1,0:T(8,128)(2,1)S(1)}, u32[]{:S(2)}, u32[]{:S(2)}) collective-permute-start(bf16[640,128]{1,0:T(8,128)(2,1)S(1)} %pad_maximum_fusion), channel_id=1, source_target_pairs={{8,0},{33,1},{10,2},{35,3},{12,4},{37,5},{14,6},{39,7},{16,8},{41,... | collective-permute-start | bytes 491528 | tf_op jit(solution)/shard_map/ppermute | solution.py:168
  11.8 12.2 %collective-permute-start.1 = (bf16[640,128]{1,0:T(8,128)(2,1)S(1)}, bf16[640,128]{1,0:T(8,128)(2,1)S(1)}, u32[]{:S(2)}, u32[]{:S(2)}) collective-permute-start(bf16[640,128]{1,0:T(8,128)(2,1)S(1)} %pad_maximum_fusion), channel_id=1, source_target_pairs={{0,0},{41,1},{2,2},{43,3},{4,4},{45,5},{6,6},{47,7},{8,8},{49,9},{... | collective-permute-start | bytes 491528 | tf_op jit(solution)/shard_map/ppermute | solution.py:168
  15.4 11.7 %collective-permute-start.9 = (bf16[640,128]{1,0:T(8,128)(2,1)S(1)}, bf16[640,128]{1,0:T(8,128)(2,1)S(1)}, u32[]{:S(2)}, u32[]{:S(2)}) collective-permute-start(bf16[640,128]{1,0:T(8,128)(2,1)S(1)} %collective-permute-done.8), channel_id=1, source_target_pairs={{64,0},{3,1},{66,2},{5,3},{68,4},{7,5},{70,6},{1,7},{72,8},{11,9},... | collective-permute-start | bytes 491528 | tf_op jit(solution)/shard_map/ppermute | solution.py:168
  18.0 9.8 %collective-permute-start.10 = (bf16[640,128]{1,0:T(8,128)(2,1)S(1)}, bf16[640,128]{1,0:T(8,128)(2,1)S(1)}, u32[]{:S(2)}, u32[]{:S(2)}) collective-permute-start(bf16[640,128]{1,0:T(8,128)(2,1)S(1)} %collective-permute-done.8), channel_id=1, source_target_pairs={{128,0},{5,1},{130,2},{7,3},{132,4},{1,5},{134,6},{3,7},{136,8},{1... | collective-permute-start | bytes 491528 | tf_op jit(solution)/shard_map/ppermute | solution.py:168
  18.6 9.2 %collective-permute-start.11 = (bf16[640,128]{1,0:T(8,128)(2,1)S(1)}, bf16[640,128]{1,0:T(8,128)(2,1)S(1)}, u32[]{:S(2)}, u32[]{:S(2)}) collective-permute-start(bf16[640,128]{1,0:T(8,128)(2,1)S(1)} %collective-permute-done.8), channel_id=1, source_target_pairs={{192,0},{7,1},{194,2},{1,3},{196,4},{3,5},{198,6},{5,7},{200,8},{1... | collective-permute-start | bytes 491528 | tf_op jit(solution)/shard_map/ppermute | solution.py:168
  24.0 7.7 %collective-permute-start.2 = (bf16[640,128]{1,0:T(8,128)(2,1)S(1)}, bf16[640,128]{1,0:T(8,128)(2,1)S(1)}, u32[]{:S(2)}, u32[]{:S(2)}) collective-permute-start(bf16[640,128]{1,0:T(8,128)(2,1)S(1)} %collective-permute-done.1), channel_id=1, source_target_pairs={{64,0},{3,1},{66,2},{5,3},{68,4},{7,5},{70,6},{1,7},{72,8},{11,9},... | collective-permute-start | bytes 491528 | tf_op jit(solution)/shard_map/ppermute | solution.py:168
  26.6 8.1 %collective-permute-start.3 = (bf16[640,128]{1,0:T(8,128)(2,1)S(1)}, bf16[640,128]{1,0:T(8,128)(2,1)S(1)}, u32[]{:S(2)}, u32[]{:S(2)}) collective-permute-start(bf16[640,128]{1,0:T(8,128)(2,1)S(1)} %collective-permute-done.1), channel_id=1, source_target_pairs={{128,0},{5,1},{130,2},{7,3},{132,4},{1,5},{134,6},{3,7},{136,8},{1... | collective-permute-start | bytes 491528 | tf_op jit(solution)/shard_map/ppermute | solution.py:168
  27.1 7.7 %collective-permute-start.4 = (bf16[640,128]{1,0:T(8,128)(2,1)S(1)}, bf16[640,128]{1,0:T(8,128)(2,1)S(1)}, u32[]{:S(2)}, u32[]{:S(2)}) collective-permute-start(bf16[640,128]{1,0:T(8,128)(2,1)S(1)} %collective-permute-done.1), channel_id=1, source_target_pairs={{192,0},{7,1},{194,2},{1,3},{196,4},{3,5},{198,6},{5,7},{200,8},{1... | collective-permute-start | bytes 491528 | tf_op jit(solution)/shard_map/ppermute | solution.py:168
  27.8 14.5 %collective-permute-start.13 = (bf16[2560,128]{1,0:T(8,128)(2,1)S(1)}, bf16[2560,128]{1,0:T(8,128)(2,1)S(1)}, u32[]{:S(2)}, u32[]{:S(2)}) collective-permute-start(bf16[2560,128]{1,0:T(8,128)(2,1)S(1)} %constant_dynamic-update-slice_fusion.4.refs_4_), channel_id=1, source_target_pairs={{6,0},{193,1},{0,2},{195,3},{2,4},{197,5},{4,6},{199,7},{14,8},{20... | collective-permute-start | bytes 1966088 | tf_op jit(solution)/shard_map/ppermute | solution.py:168
  31.7 11.5 %collective-permute-start.12 = (bf16[2560,128]{1,0:T(8,128)(2,1)S(1)}, bf16[2560,128]{1,0:T(8,128)(2,1)S(1)}, u32[]{:S(2)}, u32[]{:S(2)}) collective-permute-start(bf16[2560,128]{1,0:T(8,128)(2,1)S(1)} %constant_dynamic-update-slice_fusion.4.refs_4_), channel_id=1, source_target_pairs={{2,0},{65,1},{4,2},{67,3},{6,4},{69,5},{0,6},{71,7},{10,8},{73,9},... | collective-permute-start | bytes 1966088 | tf_op jit(solution)/shard_map/ppermute | solution.py:168
  31.7 12.1 %collective-permute-start.19 = (bf16[2560,128]{1,0:T(8,128)(2,1)S(1)}, bf16[2560,128]{1,0:T(8,128)(2,1)S(1)}, u32[]{:S(2)}, u32[]{:S(2)}) collective-permute-start(bf16[2560,128]{1,0:T(8,128)(2,1)S(1)} %constant_dynamic-update-slice_fusion.4.refs_4_), channel_id=1, source_target_pairs={{1,0},{0,1},{3,2},{2,3},{5,4},{4,5},{7,6},{6,7},{9,8},{8,9},{11,10... | collective-permute-start | bytes 1966088 | tf_op jit(solution)/shard_map/ppermute | solution.py:168
  34.8 2.7 %copy-start.3 = (s32[128,128]{1,0:T(8,128)S(1)}, s32[128,128]{1,0:T(8,128)}, u32[]{:S(2)}) copy-start(s32[128,128]{1,0:T(8,128)} %param.7) | copy-start | bytes 196612
  34.8 2.7 %copy-start.5 = (s32[128,128]{1,0:T(8,128)S(1)}, s32[128,128]{1,0:T(8,128)}, u32[]{:S(2)}) copy-start(s32[128,128]{1,0:T(8,128)} %param.8) | copy-start | bytes 196612
  34.8 13.7 %collective-permute-start.5 = (bf16[2560,128]{1,0:T(8,128)(2,1)S(1)}, bf16[2560,128]{1,0:T(8,128)(2,1)}, u32[]{:S(2)}, u32[]{:S(2)}) collective-permute-start(bf16[2560,128]{1,0:T(8,128)(2,1)S(1)} %constant_dynamic-update-slice_fusion.refs_0_), channel_id=1, source_target_pairs={{2,0},{65,1},{4,2},{67,3},{6,4},{69,5},{0,6},{71,7},{10,8},{73,9},... | collective-permute-start | bytes 1966088 | tf_op jit(solution)/shard_map/ppermute | solution.py:168
  37.8 0.7 copy-start.7
  38.4 15.0 %collective-permute-start.7 = (bf16[2560,128]{1,0:T(8,128)(2,1)S(1)}, bf16[2560,128]{1,0:T(8,128)(2,1)}, u32[]{:S(2)}, u32[]{:S(2)}) collective-permute-start(bf16[2560,128]{1,0:T(8,128)(2,1)S(1)} %constant_dynamic-update-slice_fusion.refs_0_), channel_id=1, source_target_pairs={{6,0},{193,1},{0,2},{195,3},{2,4},{197,5},{4,6},{199,7},{14,8},{20... | collective-permute-start | bytes 1966088 | tf_op jit(solution)/shard_map/ppermute | solution.py:168
  42.4 14.4 %collective-permute-start.15 = (bf16[2560,128]{1,0:T(8,128)(2,1)S(1)}, bf16[2560,128]{1,0:T(8,128)(2,1)}, u32[]{:S(2)}, u32[]{:S(2)}) collective-permute-start(bf16[2560,128]{1,0:T(8,128)(2,1)S(1)} %constant_dynamic-update-slice_fusion.refs_0_), channel_id=1, source_target_pairs={{1,0},{0,1},{3,2},{2,3},{5,4},{4,5},{7,6},{6,7},{9,8},{8,9},{11,10... | collective-permute-start | bytes 1966088 | tf_op jit(solution)/shard_map/ppermute | solution.py:168
  43.3 13.6 %collective-permute-start.14 = (bf16[2560,128]{1,0:T(8,128)(2,1)S(1)}, bf16[2560,128]{1,0:T(8,128)(2,1)}, u32[]{:S(2)}, u32[]{:S(2)}) collective-permute-start(bf16[2560,128]{1,0:T(8,128)(2,1)S(1)} %collective-permute-done.13.refs_7_), channel_id=1, source_target_pairs={{6,0},{193,1},{0,2},{195,3},{2,4},{197,5},{4,6},{199,7},{14,8},{20... | collective-permute-start | bytes 1966088 | tf_op jit(solution)/shard_map/ppermute | solution.py:168
  43.8 17.6 %collective-permute-start.20 = (bf16[2560,128]{1,0:T(8,128)(2,1)S(1)}, bf16[2560,128]{1,0:T(8,128)(2,1)}, u32[]{:S(2)}, u32[]{:S(2)}) collective-permute-start(bf16[2560,128]{1,0:T(8,128)(2,1)S(1)} %collective-permute-done.12.refs_5_), channel_id=1, source_target_pairs={{1,0},{0,1},{3,2},{2,3},{5,4},{4,5},{7,6},{6,7},{9,8},{8,9},{11,10... | collective-permute-start | bytes 1966088 | tf_op jit(solution)/shard_map/ppermute | solution.py:168
  48.6 12.9 %collective-permute-start.6 = (bf16[2560,128]{1,0:T(8,128)(2,1)}, bf16[2560,128]{1,0:T(8,128)(2,1)}, u32[]{:S(2)}, u32[]{:S(2)}) collective-permute-start(bf16[2560,128]{1,0:T(8,128)(2,1)} %collective-permute-done.5.refs_1_), channel_id=1, source_target_pairs={{2,0},{65,1},{4,2},{67,3},{6,4},{69,5},{0,6},{71,7},{10,8},{73,9},... | collective-permute-start | bytes 1966088 | tf_op jit(solution)/shard_map/ppermute | solution.py:168
  53.1 9.0 %copy-start.2 = (f32[128,128]{1,0:T(8,128)S(1)}, f32[128,128]{1,0:T(8,128)}, u32[]{:S(2)}) copy-start(f32[128,128]{1,0:T(8,128)} %param.9) | copy-start | bytes 196612
  53.4 8.7 %collective-permute-start.22 = (bf16[2560,128]{1,0:T(8,128)(2,1)S(1)}, bf16[2560,128]{1,0:T(8,128)(2,1)S(1)}, u32[]{:S(2)}, u32[]{:S(2)}) collective-permute-start(bf16[2560,128]{1,0:T(8,128)(2,1)S(1)} %collective-permute-done.13.refs_7_), channel_id=1, source_target_pairs={{1,0},{0,1},{3,2},{2,3},{5,4},{4,5},{7,6},{6,7},{9,8},{8,9},{11,10... | collective-permute-start | bytes 1966088 | tf_op jit(solution)/shard_map/ppermute | solution.py:168
  56.7 5.4 %collective-permute-start.16 = (bf16[2560,128]{1,0:T(8,128)(2,1)}, bf16[2560,128]{1,0:T(8,128)(2,1)S(1)}, u32[]{:S(2)}, u32[]{:S(2)}) collective-permute-start(bf16[2560,128]{1,0:T(8,128)(2,1)} %collective-permute-done.5.refs_1_), channel_id=1, source_target_pairs={{1,0},{0,1},{3,2},{2,3},{5,4},{4,5},{7,6},{6,7},{9,8},{8,9},{11,10... | collective-permute-start | bytes 1966088 | tf_op jit(solution)/shard_map/ppermute | solution.py:168
  56.9 6.5 %collective-permute-start.18 = (bf16[2560,128]{1,0:T(8,128)(2,1)}, bf16[2560,128]{1,0:T(8,128)(2,1)S(1)}, u32[]{:S(2)}, u32[]{:S(2)}) collective-permute-start(bf16[2560,128]{1,0:T(8,128)(2,1)} %collective-permute-done.7.refs_3_), channel_id=1, source_target_pairs={{1,0},{0,1},{3,2},{2,3},{5,4},{4,5},{7,6},{6,7},{9,8},{8,9},{11,10... | collective-permute-start | bytes 1966088 | tf_op jit(solution)/shard_map/ppermute | solution.py:168
  61.5 2.9 %collective-permute-start.21 = (bf16[2560,128]{1,0:T(8,128)(2,1)}, bf16[2560,128]{1,0:T(8,128)(2,1)S(1)}, u32[]{:S(2)}, u32[]{:S(2)}) collective-permute-start(bf16[2560,128]{1,0:T(8,128)(2,1)} %collective-permute-done.14.refs_6_), channel_id=1, source_target_pairs={{1,0},{0,1},{3,2},{2,3},{5,4},{4,5},{7,6},{6,7},{9,8},{8,9},{11,10... | collective-permute-start | bytes 1966088 | tf_op jit(solution)/shard_map/ppermute | solution.py:168
  61.5 3.8 %collective-permute-start.17 = (bf16[2560,128]{1,0:T(8,128)(2,1)}, bf16[2560,128]{1,0:T(8,128)(2,1)S(1)}, u32[]{:S(2)}, u32[]{:S(2)}) collective-permute-start(bf16[2560,128]{1,0:T(8,128)(2,1)} %collective-permute-done.6.refs_2_), channel_id=1, source_target_pairs={{1,0},{0,1},{3,2},{2,3},{5,4},{4,5},{7,6},{6,7},{9,8},{8,9},{11,10... | collective-permute-start | bytes 1966088 | tf_op jit(solution)/shard_map/ppermute | solution.py:168
  62.1 3.2 %copy-start.1 = (bf16[2560,128]{1,0:T(8,128)(2,1)}, bf16[2560,128]{1,0:T(8,128)(2,1)S(1)}, u32[]{:S(2)}) copy-start(bf16[2560,128]{1,0:T(8,128)(2,1)S(1)} %collective-permute-done.22.refs_15_) | copy-start | bytes 1966084
  88.3 0.8 copy-start.4
